TPU v7x, 8 devices: a whole 2x2x1 slice. The times are simulated.
8 devices in a mesh: dp: 8 (over z, y, x, core).
Axes of the slice: x: 2, y: 2, z: 1, core: 2. Of those that a mesh axis runs over, the one named last changes fastest.
Arguments:
- act_in: bfloat16 [1024, 7, 7, 1024], P('dp')
- shortcut: bfloat16 [1024, 7, 7, 2048], P('dp')
- labels: int32 [1024], P('dp')
- w_conv: float32 [1024, 2048], replicated
- bn_gamma: float32 [2048], replicated
- bn_beta: float32 [2048], replicated
- w_fc: float32 [2048, 1000], replicated
- fc_bias: float32 [1000], replicated
- vel_conv: float32 [1024, 2048], replicated
- vel_gamma: float32 [2048], replicated
- vel_beta: float32 [2048], replicated
- vel_fc: float32 [2048, 1000], replicated
- vel_bias: float32 [1000], replicated
- learn_rate: float32 [], replicated
Outputs:
- output 1: float32 [1024, 2048], replicated
- output 2: float32 [2048], replicated
- output 3: float32 [2048], replicated
- output 4: float32 [2048, 1000], replicated
- output 5: float32 [1000], replicated
- output 6: float32 [1024, 2048], replicated
- output 7: float32 [2048], replicated
- output 8: float32 [2048], replicated
- output 9: float32 [2048, 1000], replicated
- output 10: float32 [1000], replicated
- output 11: float32 [], replicated
All inputs are finite; a program needn't handle non-finite values.
Results may differ from a plain program's by a relative error of at most 0.00917121.
Values sent between devices are 32-bit elements.
A program may use at most 1 GiB of HBM per device.

v0:
```python
import jax
import jax.numpy as jnp
from jax import lax
from jax.sharding import PartitionSpec as P

BN_EPS = 1e-5
SMOOTHING = 0.1
MOMENTUM = 0.9
TRUST_COEF = 0.001
WEIGHT_DECAY = 5e-5


def forward_backward(act_in, shortcut, labels, w_conv, bn_gamma, bn_beta, w_fc, fc_bias, global_rows):
    per_dev = act_in.shape[0]
    spatial = act_in.shape[1] * act_in.shape[2]
    c_mid = act_in.shape[3]
    c_out = shortcut.shape[3]
    classes = w_fc.shape[1]
    pos_count = per_dev * spatial
    act_grid = act_in.reshape(per_dev, spatial, c_mid)
    conv_out = jnp.einsum('bpc,cd->bpd', act_grid, w_conv.astype(jnp.bfloat16), preferred_element_type=jnp.float32)
    batch_mean = jnp.mean(conv_out, axis=(0, 1))
    centered = conv_out - batch_mean
    inv_std = lax.rsqrt(jnp.mean(jnp.square(centered), axis=(0, 1)) + BN_EPS)
    x_hat = centered * inv_std
    pre_act = x_hat * bn_gamma + bn_beta + shortcut.reshape(per_dev, spatial, c_out).astype(jnp.float32)
    pooled = jnp.mean(jax.nn.relu(pre_act), axis=1)
    pooled_bf = pooled.astype(jnp.bfloat16)
    fc_bf = w_fc.astype(jnp.bfloat16)
    logits = jnp.dot(pooled_bf, fc_bf, preferred_element_type=jnp.float32) + fc_bias
    log_prob = jax.nn.log_softmax(logits, axis=-1)
    one_hot_lab = (labels[:, None] == jnp.arange(classes, dtype=jnp.int32)[None, :]).astype(jnp.float32)
    target = SMOOTHING / classes + (1.0 - SMOOTHING) * one_hot_lab
    loss_part = -jnp.sum(target * log_prob) / global_rows
    d_logits = (jnp.exp(log_prob) - target) / global_rows
    d_bias = jnp.sum(d_logits, axis=0)
    d_logits_bf = d_logits.astype(jnp.bfloat16)
    d_fc = jnp.einsum('bc,bk->ck', pooled_bf, d_logits_bf, preferred_element_type=jnp.float32)
    d_pool = jnp.einsum('bk,ck->bc', d_logits_bf, fc_bf, preferred_element_type=jnp.float32) / spatial
    d_pre = jnp.where(pre_act > 0, d_pool[:, None, :], 0.0)
    d_beta = jnp.sum(d_pre, axis=(0, 1))
    d_gamma = jnp.sum(d_pre * x_hat, axis=(0, 1))
    d_conv_out = (bn_gamma * inv_std) * (d_pre - d_beta / pos_count - x_hat * (d_gamma / pos_count))
    d_conv = jnp.einsum('bpc,bpd->cd', act_grid, d_conv_out.astype(jnp.bfloat16), preferred_element_type=jnp.float32)
    return d_conv, d_gamma, d_beta, d_fc, d_bias, loss_part


def lars_update(weight, gradient, velocity, learn_rate):
    w_norm = jnp.sqrt(jnp.sum(jnp.square(weight)))
    g_norm = jnp.sqrt(jnp.sum(jnp.square(gradient)))
    trust = TRUST_COEF * w_norm / (g_norm + WEIGHT_DECAY * w_norm)
    new_vel = MOMENTUM * velocity + learn_rate * trust * (gradient + WEIGHT_DECAY * weight)
    return weight - new_vel, new_vel


def solution(mesh):
    groups = mesh.shape['dp']

    def local_step(act_in, shortcut, labels, w_conv, bn_gamma, bn_beta, w_fc, fc_bias, vel_conv, vel_gamma, vel_beta, vel_fc, vel_bias, learn_rate):
        global_rows = act_in.shape[0] * groups
        local_terms = forward_backward(act_in, shortcut, labels, w_conv, bn_gamma, bn_beta, w_fc, fc_bias, global_rows)
        g_conv, g_gamma, g_beta, g_fc, g_bias, loss_val = lax.psum(local_terms, 'dp')
        conv_new, conv_vel_new = lars_update(w_conv, g_conv, vel_conv, learn_rate)
        fc_new, fc_vel_new = lars_update(w_fc, g_fc, vel_fc, learn_rate)
        gamma_vel_new = MOMENTUM * vel_gamma + learn_rate * g_gamma
        beta_vel_new = MOMENTUM * vel_beta + learn_rate * g_beta
        bias_vel_new = MOMENTUM * vel_bias + learn_rate * g_bias
        return (conv_new, bn_gamma - gamma_vel_new, bn_beta - beta_vel_new, fc_new, fc_bias - bias_vel_new, conv_vel_new, gamma_vel_new, beta_vel_new, fc_vel_new, bias_vel_new, loss_val)

    return jax.shard_map(local_step, mesh=mesh, in_specs=(P('dp'),) * 3 + (P(),) * 11, out_specs=(P(),) * 11, check_vma=False)
```

profile of v0, /device:TPU:1, one launch (start us, length us, event | category | flops | bytes accessed | tf_op | source)
XLA Modules:
  0.0 463.1 jit_solution(16826152551928789290)
XLA Ops:
  7.2 0.0 all-reduce.4.cloned.1.call-start
  7.2 36.5 %fusion.32 = (f32[2048]{0:T(1024)S(1)}, f32[128,49,2048]{2,0,1:T(8,128)}) fusion(bf16[128,49,1024]{2,0,1:T(8,128)(2,1)} %bitcast.22, f32[1024,2048]{1,0:T(8,128)} %param.17), kind=kOutput, calls=%fused_computation.53 | convolution fusion | flops 26321614848 | bytes 72622080 | tf_op jit(solution)/shard_map/bpc,cd->bpd/dot_general | solution.py:21
  43.7 16.4 %multiply_reduce_fusion = f32[2048]{0:T(1024)S(1)} fusion(f32[128,49,2048]{2,0,1:T(8,128)} %get-tuple-element.45, f32[2048]{0:T(1024)S(1)} %broadcast_multiply_fusion.2), kind=kLoop, calls=%fused_computation.9 | loop fusion | flops 38533120 | bytes 51396608 | tf_op jit(solution)/shard_map/reduce_sum | solution.py:24
  60.1 0.0 copy-start.2
  60.1 0.0 copy-start.5
  60.1 24.3 %maximum_reduce_fusion = f32[128,2048]{1,0:T(8,128)S(1)} fusion(bf16[128,7,7,2048]{3,0,2,1:T(8,128)(2,1)} %param.15, f32[2048]{0:T(1024)S(1)} %copy-done.1, f32[2048]{0:T(1024)S(1)} %copy-done, f32[2048]{0:T(1024)S(1)} %add_rsqrt_fusion, f32[128,49,2048]{2,0,1:T(8,128)} %get-tuple-element.45, f32[2048]{0:T(1024)S(1)} %broadcast_multiply_fusion.2), kind=kLoop, calls=%fused_computation.8 | loop fusion | flops 102498304 | bytes 78151680 | tf_op jit(solution)/shard_map/reduce_sum | solution.py:27
  84.4 0.0 slice-start
  84.4 4.7 %fusion.33 = (f32[128]{0:T(128)S(1)}, f32[128,1000]{0,1:T(8,128)S(1)}) fusion(f32[1000]{0:T(1024)S(1)} %copy-done.2, f32[2048,1000]{0,1:T(8,128)} %param.20, f32[128,2048]{1,0:T(8,128)S(1)} %maximum_reduce_fusion), kind=kOutput, calls=%fused_computation.54 | convolution fusion | flops 527116160 | bytes 9757088 | tf_op jit(solution)/shard_map/dot_general | solution.py:30
  89.2 0.2 exponential_reduce_fusion
  89.4 0.0 slice-start.1
  89.4 4.6 fusion.20
  93.9 0.8 multiply_reduce_fusion.5
  94.7 0.9 convolution_multiply_fusion
  96.4 29.9 %select_reduce_fusion = (f32[2048]{0:T(1024)S(1)}, f32[2048]{0:T(1024)S(1)}, pred[128,49,2048]{2,0,1:T(32,128)(4,1)}) fusion(f32[128,2048]{1,0:T(8,128)S(1)} %convolution_multiply_fusion, f32[2048]{0:T(1024)S(1)} %add_rsqrt_fusion, f32[128,49,2048]{2,0,1:T(8,128)} %get-tuple-element.45, f32[2048]{0:T(1024)S(1)} %broadcast_multiply_fusion.2, ...), kind=kLoop, calls=%fused_computation.2 | loop fusion | flops 141291520 | bytes 91013120 | tf_op jit(solution)/shard_map/reduce_sum | solution.py:41
  126.9 23.8 %all-reduce = (f32[2048]{0:T(1024)S(1)}, f32[2048]{0:T(1024)S(1)}, f32[1000]{0:T(1024)S(1)}, f32[]{:T(128)}) all-reduce(f32[2048]{0:T(1024)S(1)} %get-tuple-element.23, f32[2048]{0:T(1024)S(1)} %get-tuple-element.22, f32[1000]{0:T(1024)S(1)} %get-tuple-element.25, f32[]{:T(128)S(6)} %div.43), channel_id=1, replica_groups=mesh['dp'=8] {'dp'}, use_global_device_ids=true, to_apply=%region_10.11 | all-reduce | flops 5097 | bytes 40776 | tf_op jit(solution)/shard_map/psum | solution.py:62
  150.8 0.6 fusion.30
  151.4 39.1 %fusion.6 = f32[1024,2048]{0,1:T(8,128)} fusion(bf16[128,49,1024]{2,0,1:T(8,128)(2,1)} %bitcast.23, pred[128,49,2048]{2,0,1:T(32,128)(4,1)} %get-tuple-element.42, f32[128,49,2048]{2,0,1:T(8,128)} %get-tuple-element.45, f32[2048]{0:T(1024)S(1)} %get-tuple-element.48, f32[2048]{0:T(1024)S(1)} %get-tuple-element.49, ...), kind=kOutput, calls=%fused_computation.19 | convolution fusion | flops 26409435136 | bytes 86548480 | tf_op jit(solution)/shard_map/bpc,bpd->cd/dot_general | solution.py:44
  190.5 0.0 all-reduce.4.cloned.1.call-update
  190.5 6.0 %multiply_reduce_fusion.4 = f32[]{:T(128)} fusion(f32[2048,1000]{0,1:T(8,128)} %param.20), kind=kLoop, calls=%fused_computation.18 | loop fusion | flops 4095999 | bytes 8192004 | tf_op jit(solution)/shard_map/reduce_sum | solution.py:49
  197.3 6.1 %multiply_reduce_fusion.2 = f32[]{:T(128)} fusion(f32[1024,2048]{1,0:T(8,128)} %param.17), kind=kLoop, calls=%fused_computation.15 | loop fusion | flops 4194303 | bytes 8388612 | tf_op jit(solution)/shard_map/reduce_sum | solution.py:49
  204.1 0.0 copy-start.4
  204.1 9.3 %copy.28 = f32[1024,2048]{0,1:T(8,128)} copy(f32[1024,2048]{1,0:T(8,128)} %param.17) | data formatting | bytes 16777216 | tf_op args[3]
  213.4 9.3 %copy.25 = f32[1024,2048]{0,1:T(8,128)} copy(f32[1024,2048]{1,0:T(8,128)} %param.22) | data formatting | bytes 16777216 | tf_op args[8]
  222.6 0.6 fusion.27
  223.3 0.6 fusion.29
  223.9 172.4 %all-reduce.4.cloned.1.call-done = (f32[1024,2048]{0,1:T(8,128)}, f32[2048,1000]{0,1:T(8,128)}) async-done(((f32[1024,2048]{0,1:T(8,128)}, f32[2048,1000]{0,1:T(8,128)}), (f32[1024,2048]{0,1:T(8,128)}, f32[2048,1000]{0,1:T(8,128)})) %all-reduce.4.cloned.1.call-update) | async-done | bytes 16580624 | tf_op jit(solution)/shard_map/psum | solution.py:62
  396.2 6.0 %multiply_reduce_fusion.3 = f32[]{:T(128)} fusion(f32[2048,1000]{0,1:T(8,128)} %get-tuple-element.31), kind=kLoop, calls=%fused_computation.17 | loop fusion | flops 4095999 | bytes 8192004 | tf_op jit(solution)/shard_map/reduce_sum | solution.py:50
  403.0 6.1 %multiply_reduce_fusion.1 = f32[]{:T(128)} fusion(f32[1024,2048]{0,1:T(8,128)} %get-tuple-element.30), kind=kLoop, calls=%fused_computation.14 | loop fusion | flops 4194303 | bytes 8388612 | tf_op jit(solution)/shard_map/reduce_sum | solution.py:50
  409.9 14.2 %fusion.31 = (f32[1024,2048]{0,1:T(8,128)}, f32[1024,2048]{0,1:T(8,128)}) fusion(f32[1024,2048]{0,1:T(8,128)} %copy.28, f32[1024,2048]{0,1:T(8,128)} %get-tuple-element.30, f32[]{:T(128)S(6)} %mul.145, f32[1024,2048]{0,1:T(8,128)} %copy.25), kind=kLoop, calls=%fused_computation.52 | loop fusion | flops 12582912 | bytes 41943044 | tf_op jit(solution)/shard_map/sub | solution.py:53
  424.1 9.1 %copy.29 = f32[1024,2048]{1,0:T(8,128)} copy(f32[1024,2048]{0,1:T(8,128)} %get-tuple-element.40) | data formatting | bytes 16777216
  433.2 9.1 %copy.30 = f32[1024,2048]{1,0:T(8,128)} copy(f32[1024,2048]{0,1:T(8,128)} %get-tuple-element.41) | data formatting | bytes 16777216
  442.3 13.9 %fusion.28 = (f32[2048,1000]{0,1:T(8,128)}, f32[2048,1000]{0,1:T(8,128)}) fusion(f32[2048,1000]{0,1:T(8,128)} %param.20, f32[2048,1000]{0,1:T(8,128)} %get-tuple-element.31, f32[]{:T(128)S(6)} %mul.159, f32[2048,1000]{0,1:T(8,128)} %param.25), kind=kLoop, calls=%fused_computation.49 | loop fusion | flops 12288000 | bytes 40960004 | tf_op jit(solution)/shard_map/sub | solution.py:53
  (18 shorter events, 0.1 us)
Async XLA Ops:
  7.2 389.1 %all-reduce.4.cloned.1.call-start = ((), (), s32[]{:S(2)}) async-start(), calls=%async_computation | async-start | bytes 33161216 | tf_op jit(solution)/shard_map/psum | solution.py:62
  43.7 16.4 %copy-start = (f32[2048]{0:T(1024)S(1)}, f32[2048]{0:T(1024)}, u32[]{:S(2)}) copy-start(f32[2048]{0:T(1024)} %param.18) | copy-start | bytes 24580
  43.7 16.4 %copy-start.1 = (f32[2048]{0:T(1024)S(1)}, f32[2048]{0:T(1024)}, u32[]{:S(2)}) copy-start(f32[2048]{0:T(1024)} %param.19) | copy-start | bytes 24580
  60.1 24.3 %copy-start.2 = (f32[1000]{0:T(1024)S(1)}, f32[1000]{0:T(1024)}, u32[]{:S(2)}) copy-start(f32[1000]{0:T(1024)} %param.21) | copy-start | bytes 12004
  60.1 29.3 %copy-start.5 = (s32[128]{0:T(128)S(1)}, s32[128]{0:T(128)}, u32[]{:S(2)}) copy-start(s32[128]{0:T(128)} %param.16) | copy-start | bytes 1540
  84.4 10.3 %slice-start = ((s8[8192000]{0:T(1024)(128)(4,1)}), s8[3997696]{0:T(1024)(128)(4,1)S(1)}, s32[]{:S(2)}) async-start(s8[8192000]{0:T(1024)(128)(4,1)} %bitcast.20), calls=%async_computation.1 | async-start | bytes 7995392
  89.4 5.4 %slice-start.1 = ((s8[8192000]{0:T(1024)(128)(4,1)}), s8[4194304]{0:T(1024)(128)(4,1)S(1)}, s32[]{:S(2)}) async-start(s8[8192000]{0:T(1024)(128)(4,1)} %bitcast.20), calls=%async_computation.2 | async-start | bytes 8388608
  96.3 54.4 %copy-start.3 = (f32[2048]{0:T(1024)S(1)}, f32[2048]{0:T(1024)}, u32[]{:S(2)}) copy-start(f32[2048]{0:T(1024)} %param.23) | copy-start | bytes 24580
  204.1 18.5 %copy-start.6 = (f32[1000]{0:T(1024)S(1)}, f32[1000]{0:T(1024)}, u32[]{:S(2)}) copy-start(f32[1000]{0:T(1024)} %param.26) | copy-start | bytes 12004
  204.1 19.1 %copy-start.4 = (f32[2048]{0:T(1024)S(1)}, f32[2048]{0:T(1024)}, u32[]{:S(2)}) copy-start(f32[2048]{0:T(1024)} %param.24) | copy-start | bytes 24580
Sparse Core Ops, SparseCore 0:
  190.7 205.5 all-reduce.3
where the time goes:
time: 465 us; the launch traced here: 463 us
  waiting for transfers between devices  172 us (37%)
  other arithmetic  126 us (27%)
  matrix products  85.8 us (18%)
  local copies, waits for them, and re-layouts  36.8 us (8%)
  blocking collectives  23.8 us (5%)
  between operations  18.3 us (4%)
    psum x1, waiting for transfers between devices, local_step(): lax.psum(local_terms, 'dp')  172 us
    dot_general x1, matrix products, forward_backward(): jnp.einsum('bpc,bpd->cd', act_grid, d_conv_out.astype(jnp.bfloat16), pref...  39.1 us
    unnamed x22, local copies, waits for them, and re-layouts  36.8 us
    dot_general x1, matrix products, forward_backward(): jnp.einsum('bpc,cd->bpd', act_grid, w_conv.astype(jnp.bfloat16), preferre...  36.5 us
    reduce_sum x1, other arithmetic, forward_backward(): d_beta = jnp.sum(d_pre, axis=(0, 1))  29.9 us
    sub x2, other arithmetic, lars_update(): return (weight - new_vel, new_vel)  28.1 us
    reduce_sum x1, other arithmetic, forward_backward(): pooled = jnp.mean(jax.nn.relu(pre_act), axis=1)  24.3 us
    psum x1, blocking collectives, local_step(): lax.psum(local_terms, 'dp')  23.8 us
  transfers between devices with their start and end apart: 1, of which 1 were waited for; matrix products, arithmetic and copies ran while one was open for 7% of the time, Pallas kernels for 0%

commit v1 on v0

v1 whole, which is shorter than its diff:
```python
import functools
import jax, jax.numpy as jnp
from jax import lax
from jax.experimental import pallas as pl
from jax.experimental.pallas import tpu as pltpu

BN_EPS = 1e-5
IMG = 128
POS = 49
ROWS = IMG * POS
CIN = 1024
COUT = 2048
CB = 256
NB = COUT // CB
CH = 7
NCH = POS // CH
NT = 16
MS = 1


def fwd_kernel(a_ref, w_ref, s_ref, g_ref, b_ref, z_hbm, at_ref, pool_ref, cnt_ref, sx_ref, st_ref, zbuf, wbf, stat, zsem):
    j = pl.program_id(0)
    slot = lax.rem(j, 2)
    prev = 1 - slot

    def z_copy(jj, sl):
        return pltpu.make_async_copy(zbuf.at[sl], z_hbm.at[:, pl.ds(pl.multiple_of(jj * CB, CB), CB)], zsem.at[sl])

    @pl.when(j >= 2)
    def _():
        z_copy(j - 2, slot).wait()

    def step(do_mm, do_post):
        if do_mm:
            w = w_ref[...].astype(jnp.bfloat16)
            wbf[...] = w
            z0 = jnp.dot(a_ref[0:IMG, :], w, preferred_element_type=jnp.float32)
            m0 = jnp.sum(z0, axis=0, keepdims=True) * (1.0 / IMG)
            stat[0:8, :] = jnp.zeros((8, CB), jnp.float32)
            stat[8:16, :] = jnp.zeros((8, CB), jnp.float32)
        if do_post:
            mean = stat[16:17, :]
            inv = stat[17:18, :]
            gam = g_ref[...]
            sc = gam * inv
            sh = b_ref[...] - mean * sc
            sc_b = jnp.broadcast_to(sc, (8, CB))
            sh_b = jnp.broadcast_to(sh, (8, CB))
            pool_ref[...] = jnp.zeros_like(pool_ref)
            cnt_ref[...] = jnp.zeros_like(cnt_ref)
            sx_ref[...] = jnp.zeros_like(sx_ref)
            st_ref[...] = stat[16:24, :]

        def chunk(i, carry):
            base = pl.multiple_of(i * (CH * IMG), CH * IMG)
            if do_mm:
                for h in range(MS):
                    hr = pl.ds(base + h * (CH * IMG // MS), CH * IMG // MS)
                    zc = jnp.dot(a_ref[hr, :], wbf[...], preferred_element_type=jnp.float32)
                    zbuf[slot, hr, :] = zc
                    d = (zc - m0).reshape(CH * IMG // 8 // MS, 8, CB)
                    stat[0:8, :] += jnp.sum(d, axis=0)
                    stat[8:16, :] += jnp.sum(d * d, axis=0)
                at_ref[:, pl.ds(base, CH * IMG)] = a_ref[pl.ds(base, CH * IMG), pl.ds(pl.multiple_of(j * IMG, IMG), IMG)].astype(jnp.float32).T.astype(jnp.bfloat16)
            if do_post:
                for n in range(0, IMG, NT):
                    pa = pool_ref[n:n + NT, :]
                    ca = cnt_ref[n:n + NT, :]
                    xa = sx_ref[n:n + NT, :]
                    for p in range(CH):
                        zz = zbuf[prev, pl.ds(base + p * IMG + n, NT), :]
                        ss = s_ref[pl.ds(base + p * IMG + n, NT), :].astype(jnp.float32)
                        u = zz * sc + sh + ss
                        mk = u > 0
                        pa = pa + jnp.maximum(u, 0.0)
                        ca = ca + jnp.where(mk, 1.0, 0.0)
                        xa = xa + jnp.where(mk, zz, 0.0)
                    pool_ref[n:n + NT, :] = pa
                    cnt_ref[n:n + NT, :] = ca
                    sx_ref[n:n + NT, :] = xa
            return carry

        lax.fori_loop(0, NCH, chunk, 0)
        if do_post:
            pool_ref[...] = pool_ref[...] * (1.0 / POS)
            sx_ref[...] = (sx_ref[...] - mean * cnt_ref[...]) * inv
        if do_mm:
            dm = jnp.sum(stat[0:8, :], axis=0, keepdims=True) * (1.0 / ROWS)
            q = jnp.sum(stat[8:16, :], axis=0, keepdims=True) * (1.0 / ROWS)
            var = jnp.maximum(q - dm * dm, 0.0)
            stat[16:17, :] = m0 + dm
            stat[17:18, :] = lax.rsqrt(var + BN_EPS)
            z_copy(j, slot).start()

    @pl.when(j == 0)
    def _():
        step(True, False)

    @pl.when(jnp.logical_and(j > 0, j < NB))
    def _():
        step(True, True)

    @pl.when(j == NB)
    def _():
        step(False, True)
        z_copy(NB - 1, (NB - 1) % 2).wait()


def forward(a, w, s, gamma, beta):
    prev = lambda j: (0, jnp.maximum(j - 1, 0))
    cur = lambda j: (0, jnp.minimum(j, NB - 1))
    f32 = jnp.float32
    return pl.pallas_call(
        fwd_kernel,
        grid=(NB + 1,),
        in_specs=[
            pl.BlockSpec((ROWS, CIN), lambda j: (0, 0), pipeline_mode=pl.Buffered(1)),
            pl.BlockSpec((CIN, CB), cur),
            pl.BlockSpec((ROWS, CB), prev),
            pl.BlockSpec((1, CB), prev),
            pl.BlockSpec((1, CB), prev),
        ],
        out_specs=[
            pl.BlockSpec(memory_space=pl.ANY),
            pl.BlockSpec((IMG, ROWS), lambda j: (jnp.minimum(j, NB - 1), 0)),
            pl.BlockSpec((IMG, CB), prev),
            pl.BlockSpec((IMG, CB), prev),
            pl.BlockSpec((IMG, CB), prev),
            pl.BlockSpec((8, CB), prev),
        ],
        out_shape=[
            jax.ShapeDtypeStruct((ROWS, COUT), f32),
            jax.ShapeDtypeStruct((CIN, ROWS), jnp.bfloat16),
            jax.ShapeDtypeStruct((IMG, COUT), f32),
            jax.ShapeDtypeStruct((IMG, COUT), f32),
            jax.ShapeDtypeStruct((IMG, COUT), f32),
            jax.ShapeDtypeStruct((8, COUT), f32),
        ],
        scratch_shapes=[
            pltpu.VMEM((2, ROWS, CB), f32),
            pltpu.VMEM((CIN, CB), jnp.bfloat16),
            pltpu.VMEM((24, CB), f32),
            pltpu.SemaphoreType.DMA((2,)),
        ],
        compiler_params=pltpu.CompilerParams(vmem_limit_bytes=60 * 1024 * 1024),
        cost_estimate=pl.CostEstimate(flops=2 * ROWS * CIN * COUT, bytes_accessed=120_000_000, transcendentals=0),
        name="fwd_conv",
    )(a, w, s, gamma, beta)


def bwd_kernel(at_ref, z_ref, s_ref, sc_ref, sh_ref, bb_ref, cc_ref, da_ref, dw_ref, dz):
    j = pl.program_id(0)
    slot = lax.rem(j, 2)
    prev = 1 - slot

    def step(do_pre, do_mm):
        if do_pre:
            sc = sc_ref[...]
            sh = sh_ref[...]
            bb = bb_ref[...]
            cc = cc_ref[...]

        def pre(base, slabs):
            for n in range(0, IMG, NT):
                da = da_ref[n:n + NT, :]
                for p in range(slabs):
                    r = pl.ds(base + p * IMG + n, NT)
                    zz = z_ref[r, :]
                    u = zz * sc + sh + s_ref[r, :].astype(jnp.float32)
                    dz[slot, r, :] = (jnp.where(u > 0, da, 0.0) + (zz * cc + bb)).astype(jnp.bfloat16)

        def mm(base, size):
            return jnp.dot(at_ref[:, pl.ds(base, size)], dz[prev, pl.ds(base, size), :], preferred_element_type=jnp.float32)

        if do_mm:
            dw_ref[...] = mm(5376, 896)
        if do_pre:
            pre(5376, 7)

        def chunk(i, carry):
            base = pl.multiple_of(i * 1792, 1792)
            if do_mm:
                dw_ref[...] += mm(base, 1792)
            if do_pre:
                pre(base, 14)
            return carry
        lax.fori_loop(0, 3, chunk, 0)

    @pl.when(j == 0)
    def _():
        step(True, False)

    @pl.when(jnp.logical_and(j > 0, j < NB))
    def _():
        step(True, True)

    @pl.when(j == NB)
    def _():
        step(False, True)


def backward(at, z, s, sc, sh, bb, cc, da):
    prev = lambda j: (0, jnp.maximum(j - 1, 0))
    cur = lambda j: (0, jnp.minimum(j, NB - 1))
    row = pl.BlockSpec((1, CB), cur)
    return pl.pallas_call(
        bwd_kernel,
        grid=(NB + 1,),
        in_specs=[
            pl.BlockSpec((CIN, ROWS), lambda j: (0, 0), pipeline_mode=pl.Buffered(1)),
            pl.BlockSpec((ROWS, CB), cur),
            pl.BlockSpec((ROWS, CB), cur),
            row, row, row, row,
            pl.BlockSpec((IMG, CB), cur),
        ],
        out_specs=pl.BlockSpec((CIN, CB), prev),
        out_shape=jax.ShapeDtypeStruct((CIN, COUT), jnp.float32),
        scratch_shapes=[pltpu.VMEM((2, ROWS, CB), jnp.bfloat16)],
        compiler_params=pltpu.CompilerParams(vmem_limit_bytes=60 * 1024 * 1024),
        cost_estimate=pl.CostEstimate(flops=2 * ROWS * CIN * COUT, bytes_accessed=120_000_000, transcendentals=0),
        name="bwd_conv",
    )(at, z, s, sc, sh, bb, cc, da)
import jax
import jax.numpy as jnp
from jax.sharding import PartitionSpec as P

SMOOTHING = 0.1
MOMENTUM = 0.9
TRUST_COEF = 0.001
WEIGHT_DECAY = 5e-5


def lars_update(weight, gradient, velocity, learn_rate):
    w_norm = jnp.sqrt(jnp.sum(jnp.square(weight)))
    g_norm = jnp.sqrt(jnp.sum(jnp.square(gradient)))
    trust = TRUST_COEF * w_norm / (g_norm + WEIGHT_DECAY * w_norm)
    new_vel = MOMENTUM * velocity + learn_rate * trust * (gradient + WEIGHT_DECAY * weight)
    return weight - new_vel, new_vel


def head(pooled, labels, w_fc_t, fc_bias, total):
    bf = jnp.bfloat16
    f32 = jnp.float32
    classes = w_fc_t.shape[0]
    pb = pooled.astype(bf)
    wb = w_fc_t.astype(bf)
    logits = jnp.einsum('nc,kc->nk', pb, wb, preferred_element_type=f32) + fc_bias
    log_prob = jax.nn.log_softmax(logits, axis=-1)
    one_hot = (labels[:, None] == jnp.arange(classes, dtype=jnp.int32)[None, :]).astype(f32)
    target = SMOOTHING / classes + (1.0 - SMOOTHING) * one_hot
    loss = -jnp.sum(target * log_prob) / total
    dl = (jnp.exp(log_prob) - target) / total
    return pb, wb, dl, dl.astype(bf), loss


def solution(mesh):
    groups = mesh.shape['dp']

    def local_step(act_in, shortcut, labels, w_conv, gamma, beta, w_fc, fc_bias, vel_conv, vel_gamma, vel_beta, vel_fc, vel_bias, lr):
        f32 = jnp.float32
        total = IMG * groups
        a = act_in.transpose(1, 2, 0, 3).reshape(ROWS, CIN)
        s = shortcut.transpose(1, 2, 0, 3).reshape(ROWS, COUT)
        w_fc_t = w_fc.T
        z, at, pooled, cnt, sx, st = forward(a, w_conv, s, gamma[None], beta[None])
        pb, wb, dl, dlb, loss = head(pooled, labels, w_fc_t, fc_bias, total)
        dpool = jnp.einsum('nk,kc->nc', dlb, wb, preferred_element_type=f32) / POS
        mean = st[0:1]
        inv = st[1:2]
        gam = gamma[None]
        d_beta = jnp.sum(dpool * cnt, axis=0, keepdims=True)
        d_gamma = jnp.sum(dpool * sx, axis=0, keepdims=True)
        sc = gam * inv
        sh = beta[None] - mean * sc
        cc = -(sc * inv) * (d_gamma / ROWS)
        bb = -sc * (d_beta / ROWS) - mean * cc
        dw = backward(at, z, s, sc, sh, bb, cc, dpool * sc)
        g_fc_t = jnp.einsum('nk,nc->kc', dlb, pb, preferred_element_type=f32)
        g_bias = jnp.sum(dl, axis=0)
        g_conv, g_gamma, g_beta, g_fc_t, g_bias, loss = lax.psum((dw, d_gamma[0], d_beta[0], g_fc_t, g_bias, loss), 'dp')
        conv_new, conv_vel_new = lars_update(w_conv, g_conv, vel_conv, lr)
        fc_new, fc_vel_new = lars_update(w_fc_t, g_fc_t, vel_fc.T, lr)
        gv = MOMENTUM * vel_gamma + lr * g_gamma
        bv = MOMENTUM * vel_beta + lr * g_beta
        cv = MOMENTUM * vel_bias + lr * g_bias
        return (conv_new, gamma - gv, beta - bv, fc_new.T, fc_bias - cv, conv_vel_new, gv, bv, fc_vel_new.T, cv, loss)

    return jax.shard_map(local_step, mesh=mesh, in_specs=(P('dp'),) * 3 + (P(),) * 11, out_specs=(P(),) * 11, check_vma=False)
```

time: 465 us -> 397 us (0.85)
  Pallas kernels: 0 us -> 117 us
  matrix products: 85.8 us -> 11.6 us
  other arithmetic: 126 us -> 57.4 us
  local copies, waits for them, and re-layouts: 36.8 us -> 0.09 us
  waiting for transfers between devices: 172 us -> 165 us
    pallas_call x0 -> x2, Pallas kernels: none -> 117 us  [the longest x1 66.6 us: forward(): pl.pallas_call(fwd_kernel, grid=(NB + 1,), in_specs=[pl.BlockSpec((ROWS,...]
    dot_general x5 -> x3, matrix products: 85.8 us -> 11.6 us  [the longest x1 4.98 us: head(): jnp.einsum('nc,kc->nk', pb, wb, preferred_element_type=f32) + fc_bias]
    reduce_sum x5 -> x2, other arithmetic: 71.6 us -> 0.95 us  [the longest x1 0.8 us: head(): loss = -jnp.sum(target * log_prob) / total]
    unnamed x22 -> x26, local copies, waits for them, and re-layouts: 36.8 us -> 0.08 us
    transpose x0 -> x1, other arithmetic: none -> 13.9 us  [local_step(): return (conv_new, gamma - gv, beta - bv, fc_new.T, fc_bias - cv, conv_vel...]
    sub x2 -> x1, other arithmetic: 28.1 us -> 14.4 us  [lars_update(): return (weight - new_vel, new_vel)]
    psum x1, waiting for transfers between devices: 172 us -> 165 us  [local_step(): lax.psum((dw, d_gamma[0], d_beta[0], g_fc_t, g_bias, loss), 'dp')]
  transfers between devices with their start and end apart: 1 -> 1, of which waited for: 1 -> 1; matrix products, arithmetic and copies ran while one was open for 7% -> 4% of each run, Pallas kernels for 0% -> 0%
where the time goes in v1:
time: 397 us; the launch traced here: 395 us
  waiting for transfers between devices  165 us (42%)
  Pallas kernels  117 us (29%)
  other arithmetic  57.4 us (14%)
  blocking collectives  25.3 us (6%)
  between operations  18.4 us (5%)
  matrix products  11.6 us (3%)
    psum x1, waiting for transfers between devices, local_step(): lax.psum((dw, d_gamma[0], d_beta[0], g_fc_t, g_bias, loss), 'dp')  165 us
    pallas_call x1, Pallas kernels, forward(): pl.pallas_call(fwd_kernel, grid=(NB + 1,), in_specs=[pl.BlockSpec((ROWS,...  66.6 us
    pallas_call x1, Pallas kernels, backward(): pl.pallas_call(bwd_kernel, grid=(NB + 1,), in_specs=[pl.BlockSpec((CIN, R...  50.8 us
    psum x1, blocking collectives, local_step(): lax.psum((dw, d_gamma[0], d_beta[0], g_fc_t, g_bias, loss), 'dp')  25.3 us
    sub x1, other arithmetic, lars_update(): return (weight - new_vel, new_vel)  14.4 us
    transpose x1, other arithmetic, local_step(): return (conv_new, gamma - gv, beta - bv, fc_new.T, fc_bias - cv, conv_vel...  13.9 us
    reduce_sum x2, other arithmetic, lars_update(): w_norm = jnp.sqrt(jnp.sum(jnp.square(weight)))  12.2 us
    reduce_sum x2, other arithmetic, lars_update(): g_norm = jnp.sqrt(jnp.sum(jnp.square(gradient)))  12.2 us
  transfers between devices with their start and end apart: 1, of which 1 were waited for; matrix products, arithmetic and copies ran while one was open for 4% of the time, Pallas kernels for 0%

profile of v1, /device:TPU:1, one launch (start us, length us, event | category | flops | bytes accessed | tf_op | source)
XLA Modules:
  0.0 395.3 jit_solution(2098797258667390363)
XLA Ops:
  7.2 0.0 all-reduce.4.cloned.1.call-start
  7.2 66.6 %fwd_conv.1 = (f32[6272,2048]{1,0:T(8,128)}, bf16[1024,6272]{1,0:T(8,128)(2,1)}, f32[128,2048]{1,0:T(8,128)}, f32[128,2048]{1,0:T(8,128)}, f32[128,2048]{1,0:T(8,128)}, /*index=5*/f32[8,2048]{1,0:T(8,128)}) custom-call(bf16[6272,1024]{1,0:T(8,128)(2,1)} %bitcast.73, f32[1024,2048]{1,0:T(8,128)} %w_ref.1, bf16[6272,2048]{1,0:T(8,128)(2,1)} %bitcast.64, ...), custom_call_target="tpu_custom_call" | custom-call | flops 26306674688 | bytes 120000000 | tf_op jit(solution)/shard_map/fwd_conv/pallas_call | solution.py:113
  73.8 0.0 copy-start.5
  73.8 0.0 copy-start
  73.8 0.0 copy-start.9
  73.8 5.0 %fusion.21 = (f32[128]{0:T(128)S(1)}, f32[128,1000]{0,1:T(8,128)S(1)}) fusion(f32[1000]{0:T(1024)S(1)} %copy-done.6, f32[128,2048]{1,0:T(8,128)} %get-tuple-element.20, f32[2048,1000]{0,1:T(8,128)} %param.20), kind=kOutput, calls=%fused_computation.44 | convolution fusion | flops 524806016 | bytes 9757088 | tf_op jit(solution)/shard_map/nc,kc->nk/dot_general | solution.py:247
  78.8 0.0 slice-start
  78.8 0.0 copy-start.1
  78.8 0.0 copy-start.2
  78.9 0.2 exponential_reduce_fusion
  79.0 1.0 broadcast_multiply_fusion.1
  80.1 0.0 copy-start.3
  80.1 0.0 slice-start.1
  80.1 4.6 %fusion.10 = f32[1000,2048]{1,0:T(8,128)} fusion(f32[128,2048]{1,0:T(8,128)S(1)} %copy-done, f32[128,1000]{0,1:T(8,128)S(1)} %get-tuple-element.50, s32[128]{0:T(128)S(1)} %copy-done.9, f32[128]{0:T(128)S(1)} %log.9, f32[128]{0:T(128)S(1)} %get-tuple-element.49), kind=kOutput, calls=%fused_computation.27 | convolution fusion | flops 525574144 | bytes 9754112 | tf_op jit(solution)/shard_map/nk,nc->kc/dot_general | solution.py:278
  84.7 2.0 multiply_reduce_fusion.4
  86.7 1.6 multiply_subtract_fusion
  88.3 50.8 %bwd_conv.1 = f32[1024,2048]{1,0:T(8,128)} custom-call(bf16[1024,6272]{1,0:T(8,128)(2,1)} %get-tuple-element.17.at_ref, f32[6272,2048]{1,0:T(8,128)} %get-tuple-element.18.z_ref, bf16[6272,2048]{1,0:T(8,128)(2,1)} %bitcast.65, f32[1,2048]{1,0:T(1,128)} %copy-done.3, f32[1,2048]{1,0:T(1,128)} %get-tuple-element.48.sh_ref, ...), custom_call_target="tpu_custom_call" | custom-call | flops 26306674688 | bytes 120000000 | tf_op jit(solution)/shard_map/bwd_conv/pallas_call | solution.py:206
  139.1 0.0 all-reduce.4.cloned.1.call-update
  139.2 0.0 copy-start.10
  139.2 0.0 copy-start.7
  139.2 0.0 copy-start.8
  139.2 6.0 %fusion = f32[]{:T(128)} fusion(f32[2048,1000]{0,1:T(8,128)} %param.20), kind=kLoop, calls=%fused_computation.8 | loop fusion | flops 4095999 | bytes 8192004 | tf_op jit(solution)/shard_map/reduce_sum | solution.py:234
  145.9 6.1 %multiply_reduce_fusion.1 = f32[]{:T(128)} fusion(f32[1024,2048]{1,0:T(8,128)} %w_ref.1), kind=kLoop, calls=%fused_computation.2 | loop fusion | flops 4194303 | bytes 8388612 | tf_op jit(solution)/shard_map/reduce_sum | solution.py:234
  153.4 0.8 multiply_reduce_fusion.5
  154.9 25.3 %all-reduce = (f32[2048]{0:T(1024)S(1)}, f32[2048]{0:T(1024)S(1)}, f32[1000]{0:T(1024)S(1)}, f32[]{:T(128)}) all-reduce(f32[2048]{0:T(1024)S(1)} %get-tuple-element.24, f32[2048]{0:T(1024)S(1)} %get-tuple-element.23, f32[1000]{0:T(1024)S(1)} %get-tuple-element.26, f32[]{:T(128)S(6)} %div.41), channel_id=1, replica_groups=mesh['dp'=8] {'dp'}, use_global_device_ids=true, to_apply=%region_7.8 | all-reduce | flops 5097 | bytes 40776 | tf_op jit(solution)/shard_map/psum | solution.py:280
  180.2 0.6 fusion.17
  180.8 0.6 fusion.18
  181.4 165.0 %all-reduce.4.cloned.1.call-done = (f32[1024,2048]{1,0:T(8,128)}, f32[1000,2048]{1,0:T(8,128)}) async-done(((f32[1024,2048]{1,0:T(8,128)}, f32[1000,2048]{1,0:T(8,128)}), (f32[1024,2048]{1,0:T(8,128)}, f32[1000,2048]{1,0:T(8,128)})) %all-reduce.4.cloned.1.call-update) | async-done | bytes 16580624 | tf_op jit(solution)/shard_map/psum | solution.py:280
  346.5 6.0 %multiply_reduce_fusion.2 = f32[]{:T(128)} fusion(f32[1000,2048]{1,0:T(8,128)} %get-tuple-element.32), kind=kLoop, calls=%fused_computation.12 | loop fusion | flops 4095999 | bytes 8192004 | tf_op jit(solution)/shard_map/reduce_sum | solution.py:235
  353.2 6.1 %multiply_reduce_fusion = f32[]{:T(128)} fusion(f32[1024,2048]{1,0:T(8,128)} %get-tuple-element.31), kind=kLoop, calls=%fused_computation.1 | loop fusion | flops 4194303 | bytes 8388612 | tf_op jit(solution)/shard_map/reduce_sum | solution.py:235
  360.1 13.9 %fusion.6 = (f32[2048,1000]{0,1:T(8,128)}, f32[2048,1000]{0,1:T(8,128)}) fusion(f32[1000,2048]{1,0:T(8,128)} %get-tuple-element.32, f32[2048,1000]{0,1:T(8,128)} %param.20, f32[]{:T(128)S(6)} %mul.166, f32[2048,1000]{0,1:T(8,128)} %param.25), kind=kLoop, calls=%fused_computation.15 | loop fusion | flops 12288000 | bytes 40960004 | tf_op jit(solution)/shard_map/transpose | solution.py:286
  374.0 14.4 %fusion.20 = (f32[1024,2048]{1,0:T(8,128)}, f32[1024,2048]{1,0:T(8,128)}) fusion(f32[1024,2048]{1,0:T(8,128)} %w_ref.1, f32[1024,2048]{1,0:T(8,128)} %get-tuple-element.31, f32[]{:T(128)S(6)} %mul.151, f32[1024,2048]{1,0:T(8,128)} %param.22), kind=kLoop, calls=%fused_computation.43 | loop fusion | flops 12582912 | bytes 41943044 | tf_op jit(solution)/shard_map/sub | solution.py:238
  (18 shorter events, 0.0 us)
Async XLA Ops:
  7.2 339.3 %all-reduce.4.cloned.1.call-start = ((), (), s32[]{:S(2)}) async-start(), calls=%async_computation | async-start | bytes 33161216 | tf_op jit(solution)/shard_map/psum | solution.py:280
  7.2 66.6 %copy-start.6 = (f32[1000]{0:T(1024)S(1)}, f32[1000]{0:T(1024)}, u32[]{:S(2)}) copy-start(f32[1000]{0:T(1024)} %param.21) | copy-start | bytes 12004
  73.8 5.2 %copy-start.5 = (f32[2048]{0:T(1024)S(1)}, f32[2048]{0:T(1024)}, u32[]{:S(2)}) copy-start(f32[2048]{0:T(1024)} %param.18) | copy-start | bytes 24580
  73.8 6.2 %copy-start = (f32[128,2048]{1,0:T(8,128)S(1)}, f32[128,2048]{1,0:T(8,128)}, u32[]{:S(2)}) copy-start(f32[128,2048]{1,0:T(8,128)} %get-tuple-element.20) | copy-start | bytes 3145732
  73.8 6.2 %copy-start.9 = (s32[128]{0:T(128)S(1)}, s32[128]{0:T(128)}, u32[]{:S(2)}) copy-start(s32[128]{0:T(128)} %param.16) | copy-start | bytes 1540
  78.8 5.9 %slice-start = ((s8[8192000]{0:T(1024)(128)(4,1)}), s8[4194304]{0:T(1024)(128)(4,1)S(1)}, s32[]{:S(2)}) async-start(s8[8192000]{0:T(1024)(128)(4,1)} %bitcast.62), calls=%async_computation.1 | async-start | bytes 8388608
  78.8 5.9 %copy-start.1 = (f32[128,2048]{1,0:T(8,128)S(1)}, f32[128,2048]{1,0:T(8,128)}, u32[]{:S(2)}) copy-start(f32[128,2048]{1,0:T(8,128)} %get-tuple-element.21) | copy-start | bytes 3145732
  78.8 5.9 %copy-start.2 = (f32[128,2048]{1,0:T(8,128)S(1)}, f32[128,2048]{1,0:T(8,128)}, u32[]{:S(2)}) copy-start(f32[128,2048]{1,0:T(8,128)} %get-tuple-element.22) | copy-start | bytes 3145732
  80.1 6.7 %copy-start.3 = (f32[1,2048]{1,0:T(1,128)}, f32[1,2048]{1,0:T(1,128)S(1)}, u32[]{:S(2)}) copy-start(f32[1,2048]{1,0:T(1,128)S(1)} %get-tuple-element.42.sc_ref) | copy-start | bytes 24580
  80.1 4.6 %slice-start.1 = ((s8[8192000]{0:T(1024)(128)(4,1)}), s8[3997696]{0:T(1024)(128)(4,1)S(1)}, s32[]{:S(2)}) async-start(s8[8192000]{0:T(1024)(128)(4,1)} %bitcast.62), calls=%async_computation.2 | async-start | bytes 7995392
  84.7 2.1 copy-start.4
  139.2 41.1 %copy-start.10 = (f32[1000]{0:T(1024)S(1)}, f32[1000]{0:T(1024)}, u32[]{:S(2)}) copy-start(f32[1000]{0:T(1024)} %param.26) | copy-start | bytes 12004
  139.2 41.7 %copy-start.7 = (f32[2048]{0:T(1024)S(1)}, f32[2048]{0:T(1024)}, u32[]{:S(2)}) copy-start(f32[2048]{0:T(1024)} %param.24) | copy-start | bytes 24580
  139.2 41.6 %copy-start.8 = (f32[2048]{0:T(1024)S(1)}, f32[2048]{0:T(1024)}, u32[]{:S(2)}) copy-start(f32[2048]{0:T(1024)} %param.23) | copy-start | bytes 24580
Sparse Core Ops, SparseCore 0:
  139.3 207.1 all-reduce.3

commit v2 on v1

--- a/solution.py
+++ b/solution.py
@@ -17,8 +17,54 @@
 NT = 16
 MS = 1
 
-
-def fwd_kernel(a_ref, w_ref, s_ref, g_ref, b_ref, z_hbm, at_ref, pool_ref, cnt_ref, sx_ref, st_ref, zbuf, wbf, stat, zsem):
+MESH = pl.DeviceIdType.MESH
+TAIL = 3
+
+
+def position():
+    me = lax.axis_index('dp')
+    core = lax.rem(me, 2)
+    x = lax.rem(me // 2, 2)
+    y = me // 4
+    return me, core, x, y
+
+
+def dev(core, x, y):
+    return (y * 2 + x) * 2 + core
+
+
+def enter_all():
+    me = lax.axis_index('dp')
+    bar = pltpu.get_barrier_semaphore()
+    for k in range(1, 8):
+        pl.semaphore_signal(bar, inc=1, device_id=(lax.rem(me + k, 8),), device_id_type=MESH)
+    pl.semaphore_wait(bar, 7)
+
+
+def rcopy(src, dst, send, recv, target):
+    return pltpu.make_async_remote_copy(src_ref=src, dst_ref=dst, send_sem=send, recv_sem=recv, device_id=(target,), device_id_type=MESH)
+
+
+def gather_copies(buf, send, recv, b):
+    me, core, x, y = position()
+    ca = pl.ds(pl.multiple_of(b * CB, CB), CB // 2)
+    cb = pl.ds(pl.multiple_of(b * CB + CB // 2, CB // 2), CB // 2)
+    cc = pl.ds(pl.multiple_of(b * CB, CB), CB)
+    xn, yn, pn = dev(core, 1 - x, y), dev(core, x, 1 - y), dev(1 - core, x, y)
+    def cp(k, ref, target):
+        return rcopy(ref, ref, send.at[k, b], recv.at[k, b], target)
+    return (cp(0, buf.at[core, y, x, :, ca], yn), cp(1, buf.at[core, y, x, :, cb], xn),
+            cp(2, buf.at[core, :, x, :, ca], xn), cp(3, buf.at[core, y, :, :, cb], yn),
+            cp(4, buf.at[core, :, :, :, cc], pn))
+
+
+def when_block(b, fn):
+    @pl.when(jnp.logical_and(b >= 0, b < NB))
+    def _():
+        fn(b)
+
+
+def fwd_kernel(a_ref, w_ref, s_ref, g_ref, b_ref, lab_ref, z_hbm, at_ref, pool_ref, cnt_ref, sx_ref, st_ref, pall_ref, lall_ref, zbuf, wbf, stat, pfull, lfull, zsem, gs, gr, ls, lr):
     j = pl.program_id(0)
     slot = lax.rem(j, 2)
     prev = 1 - slot
@@ -26,7 +72,41 @@
     def z_copy(jj, sl):
         return pltpu.make_async_copy(zbuf.at[sl], z_hbm.at[:, pl.ds(pl.multiple_of(jj * CB, CB), CB)], zsem.at[sl])
 
-    @pl.when(j >= 2)
+    me, core, x, y = position()
+
+    def label_copy(k):
+        return rcopy(lab_ref, lfull.at[core, y, x], ls.at[k], lr.at[k], lax.rem(me + k, 8))
+
+    @pl.when(j == 0)
+    def _():
+        enter_all()
+        for k in range(1, 8):
+            label_copy(k).start()
+        lfull[core, y, x] = lab_ref[...]
+
+    def second(b):
+        c = gather_copies(pfull, gs, gr, b)
+        c[0].wait_recv()
+        c[1].wait_recv()
+        c[2].start()
+        c[3].start()
+
+    def third(b):
+        c = gather_copies(pfull, gs, gr, b)
+        c[2].wait_recv()
+        c[3].wait_recv()
+        c[4].start()
+
+    def last(b):
+        gather_copies(pfull, gs, gr, b)[4].wait_recv()
+        for q in range(8):
+            pall_ref[q * IMG:(q + 1) * IMG, :] = pfull[q // 4, (q // 2) % 2, q % 2, :, pl.ds(pl.multiple_of(b * CB, CB), CB)].astype(jnp.bfloat16)
+
+    when_block(j - 2, second)
+    when_block(j - 3, third)
+    when_block(j - 4, last)
+
+    @pl.when(jnp.logical_and(j >= 2, j < NB + 2))
     def _():
         z_copy(j - 2, slot).wait()
 
@@ -82,7 +162,12 @@
 
         lax.fori_loop(0, NCH, chunk, 0)
         if do_post:
-            pool_ref[...] = pool_ref[...] * (1.0 / POS)
+            pooled = pool_ref[...] * (1.0 / POS)
+            pool_ref[...] = pooled
+            pfull[core, y, x, :, pl.ds(pl.multiple_of((j - 1) * CB, CB), CB)] = pooled
+            c = gather_copies(pfull, gs, gr, j - 1)
+            c[0].start()
+            c[1].start()
             sx_ref[...] = (sx_ref[...] - mean * cnt_ref[...]) * inv
         if do_mm:
             dm = jnp.sum(stat[0:8, :], axis=0, keepdims=True) * (1.0 / ROWS)
@@ -103,22 +188,35 @@
     @pl.when(j == NB)
     def _():
         step(False, True)
-        z_copy(NB - 1, (NB - 1) % 2).wait()
-
-
-def forward(a, w, s, gamma, beta):
-    prev = lambda j: (0, jnp.maximum(j - 1, 0))
+
+    @pl.when(j == NB + TAIL)
+    def _():
+        for k in range(1, 8):
+            label_copy(k).wait()
+        lall_ref[...] = lfull[...]
+
+        def drain(b, carry):
+            for c in gather_copies(pfull, gs, gr, b):
+                c.wait_send()
+            return carry
+        lax.fori_loop(0, NB, drain, 0)
+
+
+def forward(a, w, s, gamma, beta, labels):
+    prev = lambda j: (0, jnp.clip(j - 1, 0, NB - 1))
+    late = lambda j: (0, jnp.clip(j - 4, 0, NB - 1))
     cur = lambda j: (0, jnp.minimum(j, NB - 1))
     f32 = jnp.float32
     return pl.pallas_call(
         fwd_kernel,
-        grid=(NB + 1,),
+        grid=(NB + 1 + TAIL,),
         in_specs=[
             pl.BlockSpec((ROWS, CIN), lambda j: (0, 0), pipeline_mode=pl.Buffered(1)),
             pl.BlockSpec((CIN, CB), cur),
             pl.BlockSpec((ROWS, CB), prev),
             pl.BlockSpec((1, CB), prev),
             pl.BlockSpec((1, CB), prev),
+            pl.BlockSpec((8, IMG), lambda j: (0, 0)),
         ],
         out_specs=[
             pl.BlockSpec(memory_space=pl.ANY),
@@ -127,6 +225,8 @@
             pl.BlockSpec((IMG, CB), prev),
             pl.BlockSpec((IMG, CB), prev),
             pl.BlockSpec((8, CB), prev),
+            pl.BlockSpec((8 * IMG, CB), late),
+            pl.BlockSpec((2, 2, 2, 8, IMG), lambda j: (0, 0, 0, 0, 0)),
         ],
         out_shape=[
             jax.ShapeDtypeStruct((ROWS, COUT), f32),
@@ -135,23 +235,124 @@
             jax.ShapeDtypeStruct((IMG, COUT), f32),
             jax.ShapeDtypeStruct((IMG, COUT), f32),
             jax.ShapeDtypeStruct((8, COUT), f32),
+            jax.ShapeDtypeStruct((8 * IMG, COUT), jnp.bfloat16),
+            jax.ShapeDtypeStruct((2, 2, 2, 8, IMG), jnp.int32),
         ],
         scratch_shapes=[
             pltpu.VMEM((2, ROWS, CB), f32),
             pltpu.VMEM((CIN, CB), jnp.bfloat16),
             pltpu.VMEM((24, CB), f32),
+            pltpu.VMEM((2, 2, 2, IMG, COUT), f32),
+            pltpu.VMEM((2, 2, 2, 8, IMG), jnp.int32),
             pltpu.SemaphoreType.DMA((2,)),
+            pltpu.SemaphoreType.DMA((5, NB)),
+            pltpu.SemaphoreType.DMA((5, NB)),
+            pltpu.SemaphoreType.DMA((8,)),
+            pltpu.SemaphoreType.DMA((8,)),
         ],
-        compiler_params=pltpu.CompilerParams(vmem_limit_bytes=60 * 1024 * 1024),
+        compiler_params=pltpu.CompilerParams(vmem_limit_bytes=60 * 1024 * 1024, collective_id=0, has_side_effects=True),
         cost_estimate=pl.CostEstimate(flops=2 * ROWS * CIN * COUT, bytes_accessed=120_000_000, transcendentals=0),
         name="fwd_conv",
-    )(a, w, s, gamma, beta)
-
-
-def bwd_kernel(at_ref, z_ref, s_ref, sc_ref, sh_ref, bb_ref, cc_ref, da_ref, dw_ref, dz):
+    )(a, w, s, gamma, beta, labels)
+
+
+BTAIL = 7
+QR = CIN // 8
+
+
+def bwd_kernel(at_ref, z_ref, s_ref, sc_ref, sh_ref, bb_ref, cc_ref, da_ref, db_ref, g_hbm, dbo_ref,
+               dz, dw, rd, ha, hb, ra, rb, ka, kb, r2a, r2b, gfull, dball, ss, rs, gs, gr, bs, br, osem):
     j = pl.program_id(0)
     slot = lax.rem(j, 2)
     prev = 1 - slot
+    me, core, x, y = position()
+    xn, yn, pn = dev(core, 1 - x, y), dev(core, x, 1 - y), dev(1 - core, x, y)
+    half = CIN // 2
+    HC = CB // 2
+
+    def db_copy(k):
+        return rcopy(db_ref, dball.at[me], bs.at[k], br.at[k], lax.rem(me + k, 8))
+
+    @pl.when(j == 0)
+    def _():
+        enter_all()
+        for k in range(1, 8):
+            db_copy(k).start()
+        dball[me] = db_ref[...]
+
+    def out_copy(b):
+        cc = pl.ds(pl.multiple_of(b * CB, CB), CB)
+        return pltpu.make_async_copy(gfull.at[:, :, :, :, cc], g_hbm.at[:, :, :, :, cc], osem.at[b])
+
+    def core_copy(b):
+        return rcopy(dw.at[lax.rem(b, 2), pl.ds(pl.multiple_of((1 - core) * half, half), half), :], rd.at[b], ss.at[0, b], rs.at[0, b], pn)
+
+    def first_copies(b):
+        sl = lax.rem(b, 2)
+        return (rcopy(ha.at[sl, 1 - x], ra.at[b], ss.at[1, b], rs.at[1, b], xn),
+                rcopy(hb.at[sl, 1 - y], rb.at[b], ss.at[2, b], rs.at[2, b], yn))
+
+    def second_copies(b):
+        sl = lax.rem(b, 2)
+        return (rcopy(ka.at[sl, 1 - y], r2a.at[b], ss.at[3, b], rs.at[3, b], yn),
+                rcopy(kb.at[sl, 1 - x], r2b.at[b], ss.at[4, b], rs.at[4, b], xn))
+
+    def stage1(b):
+        c = core_copy(b)
+        c.wait()
+        sl = lax.rem(b, 2)
+        for py in range(2):
+            for px in range(2):
+                q = py * 2 + px
+                own = pl.ds(pl.multiple_of(core * half + q * QR, QR), QR)
+                ha[sl, px, py] = dw[sl, own, 0:HC] + rd[b, q * QR:(q + 1) * QR, 0:HC]
+                hb[sl, py, px] = dw[sl, own, HC:CB] + rd[b, q * QR:(q + 1) * QR, HC:CB]
+        for f in first_copies(b):
+            f.start()
+
+    def stage2(b):
+        sl = lax.rem(b, 2)
+        for f in first_copies(b):
+            f.wait()
+        for k in range(2):
+            ka[sl, k] = ha[sl, x, k] + ra[b, k]
+            kb[sl, k] = hb[sl, y, k] + rb[b, k]
+        for f in second_copies(b):
+            f.start()
+
+    def stage3(b):
+        sl = lax.rem(b, 2)
+        for f in second_copies(b):
+            f.wait()
+        gfull[core, y, x, :, pl.ds(pl.multiple_of(b * CB, CB), HC)] = ka[sl, y] + r2a[b]
+        gfull[core, y, x, :, pl.ds(pl.multiple_of(b * CB + HC, HC), HC)] = kb[sl, x] + r2b[b]
+        c = gather_copies(gfull, gs, gr, b)
+        c[0].start()
+        c[1].start()
+
+    def stage4(b):
+        c = gather_copies(gfull, gs, gr, b)
+        c[0].wait_recv()
+        c[1].wait_recv()
+        c[2].start()
+        c[3].start()
+
+    def stage5(b):
+        c = gather_copies(gfull, gs, gr, b)
+        c[2].wait_recv()
+        c[3].wait_recv()
+        c[4].start()
+
+    def stage6(b):
+        gather_copies(gfull, gs, gr, b)[4].wait_recv()
+        out_copy(b).start()
+
+    when_block(j - 2, stage1)
+    when_block(j - 3, stage2)
+    when_block(j - 4, stage3)
+    when_block(j - 5, stage4)
+    when_block(j - 6, stage5)
+    when_block(j - 7, stage6)
 
     def step(do_pre, do_mm):
         if do_pre:
@@ -173,18 +374,20 @@
             return jnp.dot(at_ref[:, pl.ds(base, size)], dz[prev, pl.ds(base, size), :], preferred_element_type=jnp.float32)
 
         if do_mm:
-            dw_ref[...] = mm(5376, 896)
+            dw[prev] = mm(5376, 896)
         if do_pre:
             pre(5376, 7)
 
         def chunk(i, carry):
             base = pl.multiple_of(i * 1792, 1792)
             if do_mm:
-                dw_ref[...] += mm(base, 1792)
+                dw[prev] += mm(base, 1792)
             if do_pre:
                 pre(base, 14)
             return carry
         lax.fori_loop(0, 3, chunk, 0)
+        if do_mm:
+            core_copy(j - 1).start()
 
     @pl.when(j == 0)
     def _():
@@ -198,28 +401,66 @@
     def _():
         step(False, True)
 
-
-def backward(at, z, s, sc, sh, bb, cc, da):
-    prev = lambda j: (0, jnp.maximum(j - 1, 0))
+    @pl.when(j == NB + BTAIL - 1)
+    def _():
+        for k in range(1, 8):
+            db_copy(k).wait()
+        acc = dball[0]
+        for k in range(1, 8):
+            acc = acc + dball[k]
+        dbo_ref[...] = acc
+
+        def drain(b, carry):
+            for c in gather_copies(gfull, gs, gr, b):
+                c.wait_send()
+            out_copy(b).wait()
+            return carry
+        lax.fori_loop(0, NB, drain, 0)
+
+
+def backward(at, z, s, sc, sh, bb, cc, da, dgb):
+    f32 = jnp.float32
     cur = lambda j: (0, jnp.minimum(j, NB - 1))
     row = pl.BlockSpec((1, CB), cur)
     return pl.pallas_call(
         bwd_kernel,
-        grid=(NB + 1,),
+        grid=(NB + BTAIL,),
         in_specs=[
             pl.BlockSpec((CIN, ROWS), lambda j: (0, 0), pipeline_mode=pl.Buffered(1)),
             pl.BlockSpec((ROWS, CB), cur),
             pl.BlockSpec((ROWS, CB), cur),
             row, row, row, row,
             pl.BlockSpec((IMG, CB), cur),
+            pl.BlockSpec((16, CB), lambda j: (0, 0)),
         ],
-        out_specs=pl.BlockSpec((CIN, CB), prev),
-        out_shape=jax.ShapeDtypeStruct((CIN, COUT), jnp.float32),
-        scratch_shapes=[pltpu.VMEM((2, ROWS, CB), jnp.bfloat16)],
-        compiler_params=pltpu.CompilerParams(vmem_limit_bytes=60 * 1024 * 1024),
+        out_specs=[pl.BlockSpec(memory_space=pl.ANY), pl.BlockSpec((16, CB), lambda j: (0, 0))],
+        out_shape=[jax.ShapeDtypeStruct((2, 2, 2, QR, COUT), f32), jax.ShapeDtypeStruct((16, CB), f32)],
+        scratch_shapes=[
+            pltpu.VMEM((2, ROWS, CB), jnp.bfloat16),
+            pltpu.VMEM((2, CIN, CB), f32),
+            pltpu.VMEM((NB, CIN // 2, CB), f32),
+            pltpu.VMEM((2, 2, 2, QR, CB // 2), f32),
+            pltpu.VMEM((2, 2, 2, QR, CB // 2), f32),
+            pltpu.VMEM((NB, 2, QR, CB // 2), f32),
+            pltpu.VMEM((NB, 2, QR, CB // 2), f32),
+            pltpu.VMEM((2, 2, QR, CB // 2), f32),
+            pltpu.VMEM((2, 2, QR, CB // 2), f32),
+            pltpu.VMEM((NB, QR, CB // 2), f32),
+            pltpu.VMEM((NB, QR, CB // 2), f32),
+            pltpu.VMEM((2, 2, 2, QR, COUT), f32),
+            pltpu.VMEM((8, 16, CB), f32),
+            pltpu.SemaphoreType.DMA((5, NB)),
+            pltpu.SemaphoreType.DMA((5, NB)),
+            pltpu.SemaphoreType.DMA((5, NB)),
+            pltpu.SemaphoreType.DMA((5, NB)),
+            pltpu.SemaphoreType.DMA((8,)),
+            pltpu.SemaphoreType.DMA((8,)),
+            pltpu.SemaphoreType.DMA((NB,)),
+        ],
+        compiler_params=pltpu.CompilerParams(vmem_limit_bytes=63 * 1024 * 1024, collective_id=1, has_side_effects=True),
         cost_estimate=pl.CostEstimate(flops=2 * ROWS * CIN * COUT, bytes_accessed=120_000_000, transcendentals=0),
         name="bwd_conv",
-    )(at, z, s, sc, sh, bb, cc, da)
+    )(at, z, s, sc, sh, bb, cc, da, dgb)
 import jax
 import jax.numpy as jnp
 from jax.sharding import PartitionSpec as P
@@ -238,11 +479,10 @@
     return weight - new_vel, new_vel
 
 
-def head(pooled, labels, w_fc_t, fc_bias, total):
+def head(pb, labels, w_fc_t, fc_bias, total):
     bf = jnp.bfloat16
     f32 = jnp.float32
     classes = w_fc_t.shape[0]
-    pb = pooled.astype(bf)
     wb = w_fc_t.astype(bf)
     logits = jnp.einsum('nc,kc->nk', pb, wb, preferred_element_type=f32) + fc_bias
     log_prob = jax.nn.log_softmax(logits, axis=-1)
@@ -262,8 +502,9 @@
         a = act_in.transpose(1, 2, 0, 3).reshape(ROWS, CIN)
         s = shortcut.transpose(1, 2, 0, 3).reshape(ROWS, COUT)
         w_fc_t = w_fc.T
-        z, at, pooled, cnt, sx, st = forward(a, w_conv, s, gamma[None], beta[None])
-        pb, wb, dl, dlb, loss = head(pooled, labels, w_fc_t, fc_bias, total)
+        lab8 = jnp.broadcast_to(labels[None], (8, IMG))
+        z, at, pooled, cnt, sx, st, pall, lall = forward(a, w_conv, s, gamma[None], beta[None], lab8)
+        _, wb, _, dlb, _ = head(pooled.astype(jnp.bfloat16), labels, w_fc_t, fc_bias, total)
         dpool = jnp.einsum('nk,kc->nc', dlb, wb, preferred_element_type=f32) / POS
         mean = st[0:1]
         inv = st[1:2]
@@ -274,10 +515,14 @@
         sh = beta[None] - mean * sc
         cc = -(sc * inv) * (d_gamma / ROWS)
         bb = -sc * (d_beta / ROWS) - mean * cc
-        dw = backward(at, z, s, sc, sh, bb, cc, dpool * sc)
-        g_fc_t = jnp.einsum('nk,nc->kc', dlb, pb, preferred_element_type=f32)
+        dgb = jnp.concatenate([d_gamma.reshape(8, CB), d_beta.reshape(8, CB)])
+        g8, dgb = backward(at, z, s, sc, sh, bb, cc, dpool * sc, dgb)
+        g_conv = g8.reshape(CIN, COUT)
+        g_gamma = dgb[0:8].reshape(COUT)
+        g_beta = dgb[8:16].reshape(COUT)
+        _, _, dl, dlb, loss = head(pall, lall[:, :, :, 0].reshape(total), w_fc_t, fc_bias, total)
+        g_fc_t = jnp.einsum('nk,nc->kc', dlb, pall, preferred_element_type=f32)
         g_bias = jnp.sum(dl, axis=0)
-        g_conv, g_gamma, g_beta, g_fc_t, g_bias, loss = lax.psum((dw, d_gamma[0], d_beta[0], g_fc_t, g_bias, loss), 'dp')
         conv_new, conv_vel_new = lars_update(w_conv, g_conv, vel_conv, lr)
         fc_new, fc_vel_new = lars_update(w_fc_t, g_fc_t, vel_fc.T, lr)
         gv = MOMENTUM * vel_gamma + lr * g_gamma

time: 397 us -> 301 us (0.76)
  waiting for transfers between devices: 165 us -> 0 us
  Pallas kernels: 117 us -> 204 us
  blocking collectives: 25.3 us -> 0 us
  matrix products: 11.6 us -> 31.7 us
  between operations: 18.4 us -> 6.16 us
    psum x1 -> x0, waiting for transfers between devices: 165 us -> none  [local_step(): lax.psum((dw, d_gamma[0], d_beta[0], g_fc_t, g_bias, loss), 'dp')]
    pallas_call x2, Pallas kernels: 117 us -> 204 us  [the longest x1 104 us: forward(): pl.pallas_call(fwd_kernel, grid=(NB + 1 + TAIL,), in_specs=[pl.BlockSpec(...]
    psum x1 -> x0, blocking collectives: 25.3 us -> none  [local_step(): lax.psum((dw, d_gamma[0], d_beta[0], g_fc_t, g_bias, loss), 'dp')]
    transpose x1 -> x0, other arithmetic: 13.9 us -> none  [local_step(): return (conv_new, gamma - gv, beta - bv, fc_new.T, fc_bias - cv, conv_vel...]
    sub x1 -> x2, other arithmetic: 14.4 us -> 26.5 us  [lars_update(): return (weight - new_vel, new_vel)]
    dot_general x1, matrix products: 4.6 us -> 13 us  [local_step(): g_fc_t = jnp.einsum('nk,nc->kc', dlb, pall, preferred_element_type=f32)]
    dot_general x1 -> x2, matrix products: 4.98 us -> 13.2 us  [head(): jnp.einsum('nc,kc->nk', pb, wb, preferred_element_type=f32) + fc_bias]
    reduce_sum x2 -> x1, other arithmetic: 12.2 us -> 6.15 us  [lars_update(): g_norm = jnp.sqrt(jnp.sum(jnp.square(gradient)))]
  transfers between devices with their start and end apart: 1 -> 0, of which waited for: 1 -> 0; matrix products, arithmetic and copies ran while one was open for 4% -> 0% of each run, Pallas kernels for 0% -> 0%
where the time goes in v2:
time: 301 us; the launch traced here: 300 us
  Pallas kernels  204 us (68%)
  other arithmetic  54.8 us (18%)
  matrix products  31.7 us (11%)
  between operations  6.16 us (2%)
  local copies, waits for them, and re-layouts  3.54 us (1%)
    pallas_call x1, Pallas kernels, forward(): pl.pallas_call(fwd_kernel, grid=(NB + 1 + TAIL,), in_specs=[pl.BlockSpec(...  104 us
    pallas_call x1, Pallas kernels, backward(): pl.pallas_call(bwd_kernel, grid=(NB + BTAIL,), in_specs=[pl.BlockSpec((CI...  100 us
    sub x2, other arithmetic, lars_update(): return (weight - new_vel, new_vel)  26.5 us
    dot_general x2, matrix products, head(): jnp.einsum('nc,kc->nk', pb, wb, preferred_element_type=f32) + fc_bias  13.2 us
    dot_general x1, matrix products, local_step(): g_fc_t = jnp.einsum('nk,nc->kc', dlb, pall, preferred_element_type=f32)  13 us
    reduce_sum x2, other arithmetic, lars_update(): w_norm = jnp.sqrt(jnp.sum(jnp.square(weight)))  12.3 us
    reduce_sum x1, other arithmetic, lars_update(): g_norm = jnp.sqrt(jnp.sum(jnp.square(gradient)))  6.15 us

profile of v2, /device:TPU:1, one launch (start us, length us, event | category | flops | bytes accessed | tf_op | source)
XLA Modules:
  0.0 300.0 jit_solution(1673706980404055167)
XLA Ops:
  1.3 6.1 %multiply_reduce_fusion.3 = f32[]{:T(128)} fusion(f32[2048,1000]{0,1:T(8,128)} %param.20), kind=kLoop, calls=%fused_computation.9 | loop fusion | flops 4095999 | bytes 8192004 | tf_op jit(solution)/shard_map/reduce_sum | solution.py:475
  8.1 0.0 copy-start.11
  8.1 6.1 %multiply_reduce_fusion.1 = f32[]{:T(128)} fusion(f32[1024,2048]{1,0:T(8,128)} %w_ref.1), kind=kLoop, calls=%fused_computation.4 | loop fusion | flops 4194303 | bytes 8388612 | tf_op jit(solution)/shard_map/reduce_sum | solution.py:475
  15.0 0.6 broadcast_in_dim.14.lab_ref
  15.6 103.6 %fwd_conv.1 = (f32[6272,2048]{1,0:T(8,128)}, bf16[1024,6272]{1,0:T(8,128)(2,1)}, f32[128,2048]{1,0:T(8,128)}, f32[128,2048]{1,0:T(8,128)}, f32[128,2048]{1,0:T(8...) custom-call(bf16[6272,1024]{1,0:T(8,128)(2,1)} %bitcast.49, ...), custom_call_target="tpu_custom_call" | custom-call | flops 26306674688 | bytes 120000000 | tf_op jit(solution)/shard_map/fwd_conv/pallas_call | solution.py:210
  119.2 0.8 slice.19
  120.0 0.9 broadcast_multiply_fusion.1
  120.8 0.0 copy-start.6
  120.8 0.0 copy-done.3
  120.9 5.0 %fusion.35 = (f32[128]{0:T(128)S(1)}, f32[128,1000]{0,1:T(8,128)S(1)}) fusion(f32[1000]{0:T(1024)S(1)} %copy-done.3, f32[2048,1000]{0,1:T(8,128)} %param.20, f32[128,2048]{1,0:T(8,128)} %get-tuple-element.24), kind=kOutput, calls=%fused_computation.66 | convolution fusion | flops 526854016 | bytes 9757088 | tf_op jit(solution)/shard_map/nc,kc->nk/dot_general | solution.py:487
  125.9 0.2 exponential_reduce_fusion.1
  126.1 0.0 copy-start.4
  126.1 5.4 %multiply_reduce_fusion.6 = (f32[2048]{0:T(1024)S(1)}, f32[2048]{0:T(1024)S(1)}, f32[128,2048]{1,0:T(8,128)}) fusion(f32[128,2048]{1,0:T(8,128)S(1)} %copy-done.1, f32[128,2048]{1,0:T(8,128)S(1)} %copy-done.2, f32[2048]{0:T(1024)S(1)} %bitcast.36, f32[2048,1000]{0,1:T(8,128)} %param.20, f32[128,1000]{0,1:T(8,128)S(1)} %get-tuple-element.54, ...), kind=kOutput, calls=%fused_computation.21 | convolution fusion | flops 528928768 | bytes 11875840 | tf_op jit(solution)/shard_map/nk,kc->nc/dot_general | solution.py:508
  131.5 0.6 pad_maximum_fusion.db_ref
  132.2 1.6 multiply_subtract_fusion
  133.7 100.3 %bwd_conv.1 = (f32[2,2,2,128,2048]{4,3,2,1,0:T(8,128)}, f32[16,256]{1,0:T(8,128)}) custom-call(bf16[1024,6272]{1,0:T(8,128)(2,1)} %get-tuple-element.21.at_ref, f32[6272,2048]{1,0:T(8,128)} %get-tuple-element.22.z_ref, bf16[6272,2048]{1,0:T(8,128)(2,1)} %bitcast.48, f32[1,2048]{1,0:T(1,128)} %copy-done.6, f32[1,2048]{1,0:T(1,128)} %get-tuple-element.50.sh_ref, ...), custom_call_target="tpu_custom_call" | custom-call | flops 26306674688 | bytes 120000000 | tf_op jit(solution)/shard_map/bwd_conv/pallas_call | solution.py:425
  234.0 0.0 copy-start.8
  234.0 0.0 copy-start.9
  234.0 6.2 %multiply_reduce_fusion = f32[]{:T(128)} fusion(f32[2,2,2,128,2048]{4,3,2,1,0:T(8,128)} %get-tuple-element.27), kind=kLoop, calls=%fused_computation.3 | loop fusion | flops 4194303 | bytes 8388612 | tf_op jit(solution)/shard_map/reduce_sum | solution.py:476
  241.0 0.6 fusion.32
  241.6 0.6 fusion.31
  242.2 8.2 %add_reduce_fusion = (f32[1024]{0:T(1024)S(1)}, f32[1024,1000]{0,1:T(8,128)S(1)}) fusion(f32[1000]{0:T(1024)S(1)} %copy-done.3, bf16[1024,2048]{1,0:T(8,128)(2,1)} %get-tuple-element.29, f32[2048,1000]{0,1:T(8,128)} %param.20), kind=kOutput, calls=%fused_computation.16 | convolution fusion | flops 4198398976 | bytes 16490400 | tf_op jit(solution)/shard_map/nc,kc->nk/dot_general | solution.py:487
  250.4 0.0 copy-start
  250.4 0.7 exponential_reduce_fusion
  251.2 1.2 copy-done
  252.4 4.1 %multiply_reduce_fusion.4 = (f32[]{:T(128)}, f32[1000]{0:T(1024)S(1)}) fusion(f32[1024,1000]{0,1:T(8,128)S(1)} %get-tuple-element.56, s32[1024]{0:T(1024)S(1)} %bitcast.45, f32[1024]{0:T(1024)S(1)} %log.19, f32[1024]{0:T(1024)S(1)} %get-tuple-element.55, f32[1000]{0:T(1024)S(1)} %copy-done.3), kind=kLoop, calls=%fused_computation.10 | loop fusion | flops 11262999 | bytes 4116292 | tf_op jit(solution)/shard_map/reduce_sum | solution.py:491
  257.2 0.0 copy-start.10
  257.2 13.0 %multiply_reduce_fusion.2 = (f32[]{:T(128)}, f32[1000,2048]{1,0:T(8,128)}) fusion(bf16[1024,2048]{1,0:T(8,128)(2,1)} %get-tuple-element.29, s32[1024]{0:T(1024)S(1)} %bitcast.46, f32[1024]{0:T(1024)S(1)} %log.19, f32[1024]{0:T(1024)S(1)} %get-tuple-element.55, f32[1024,1000]{0,1:T(8,128)} %copy-done, f32[1000]{0:T(1024)S(1)} %copy-done.3), kind=kOutput, calls=%fused_computation.8 | convolution fusion | flops 4207616000 | bytes 16498596 | tf_op jit(solution)/shard_map/nk,nc->kc/dot_general | solution.py:524
  270.9 0.6 fusion.28
  271.5 15.2 %fusion.29 = (f32[2048,1000]{0,1:T(8,128)}, f32[2048,1000]{0,1:T(8,128)}) fusion(f32[2048,1000]{0,1:T(8,128)} %param.20, f32[1000,2048]{1,0:T(8,128)} %get-tuple-element.58, f32[]{:T(128)S(6)} %mul.184, f32[2048,1000]{0,1:T(8,128)} %param.25), kind=kLoop, calls=%fused_computation.62 | loop fusion | flops 12288000 | bytes 40960004 | tf_op jit(solution)/shard_map/sub | solution.py:479
  286.7 0.9 slice-done.1
  287.6 11.3 %fusion.33 = (f32[1024,2048]{1,0:T(8,128)}, f32[1024,2048]{1,0:T(8,128)}) fusion(f32[1024,2048]{1,0:T(8,128)S(1)} %bitcast.35, f32[2,2,2,128,2048]{4,3,2,1,0:T(8,128)} %get-tuple-element.27, f32[]{:T(128)S(6)} %mul.166, f32[1024,2048]{1,0:T(8,128)} %param.22), kind=kLoop, calls=%fused_computation.65 | loop fusion | flops 12582912 | bytes 41943044 | tf_op jit(solution)/shard_map/sub | solution.py:479
  (27 shorter events, 0.1 us)
Async XLA Ops:
  8.1 6.9 %copy-start.11 = (s32[128]{0:T(128)S(1)}, s32[128]{0:T(128)}, u32[]{:S(2)}) copy-start(s32[128]{0:T(128)} %param.16) | copy-start | bytes 1540
  15.5 104.4 %copy-start.5 = (f32[2048]{0:T(1024)S(1)}, f32[2048]{0:T(1024)}, u32[]{:S(2)}) copy-start(f32[2048]{0:T(1024)} %param.18) | copy-start | bytes 24580
  15.6 105.3 %copy-start.3 = (f32[1000]{0:T(1024)S(1)}, f32[1000]{0:T(1024)}, u32[]{:S(2)}) copy-start(f32[1000]{0:T(1024)} %param.21) | copy-start | bytes 12004
  120.8 11.3 %copy-start.6 = (f32[1,2048]{1,0:T(1,128)}, f32[1,2048]{1,0:T(1,128)S(1)}, u32[]{:S(2)}) copy-start(f32[1,2048]{1,0:T(1,128)S(1)} %get-tuple-element.46.sc_ref) | copy-start | bytes 24580
  120.8 5.2 %copy-start.1 = (f32[128,2048]{1,0:T(8,128)S(1)}, f32[128,2048]{1,0:T(8,128)}, u32[]{:S(2)}) copy-start(f32[128,2048]{1,0:T(8,128)} %get-tuple-element.25) | copy-start | bytes 3145732
  120.9 5.2 %copy-start.2 = (f32[128,2048]{1,0:T(8,128)S(1)}, f32[128,2048]{1,0:T(8,128)}, u32[]{:S(2)}) copy-start(f32[128,2048]{1,0:T(8,128)} %get-tuple-element.26) | copy-start | bytes 3145732
  126.1 6.1 %copy-start.4 = (f32[2048]{0:T(1024)S(1)}, f32[2048]{0:T(1024)}, u32[]{:S(2)}) copy-start(f32[2048]{0:T(1024)} %param.19) | copy-start | bytes 24580
  234.0 6.9 %copy-start.7 = (f32[16,256]{1,0:T(8,128)S(1)}, f32[16,256]{1,0:T(8,128)}, u32[]{:S(2)}) copy-start(f32[16,256]{1,0:T(8,128)} %get-tuple-element.28) | copy-start | bytes 49156
  234.0 7.0 %copy-start.8 = (f32[2048]{0:T(1024)S(1)}, f32[2048]{0:T(1024)}, u32[]{:S(2)}) copy-start(f32[2048]{0:T(1024)} %param.23) | copy-start | bytes 24580
  234.0 7.6 %copy-start.9 = (f32[2048]{0:T(1024)S(1)}, f32[2048]{0:T(1024)}, u32[]{:S(2)}) copy-start(f32[2048]{0:T(1024)} %param.24) | copy-start | bytes 24580
  250.4 2.0 copy-start
  257.2 13.7 %copy-start.10 = (f32[1000]{0:T(1024)S(1)}, f32[1000]{0:T(1024)}, u32[]{:S(2)}) copy-start(f32[1000]{0:T(1024)} %param.26) | copy-start | bytes 12004
  271.5 15.2 %slice-start = ((s8[8388608]{0:T(1024)(128)(4,1)}), s8[4194304]{0:T(1024)(128)(4,1)S(1)}, s32[]{:S(2)}) async-start(s8[8388608]{0:T(1024)(128)(4,1)} %bitcast.34), calls=%async_computation | async-start | bytes 8388608
  271.5 16.1 %slice-start.1 = ((s8[8388608]{0:T(1024)(128)(4,1)}), s8[4194304]{0:T(1024)(128)(4,1)S(1)}, s32[]{:S(2)}) async-start(s8[8388608]{0:T(1024)(128)(4,1)} %bitcast.34), calls=%async_computation.1 | async-start | bytes 8388608

commit v3 on v2

--- a/solution.py
+++ b/solution.py
@@ -64,13 +64,13 @@
         fn(b)
 
 
-def fwd_kernel(a_ref, w_ref, s_ref, g_ref, b_ref, lab_ref, z_hbm, at_ref, pool_ref, cnt_ref, sx_ref, st_ref, pall_ref, lall_ref, zbuf, wbf, stat, pfull, lfull, zsem, gs, gr, ls, lr):
+def fwd_kernel(a_ref, w_ref, s_ref, g_ref, b_ref, lab_ref, z_hbm, at_ref, pool_ref, cnt_ref, sx_ref, st_ref, pall_ref, lall_ref, wsq_ref, zbuf, wbf, stat, pfull, lfull, zsem, gs, gr, ls, lr):
     j = pl.program_id(0)
     slot = lax.rem(j, 2)
     prev = 1 - slot
 
     def z_copy(jj, sl):
-        return pltpu.make_async_copy(zbuf.at[sl], z_hbm.at[:, pl.ds(pl.multiple_of(jj * CB, CB), CB)], zsem.at[sl])
+        return pltpu.make_async_copy(zbuf.at[sl], z_hbm.at[jj], zsem.at[sl])
 
     me, core, x, y = position()
 
@@ -83,6 +83,7 @@
         for k in range(1, 8):
             label_copy(k).start()
         lfull[core, y, x] = lab_ref[...]
+        wsq_ref[...] = jnp.zeros_like(wsq_ref)
 
     def second(b):
         c = gather_copies(pfull, gs, gr, b)
@@ -102,9 +103,12 @@
         for q in range(8):
             pall_ref[q * IMG:(q + 1) * IMG, :] = pfull[q // 4, (q // 2) % 2, q % 2, :, pl.ds(pl.multiple_of(b * CB, CB), CB)].astype(jnp.bfloat16)
 
-    when_block(j - 2, second)
-    when_block(j - 3, third)
-    when_block(j - 4, last)
+    def stages():
+        when_block(j - 2, second)
+        when_block(j - 3, third)
+        when_block(j - 4, last)
+
+    pl.when(j > NB)(stages)
 
     @pl.when(jnp.logical_and(j >= 2, j < NB + 2))
     def _():
@@ -112,7 +116,9 @@
 
     def step(do_mm, do_post):
         if do_mm:
-            w = w_ref[...].astype(jnp.bfloat16)
+            wf = w_ref[...]
+            wsq_ref[...] += jnp.sum((wf * wf).reshape(CIN // 8, 8, CB), axis=0)
+            w = wf.astype(jnp.bfloat16)
             wbf[...] = w
             z0 = jnp.dot(a_ref[0:IMG, :], w, preferred_element_type=jnp.float32)
             m0 = jnp.sum(z0, axis=0, keepdims=True) * (1.0 / IMG)
@@ -133,6 +139,8 @@
 
         def chunk(i, carry):
             base = pl.multiple_of(i * (CH * IMG), CH * IMG)
+            if do_post:
+                pl.when(i == 4)(stages)
             if do_mm:
                 for h in range(MS):
                     hr = pl.ds(base + h * (CH * IMG // MS), CH * IMG // MS)
@@ -227,9 +235,10 @@
             pl.BlockSpec((8, CB), prev),
             pl.BlockSpec((8 * IMG, CB), late),
             pl.BlockSpec((2, 2, 2, 8, IMG), lambda j: (0, 0, 0, 0, 0)),
+            pl.BlockSpec((8, CB), lambda j: (0, 0)),
         ],
         out_shape=[
-            jax.ShapeDtypeStruct((ROWS, COUT), f32),
+            jax.ShapeDtypeStruct((NB, ROWS, CB), f32),
             jax.ShapeDtypeStruct((CIN, ROWS), jnp.bfloat16),
             jax.ShapeDtypeStruct((IMG, COUT), f32),
             jax.ShapeDtypeStruct((IMG, COUT), f32),
@@ -237,6 +246,7 @@
             jax.ShapeDtypeStruct((8, COUT), f32),
             jax.ShapeDtypeStruct((8 * IMG, COUT), jnp.bfloat16),
             jax.ShapeDtypeStruct((2, 2, 2, 8, IMG), jnp.int32),
+            jax.ShapeDtypeStruct((8, CB), f32),
         ],
         scratch_shapes=[
             pltpu.VMEM((2, ROWS, CB), f32),
@@ -260,7 +270,7 @@
 QR = CIN // 8
 
 
-def bwd_kernel(at_ref, z_ref, s_ref, sc_ref, sh_ref, bb_ref, cc_ref, da_ref, db_ref, g_hbm, dbo_ref,
+def bwd_kernel(at_ref, z_ref, s_ref, sc_ref, sh_ref, bb_ref, cc_ref, da_ref, db_ref, g_hbm, dbo_ref, gsq_ref,
                dz, dw, rd, ha, hb, ra, rb, ka, kb, r2a, r2b, gfull, dball, ss, rs, gs, gr, bs, br, osem):
     j = pl.program_id(0)
     slot = lax.rem(j, 2)
@@ -279,6 +289,7 @@
         for k in range(1, 8):
             db_copy(k).start()
         dball[me] = db_ref[...]
+        gsq_ref[...] = jnp.zeros_like(gsq_ref)
 
     def out_copy(b):
         cc = pl.ds(pl.multiple_of(b * CB, CB), CB)
@@ -346,13 +357,22 @@
     def stage6(b):
         gather_copies(gfull, gs, gr, b)[4].wait_recv()
         out_copy(b).start()
-
-    when_block(j - 2, stage1)
-    when_block(j - 3, stage2)
-    when_block(j - 4, stage3)
-    when_block(j - 5, stage4)
-    when_block(j - 6, stage5)
-    when_block(j - 7, stage6)
+        cc = pl.ds(pl.multiple_of(b * CB, CB), CB)
+        acc = gsq_ref[...]
+        for q in range(8):
+            gv = gfull[q // 4, (q // 2) % 2, q % 2, :, cc]
+            acc = acc + jnp.sum((gv * gv).reshape(QR // 8, 8, CB), axis=0)
+        gsq_ref[...] = acc
+
+    def stages():
+        when_block(j - 2, stage1)
+        when_block(j - 3, stage2)
+        when_block(j - 4, stage3)
+        when_block(j - 5, stage4)
+        when_block(j - 6, stage5)
+        when_block(j - 7, stage6)
+
+    pl.when(j > NB)(stages)
 
     def step(do_pre, do_mm):
         if do_pre:
@@ -380,6 +400,8 @@
 
         def chunk(i, carry):
             base = pl.multiple_of(i * 1792, 1792)
+            if do_mm:
+                pl.when(i == 1)(stages)
             if do_mm:
                 dw[prev] += mm(base, 1792)
             if do_pre:
@@ -427,14 +449,14 @@
         grid=(NB + BTAIL,),
         in_specs=[
             pl.BlockSpec((CIN, ROWS), lambda j: (0, 0), pipeline_mode=pl.Buffered(1)),
-            pl.BlockSpec((ROWS, CB), cur),
+            pl.BlockSpec((None, ROWS, CB), lambda j: (jnp.minimum(j, NB - 1), 0, 0)),
             pl.BlockSpec((ROWS, CB), cur),
             row, row, row, row,
             pl.BlockSpec((IMG, CB), cur),
-            pl.BlockSpec((16, CB), lambda j: (0, 0)),
+            pl.BlockSpec((2, COUT), lambda j: (0, 0)),
         ],
-        out_specs=[pl.BlockSpec(memory_space=pl.ANY), pl.BlockSpec((16, CB), lambda j: (0, 0))],
-        out_shape=[jax.ShapeDtypeStruct((2, 2, 2, QR, COUT), f32), jax.ShapeDtypeStruct((16, CB), f32)],
+        out_specs=[pl.BlockSpec(memory_space=pl.ANY), pl.BlockSpec((2, COUT), lambda j: (0, 0)), pl.BlockSpec((8, CB), lambda j: (0, 0))],
+        out_shape=[jax.ShapeDtypeStruct((2, 2, 2, QR, COUT), f32), jax.ShapeDtypeStruct((2, COUT), f32), jax.ShapeDtypeStruct((8, CB), f32)],
         scratch_shapes=[
             pltpu.VMEM((2, ROWS, CB), jnp.bfloat16),
             pltpu.VMEM((2, CIN, CB), f32),
@@ -448,7 +470,7 @@
             pltpu.VMEM((NB, QR, CB // 2), f32),
             pltpu.VMEM((NB, QR, CB // 2), f32),
             pltpu.VMEM((2, 2, 2, QR, COUT), f32),
-            pltpu.VMEM((8, 16, CB), f32),
+            pltpu.VMEM((8, 2, COUT), f32),
             pltpu.SemaphoreType.DMA((5, NB)),
             pltpu.SemaphoreType.DMA((5, NB)),
             pltpu.SemaphoreType.DMA((5, NB)),
@@ -461,22 +483,179 @@
         cost_estimate=pl.CostEstimate(flops=2 * ROWS * CIN * COUT, bytes_accessed=120_000_000, transcendentals=0),
         name="bwd_conv",
     )(at, z, s, sc, sh, bb, cc, da, dgb)
-import jax
-import jax.numpy as jnp
-from jax.sharding import PartitionSpec as P
+
 
 SMOOTHING = 0.1
 MOMENTUM = 0.9
 TRUST_COEF = 0.001
 WEIGHT_DECAY = 5e-5
-
-
-def lars_update(weight, gradient, velocity, learn_rate):
-    w_norm = jnp.sqrt(jnp.sum(jnp.square(weight)))
-    g_norm = jnp.sqrt(jnp.sum(jnp.square(gradient)))
-    trust = TRUST_COEF * w_norm / (g_norm + WEIGHT_DECAY * w_norm)
-    new_vel = MOMENTUM * velocity + learn_rate * trust * (gradient + WEIGHT_DECAY * weight)
-    return weight - new_vel, new_vel
+CLASSES = 1000
+KP = 1024
+UB = 128
+FB = 200
+NU = CIN // UB
+NF = CLASSES // FB
+TOTAL = 8 * IMG
+
+
+def trust_of(wsq, gsq):
+    total = lambda v: jnp.sum(jnp.sum(v, axis=0, keepdims=True), axis=1, keepdims=True)
+    wn = jnp.sqrt(total(wsq))
+    gn = jnp.sqrt(total(gsq))
+    return TRUST_COEF * wn / (gn + WEIGHT_DECAY * wn)
+
+
+def update_kernel(lr_ref, w_ref, v_ref, g_ref, wsq_ref, gsq_ref, wt_hbm, vt_ref, pall_hbm, lab_ref, bias_ref, vbias_ref,
+                  gam_ref, bet_ref, vgam_ref, vbet_ref, dgb_ref,
+                  wo_ref, vo_ref, wto_ref, vto_ref, bo_ref, vbo_ref, go_ref, vgo_ref, beo_ref, vbeo_ref, loss_ref,
+                  wt, wtb, pall, dlt, gfc, fsq, gb, ls, sem):
+    j = pl.program_id(0)
+    f32 = jnp.float32
+    lr = lr_ref[0]
+
+    def wt_copy():
+        return pltpu.make_async_copy(wt_hbm, wt, sem.at[0])
+
+    def pall_copy():
+        return pltpu.make_async_copy(pall_hbm, pall, sem.at[1])
+
+    @pl.when(j == 0)
+    def _():
+        wt_copy().start()
+        pall_copy().start()
+        gb[...] = jnp.zeros_like(gb)
+        ls[...] = jnp.zeros_like(ls)
+        fsq[...] = jnp.zeros_like(fsq)
+        for (p, v, po, vo, g) in ((gam_ref, vgam_ref, go_ref, vgo_ref, dgb_ref[0:1, :]), (bet_ref, vbet_ref, beo_ref, vbeo_ref, dgb_ref[1:2, :])):
+            nv = MOMENTUM * v[...] + lr * g
+            vo[...] = nv
+            po[...] = p[...] - nv
+
+    @pl.when(j < NU)
+    def _():
+        rate = jnp.broadcast_to(lr * trust_of(wsq_ref[...], gsq_ref[...]), (8, CB))
+
+        def row(i, carry):
+            r = pl.ds(pl.multiple_of(i * 8, 8), 8)
+            for c in range(0, COUT, CB):
+                cc = slice(c, c + CB)
+                w = w_ref[r, cc]
+                nv = MOMENTUM * v_ref[r, cc] + rate * (g_ref[r, cc] + WEIGHT_DECAY * w)
+                vo_ref[r, cc] = nv
+                wo_ref[r, cc] = w - nv
+            return carry
+        lax.fori_loop(0, UB // 8, row, 0)
+
+    @pl.when(j == 1)
+    def _():
+        wt_copy().wait()
+        pall_copy().wait()
+
+        def row(i, acc):
+            r = pl.ds(pl.multiple_of(i * 40, 40), 40)
+            w = wt[r, :]
+            wtb[r, :] = w.astype(jnp.bfloat16)
+            return acc + jnp.sum((w * w).reshape(5, 8, COUT), axis=0)
+        fsq[0] = lax.fori_loop(0, CLASSES // 40, row, jnp.zeros((8, COUT), f32))
+        wtb[CLASSES:KP, :] = jnp.zeros((KP - CLASSES, COUT), jnp.bfloat16)
+
+    def logits_block(i):
+        rows = pl.ds(pl.multiple_of(i * IMG, IMG), IMG)
+        lg = lax.dot_general(pall[rows, :], wtb[...], (((1,), (1,)), ((), ())), preferred_element_type=f32)
+        cls = lax.broadcasted_iota(jnp.int32, (IMG, KP), 1)
+        valid = cls < CLASSES
+        lg = jnp.where(valid, lg + bias_ref[...], -1e30)
+        mx = jnp.max(lg, axis=1, keepdims=True)
+        sh = lg - mx
+        ex = jnp.exp(sh)
+        lse = jnp.log(jnp.sum(ex, axis=1, keepdims=True))
+        lp = sh - lse
+        tg = jnp.where(valid, SMOOTHING / CLASSES + jnp.where(lab_ref[rows, :] == cls, 1.0 - SMOOTHING, 0.0), 0.0)
+        ls[...] += jnp.sum((tg * lp).reshape(IMG // 8, 8, KP), axis=0)
+        dl = (jnp.exp(lp) - tg) * (1.0 / TOTAL)
+        gb[...] += jnp.sum(dl.reshape(IMG // 8, 8, KP), axis=0)
+        dlt[:, rows] = dl.T.astype(jnp.bfloat16)
+
+    @pl.when(jnp.logical_and(j >= 2, j < 6))
+    def _():
+        logits_block((j - 2) * 2)
+        logits_block((j - 2) * 2 + 1)
+
+    @pl.when(jnp.logical_and(j >= 6, j < 8))
+    def _():
+        rows = pl.ds(pl.multiple_of((j - 6) * 512, 512), 512)
+
+        def col(i, carry):
+            cc = pl.ds(pl.multiple_of(i * 256, 256), 256)
+            g = jnp.dot(dlt[rows, :], pall[:, cc], preferred_element_type=f32)
+            gfc[rows, cc] = g
+            fsq[1, :, cc] += jnp.sum((g * g).reshape(64, 8, 256), axis=0)
+            return carry
+        lax.fori_loop(0, COUT // 256, col, 0)
+
+    @pl.when(j >= NU)
+    def _():
+        rate = jnp.broadcast_to(lr * trust_of(fsq[0], fsq[1]), (8, CB))
+        base = pl.multiple_of((j - NU) * FB, 8)
+
+        def row(i, carry):
+            o = pl.multiple_of(i * 8, 8)
+            r = pl.ds(o, 8)
+            a = pl.ds(pl.multiple_of(base + o, 8), 8)
+            for c in range(0, COUT, CB):
+                cc = slice(c, c + CB)
+                w = wt[a, cc]
+                nv = MOMENTUM * vt_ref[r, cc] + rate * (gfc[a, cc] + WEIGHT_DECAY * w)
+                vto_ref[r, cc] = nv
+                wto_ref[r, cc] = w - nv
+            return carry
+        lax.fori_loop(0, FB // 8, row, 0)
+
+    @pl.when(j == NU)
+    def _():
+        g = jnp.sum(gb[...], axis=0, keepdims=True)
+        nv = MOMENTUM * vbias_ref[...] + lr * g
+        vbo_ref[...] = nv
+        bo_ref[...] = bias_ref[...] - nv
+        tot = jnp.sum(jnp.sum(ls[...], axis=0, keepdims=True), axis=1, keepdims=True)
+        loss_ref[...] = jnp.broadcast_to(tot * (-1.0 / TOTAL), (8, 128))
+
+
+def update_all(lr, w, v, g, wsq, gsq, wt, vt, pall, lab, bias, vbias, gamma, beta, vgamma, vbeta, dgb):
+    f32 = jnp.float32
+    S = jax.ShapeDtypeStruct
+    conv = pl.BlockSpec((UB, COUT), lambda j: (jnp.minimum(j, NU - 1), 0))
+    fc = pl.BlockSpec((FB, COUT), lambda j: (jnp.clip(j - NU, 0, NF - 1), 0))
+    full = lambda *sh: pl.BlockSpec(sh, lambda j: (0,) * len(sh))
+    hbm = pl.BlockSpec(memory_space=pl.ANY)
+    vec = full(1, COUT)
+    bvec = full(1, KP)
+    return pl.pallas_call(
+        update_kernel,
+        grid=(NU + NF,),
+        in_specs=[pl.BlockSpec(memory_space=pltpu.SMEM), conv, conv, conv, full(8, CB), full(8, CB), hbm, fc, hbm, full(TOTAL, 1), bvec, bvec,
+                  vec, vec, vec, vec, full(2, COUT)],
+        out_specs=[conv, conv, fc, fc, bvec, bvec, vec, vec, vec, vec, full(8, 128)],
+        out_shape=[S((CIN, COUT), f32), S((CIN, COUT), f32), S((CLASSES, COUT), f32), S((CLASSES, COUT), f32), S((1, KP), f32), S((1, KP), f32),
+                   S((1, COUT), f32), S((1, COUT), f32), S((1, COUT), f32), S((1, COUT), f32), S((8, 128), f32)],
+        scratch_shapes=[
+            pltpu.VMEM((CLASSES, COUT), f32),
+            pltpu.VMEM((KP, COUT), jnp.bfloat16),
+            pltpu.VMEM((TOTAL, COUT), jnp.bfloat16),
+            pltpu.VMEM((KP, TOTAL), jnp.bfloat16),
+            pltpu.VMEM((KP, COUT), f32),
+            pltpu.VMEM((2, 8, COUT), f32),
+            pltpu.VMEM((8, KP), f32),
+            pltpu.VMEM((8, KP), f32),
+            pltpu.SemaphoreType.DMA((2,)),
+        ],
+        compiler_params=pltpu.CompilerParams(vmem_limit_bytes=63 * 1024 * 1024),
+        cost_estimate=pl.CostEstimate(flops=9_000_000_000, bytes_accessed=80_000_000, transcendentals=0),
+        name="update",
+    )(lr, w, v, g, wsq, gsq, wt, vt, pall, lab, bias, vbias, gamma, beta, vgamma, vbeta, dgb)
+
+
+from jax.sharding import PartitionSpec as P
 
 
 def head(pb, labels, w_fc_t, fc_bias, total):
@@ -503,7 +682,7 @@
         s = shortcut.transpose(1, 2, 0, 3).reshape(ROWS, COUT)
         w_fc_t = w_fc.T
         lab8 = jnp.broadcast_to(labels[None], (8, IMG))
-        z, at, pooled, cnt, sx, st, pall, lall = forward(a, w_conv, s, gamma[None], beta[None], lab8)
+        z, at, pooled, cnt, sx, st, pall, lall, wsq = forward(a, w_conv, s, gamma[None], beta[None], lab8)
         _, wb, _, dlb, _ = head(pooled.astype(jnp.bfloat16), labels, w_fc_t, fc_bias, total)
         dpool = jnp.einsum('nk,kc->nc', dlb, wb, preferred_element_type=f32) / POS
         mean = st[0:1]
@@ -515,19 +694,12 @@
         sh = beta[None] - mean * sc
         cc = -(sc * inv) * (d_gamma / ROWS)
         bb = -sc * (d_beta / ROWS) - mean * cc
-        dgb = jnp.concatenate([d_gamma.reshape(8, CB), d_beta.reshape(8, CB)])
-        g8, dgb = backward(at, z, s, sc, sh, bb, cc, dpool * sc, dgb)
-        g_conv = g8.reshape(CIN, COUT)
-        g_gamma = dgb[0:8].reshape(COUT)
-        g_beta = dgb[8:16].reshape(COUT)
-        _, _, dl, dlb, loss = head(pall, lall[:, :, :, 0].reshape(total), w_fc_t, fc_bias, total)
-        g_fc_t = jnp.einsum('nk,nc->kc', dlb, pall, preferred_element_type=f32)
-        g_bias = jnp.sum(dl, axis=0)
-        conv_new, conv_vel_new = lars_update(w_conv, g_conv, vel_conv, lr)
-        fc_new, fc_vel_new = lars_update(w_fc_t, g_fc_t, vel_fc.T, lr)
-        gv = MOMENTUM * vel_gamma + lr * g_gamma
-        bv = MOMENTUM * vel_beta + lr * g_beta
-        cv = MOMENTUM * vel_bias + lr * g_bias
-        return (conv_new, gamma - gv, beta - bv, fc_new.T, fc_bias - cv, conv_vel_new, gv, bv, fc_vel_new.T, cv, loss)
+        dgb = jnp.concatenate([d_gamma, d_beta])
+        g8, dgb, gsq = backward(at, z, s, sc, sh, bb, cc, dpool * sc, dgb)
+        pad = lambda b: jnp.pad(b, (0, KP - CLASSES))[None]
+        wo, vo, wto, vto, bo, vbo, go, vgo, beo, vbeo, loss = update_all(
+            lr.reshape(1), w_conv, vel_conv, g8.reshape(CIN, COUT), wsq, gsq, w_fc_t, vel_fc.T, pall, lall[:, :, :, 0].reshape(total, 1),
+            pad(fc_bias), pad(vel_bias), gamma[None], beta[None], vel_gamma[None], vel_beta[None], dgb)
+        return (wo, go[0], beo[0], wto.T, bo[0, :CLASSES], vo, vgo[0], vbeo[0], vto.T, vbo[0, :CLASSES], loss[0, 0])
 
     return jax.shard_map(local_step, mesh=mesh, in_specs=(P('dp'),) * 3 + (P(),) * 11, out_specs=(P(),) * 11, check_vma=False)

time: 301 us -> 249 us (0.83)
  other arithmetic: 54.8 us -> 3.19 us
  Pallas kernels: 204 us -> 227 us
  matrix products: 31.7 us -> 10.3 us
  between operations: 6.16 us -> 1.39 us
  local copies, waits for them, and re-layouts: 3.54 us -> 6.97 us
    pallas_call x0 -> x1, Pallas kernels: none -> 43.7 us  [update_all(): pl.pallas_call(update_kernel, grid=(NU + NF,), in_specs=[pl.BlockSpec(mem...]
    sub x5 -> x0, other arithmetic: 28.3 us -> none  [the longest x2 26.5 us: lars_update(): return (weight - new_vel, new_vel)]
    reduce_sum x4 -> x0, other arithmetic: 22.5 us -> none  [the longest x2 12.3 us: lars_update(): w_norm = jnp.sqrt(jnp.sum(jnp.square(weight)))]
    pallas_call x1, Pallas kernels: 104 us -> 84.7 us  [forward(): pl.pallas_call(fwd_kernel, grid=(NB + 1 + TAIL,), in_specs=[pl.BlockSpec(...]
    dot_general x1 -> x0, matrix products: 13 us -> none  [local_step(): g_fc_t = jnp.einsum('nk,nc->kc', dlb, pall, preferred_element_type=f32)]
    dot_general x2 -> x1, matrix products: 13.2 us -> 4.91 us  [head(): jnp.einsum('nc,kc->nk', pb, wb, preferred_element_type=f32) + fc_bias]
where the time goes in v3:
time: 249 us; the launch traced here: 248 us
  Pallas kernels  227 us (91%)
  matrix products  10.3 us (4%)
  local copies, waits for them, and re-layouts  6.97 us (3%)
  other arithmetic  3.19 us (1%)
    pallas_call x1, Pallas kernels, backward(): pl.pallas_call(bwd_kernel, grid=(NB + BTAIL,), in_specs=[pl.BlockSpec((CI...  98.2 us
    pallas_call x1, Pallas kernels, forward(): pl.pallas_call(fwd_kernel, grid=(NB + 1 + TAIL,), in_specs=[pl.BlockSpec(...  84.7 us
    pallas_call x1, Pallas kernels, update_all(): pl.pallas_call(update_kernel, grid=(NU + NF,), in_specs=[pl.BlockSpec(mem...  43.7 us
    dot_general x1, matrix products, local_step(): dpool = jnp.einsum('nk,kc->nc', dlb, wb, preferred_element_type=f32) / POS  5.36 us

profile of v3, /device:TPU:1, one launch (start us, length us, event | category | flops | bytes accessed | tf_op | source)
XLA Modules:
  0.0 248.4 jit_solution(5030592925420447191)
XLA Ops:
  1.3 1.3 pad.8
  2.6 1.2 broadcast_in_dim.20.lab_ref
  3.8 1.3 pad.7
  5.1 0.0 copy-start.3
  5.1 0.0 copy-start.5
  5.1 84.7 %fwd_conv.1 = (f32[8,6272,256]{2,1,0:T(8,128)}, bf16[1024,6272]{1,0:T(8,128)(2,1)}, f32[128,2048]{1,0:T(8,128)}, f32[128,2048]{1,0:T(8,128)}, f32[128,2048]{1,0:...) custom-call(bf16[6272,1024]{1,0:T(8,128)(2,1)} %bitcast.79, ...), custom_call_target="tpu_custom_call" | custom-call | flops 26306674688 | bytes 120000000 | tf_op jit(solution)/shard_map/fwd_conv/pallas_call | solution.py:218
  89.8 0.0 copy-start
  89.8 0.0 copy-start.1
  89.8 0.0 copy-start.6
  89.8 0.9 slice.20
  90.7 0.0 copy-done.3
  90.7 0.9 broadcast_multiply_fusion.1
  91.6 0.0 copy-start.4
  91.6 0.0 copy-done.5
  91.6 4.9 %fusion.23 = (f32[128]{0:T(128)S(1)}, f32[128,1000]{0,1:T(8,128)S(1)}) fusion(f32[1000]{0:T(1024)S(1)} %copy-done.5, f32[128,2048]{1,0:T(8,128)} %get-tuple-element.37, f32[2048,1000]{0,1:T(8,128)} %param.20), kind=kOutput, calls=%fused_computation.31 | convolution fusion | flops 524806016 | bytes 9757088 | tf_op jit(solution)/shard_map/nc,kc->nk/dot_general | solution.py:666
  96.5 0.0 copy-start.2
  96.5 0.2 exponential_reduce_fusion
  96.7 0.0 copy-done
  96.7 0.0 copy-done.1
  96.7 0.0 copy-done.6
  96.7 5.4 %multiply_reduce_fusion.1 = (f32[2048]{0:T(1024)S(1)}, f32[2048]{0:T(1024)S(1)}, f32[128,2048]{1,0:T(8,128)}) fusion(f32[128,2048]{1,0:T(8,128)S(1)} %copy-done, f32[128,2048]{1,0:T(8,128)S(1)} %copy-done.1, f32[2048]{0:T(1024)S(1)} %bitcast.71, f32[128,1000]{0,1:T(8,128)S(1)} %get-tuple-element.66, s32[128]{0:T(128)S(1)} %copy-done.6, f32[128]{0:T(128)S(1)} %log.9, ...), kind=kOutput, calls=%fused_computation.6 | convolution fusion | flops 526880768 | bytes 11875840 | tf_op jit(solution)/shard_map/nk,kc->nc/dot_general | solution.py:687
  102.1 0.0 copy-done.4
  102.1 0.0 copy-done.2
  102.1 1.6 multiply_subtract_fusion
  103.6 0.6 pad_maximum_fusion.db_ref
  104.2 98.2 %bwd_conv.1 = (f32[2,2,2,128,2048]{4,3,2,1,0:T(8,128)}, f32[2,2048]{1,0:T(2,128)}, f32[8,256]{1,0:T(8,128)}) custom-call(bf16[1024,6272]{1,0:T(8,128)(2,1)} %get-tuple-element.34.at_ref, f32[8,6272,256]{2,1,0:T(8,128)} %get-tuple-element.35.z_ref, bf16[6272,2048]{1,0:T(8,128)(2,1)} %bitcast.78, f32[1,2048]{1,0:T(1,128)} %copy-done.4, ...), custom_call_target="tpu_custom_call" | custom-call | flops 26306674688 | bytes 120000000 | tf_op jit(solution)/shard_map/bwd_conv/pallas_call | solution.py:447
  202.5 1.0 copy.25.lab_ref
  203.5 43.7 %update.1 = (f32[1024,2048]{1,0:T(8,128)}, f32[1024,2048]{1,0:T(8,128)}, f32[1000,2048]{1,0:T(8,128)}, f32[1000,2048]{1,0:T(8,128)}, f32[1,1024]{1,0:T(1,128)}, ...) custom-call(f32[1]{0:T(128)} %bitcast.57.lr_ref, ...), custom_call_target="tpu_custom_call" | custom-call | flops 8999999488 | bytes 80000000 | tf_op jit(solution)/shard_map/update/pallas_call | solution.py:633
  247.2 1.2 slice.23
  (1 shorter events, 0.0 us)
Async XLA Ops:
  5.1 85.6 %copy-start.3 = (f32[2048]{0:T(1024)S(1)}, f32[2048]{0:T(1024)}, u32[]{:S(2)}) copy-start(f32[2048]{0:T(1024)} %param.18) | copy-start | bytes 24580
  5.1 86.5 %copy-start.5 = (f32[1000]{0:T(1024)S(1)}, f32[1000]{0:T(1024)}, u32[]{:S(2)}) copy-start(f32[1000]{0:T(1024)} %param.21) | copy-start | bytes 12004
  89.8 6.9 %copy-start = (f32[128,2048]{1,0:T(8,128)S(1)}, f32[128,2048]{1,0:T(8,128)}, u32[]{:S(2)}) copy-start(f32[128,2048]{1,0:T(8,128)} %get-tuple-element.38) | copy-start | bytes 3145732
  89.8 6.9 %copy-start.1 = (f32[128,2048]{1,0:T(8,128)S(1)}, f32[128,2048]{1,0:T(8,128)}, u32[]{:S(2)}) copy-start(f32[128,2048]{1,0:T(8,128)} %get-tuple-element.39) | copy-start | bytes 3145732
  89.8 6.9 %copy-start.6 = (s32[128]{0:T(128)S(1)}, s32[128]{0:T(128)}, u32[]{:S(2)}) copy-start(s32[128]{0:T(128)} %param.16) | copy-start | bytes 1540
  91.6 10.5 %copy-start.4 = (f32[1,2048]{1,0:T(1,128)}, f32[1,2048]{1,0:T(1,128)S(1)}, u32[]{:S(2)}) copy-start(f32[1,2048]{1,0:T(1,128)S(1)} %get-tuple-element.60.sc_ref) | copy-start | bytes 24580
  96.5 5.6 %copy-start.2 = (f32[2048]{0:T(1024)S(1)}, f32[2048]{0:T(1024)}, u32[]{:S(2)}) copy-start(f32[2048]{0:T(1024)} %param.19) | copy-start | bytes 24580

commit v4 on v0

v4 whole, which is shorter than its diff:
```python
import functools
import jax
import jax.numpy as jnp
from jax import lax
from jax.experimental import pallas as pl
from jax.experimental.pallas import tpu as pltpu
from jax.sharding import PartitionSpec as P

BN_EPS = 1e-5
SMOOTHING = 0.1
MOMENTUM = 0.9
TRUST_COEF = 0.001
WEIGHT_DECAY = 5e-5

LANES = 128
SUB = 8
IMG = 128
POS = 49
ROWS = IMG * POS
CIN = 1024
COUT = 2048
CLASSES = 1000
KP = 1024
DEVS = 8
TOTAL = DEVS * IMG
CB = 256
HC = CB // 2
NB = COUT // CB
CH = 7
NCH = POS // CH
NT = 16
APAD = CIN + LANES
TAIL = 3
BTAIL = 7
QR = CIN // DEVS
HALF = CIN // 2
BIG = 1792
BTILE = BIG // IMG
NBIG = ROWS // BIG
UB = 128
FB = 208
NU = CIN // UB
NF = pl.cdiv(CLASSES, FB)
LB = 256
MIB = 1024 * 1024
F32 = jnp.float32
BF16 = jnp.bfloat16
MESH = pl.DeviceIdType.MESH
XN, YN, PN = 'x', 'y', 'core'


def dot(a, b):
    return jnp.dot(a, b, preferred_element_type=F32)


def dot_t(a, b):
    return lax.dot_general(a, b, (((1,), (1,)), ((), ())), preferred_element_type=F32)


def fold(v, axis=0):
    return jnp.sum(v.reshape(v.shape[0] // SUB, SUB, v.shape[1]), axis=axis)


def rowsum(v, axis=0):
    return jnp.sum(v, axis=axis, keepdims=True)


def lanesum(v, axis=1):
    return jnp.sum(v, axis=axis, keepdims=True)


def cols(b, size=CB, at=0):
    return pl.ds(pl.multiple_of(b * CB + at, LANES), size)


def span(i, size):
    return pl.ds(pl.multiple_of(i * size, SUB), size)


def position():
    me = lax.axis_index('dp')
    return me, lax.rem(me, 2), lax.rem(me // 2, 2), me // 4


def dev(core, x, y):
    return (y * 2 + x) * 2 + core


def neighbour(name):
    me, core, x, y = position()
    flip = lambda v, k: 1 - v if k == name else v
    return dev(flip(core, PN), flip(x, XN), flip(y, YN))


def enter_all():
    me = lax.axis_index('dp')
    bar = pltpu.get_barrier_semaphore()
    for k in range(1, DEVS):
        pl.semaphore_signal(bar, inc=1, device_id=(lax.rem(me + k, DEVS),), device_id_type=MESH)
    pl.semaphore_wait(bar, DEVS - 1)


def rcopy(src, dst, send, recv, target):
    return pltpu.make_async_remote_copy(src_ref=src, dst_ref=dst, send_sem=send, recv_sem=recv, device_id=(target,), device_id_type=MESH)


def each(fn, copies):
    for c in copies:
        fn(c)


def start(c):
    c.start()


def wait(c):
    c.wait()


def wait_send(c):
    c.wait_send()


def wait_recv(c):
    c.wait_recv()


def gather_own(buf, send, recv, b, ka=0, kb=1):
    me, core, x, y = position()
    a, c = buf.at[core, y, x, :, cols(b, HC)], buf.at[core, y, x, :, cols(b, HC, HC)]
    return rcopy(a, a, send.at[ka, b], recv.at[ka, b], neighbour(YN)), rcopy(c, c, send.at[kb, b], recv.at[kb, b], neighbour(XN))


def gather_on(buf, send, recv, b, ka=2, kb=3):
    me, core, x, y = position()
    a, c = buf.at[core, :, x, :, cols(b, HC)], buf.at[core, y, :, :, cols(b, HC, HC)]
    return rcopy(a, a, send.at[ka, b], recv.at[ka, b], neighbour(XN)), rcopy(c, c, send.at[kb, b], recv.at[kb, b], neighbour(YN))


def gather_core(buf, send, recv, b, k=4):
    me, core, x, y = position()
    a = buf.at[core, :, :, :, cols(b)]
    return (rcopy(a, a, send.at[k, b], recv.at[k, b], neighbour(PN)),)


def gather_all(*a):
    return gather_own(*a) + gather_on(*a) + gather_core(*a)


def when_block(b, fn):
    @pl.when(jnp.logical_and(b >= 0, b < NB))
    def _():
        fn(b)


def stage_list(j, fns, lag=2):
    for k, fn in enumerate(fns):
        when_block(j - lag - k, fn)


def pieces():
    return [(c, y, x) for c in range(2) for y in range(2) for x in range(2)]


def softmax_terms(logits, bias, labels):
    n = logits.shape[0]
    cls = lax.broadcasted_iota(jnp.int32, (n, KP), 1)
    valid = cls < CLASSES
    lg = jnp.where(valid, logits + bias, -1e30)
    sh = lg - jnp.max(lg, axis=1, keepdims=True)
    lp = sh - jnp.log(lanesum(jnp.exp(sh)))
    lab = jnp.concatenate([labels] * (KP // LANES), axis=1)
    hit = lab == cls.astype(F32)
    tg = jnp.where(valid, SMOOTHING / CLASSES + jnp.where(hit, 1.0 - SMOOTHING, 0.0), 0.0)
    return tg * lp, (jnp.exp(lp) - tg) * (1.0 / TOTAL)


def label_rows(row):
    return jnp.broadcast_to(row.astype(F32), (IMG, IMG)).T


def set_bias(bpad, bias_ref):
    bpad[:] = jnp.zeros_like(bpad)
    bpad[:, :CLASSES] = bias_ref[:]


def fwd_kernel(a_hbm, w_ref, s_ref, g_ref, b_ref, lab_ref, bias_ref, wt_hbm,
               z_hbm, at_ref, pall_ref, lall_ref, wsq_ref, fsq_ref, wtb_hbm, da_ref, sc_ref, sh_ref, bb_ref, cc_ref, db_ref,
               abf, zbuf, wbf, stat, pfull, lfull, pool, cnt, sx, sv, wtb, bpad, asem, zsem, wsem, osem, gs, gr, ls, lr):
    j = pl.program_id(0)
    slot = lax.rem(j, 2)
    prev = 1 - slot
    me, core, x, y = position()
    crow = CH * IMG

    def a_copy(i):
        r = span(i, crow)
        return pltpu.make_async_copy(a_hbm.at[r, :], abf.at[r, :CIN], asem.at[i])

    def z_copy(jj):
        sl = lax.rem(jj, 2)
        return pltpu.make_async_copy(zbuf.at[sl], z_hbm.at[jj], zsem.at[sl])

    def wt_view(b):
        return zbuf.at[b // 6, pl.ds((b % 6) * CLASSES, CLASSES), :]

    def wt_copy(b):
        return pltpu.make_async_copy(wt_hbm.at[:, pl.ds(b * CB, CB)], wt_view(b), wsem.at[b])

    def wtb_copy():
        return pltpu.make_async_copy(wtb, wtb_hbm, osem)

    def label_copy(k):
        return rcopy(lab_ref, lfull.at[core, y, x], ls.at[k], lr.at[k], lax.rem(me + k, DEVS))

    labels = [label_copy(k) for k in range(1, DEVS)]

    @pl.when(j == 0)
    def _():
        for i in range(NCH):
            a_copy(i).start()
        enter_all()
        each(start, labels)
        lfull[core, y, x] = lab_ref[:]
        wsq_ref[:] = jnp.zeros_like(wsq_ref)
        set_bias(bpad, bias_ref)

    def second(b):
        each(wait_recv, gather_own(pfull, gs, gr, b))
        each(start, gather_on(pfull, gs, gr, b))

    def third(b):
        each(wait_recv, gather_on(pfull, gs, gr, b))
        each(start, gather_core(pfull, gs, gr, b))

    def last(b):
        each(wait_recv, gather_core(pfull, gs, gr, b))
        for q, (c, py, px) in enumerate(pieces()):
            pall_ref[span(q, IMG), :] = pfull[c, py, px, :, cols(b)].astype(BF16)

    def stages():
        stage_list(j, (second, third, last))

    @pl.when(jnp.logical_and(j >= 2, j < NB + 2))
    def _():
        z_copy(j - 2).wait()

    def step(first, do_mm, do_post):
        if do_mm:
            wf = w_ref[:]
            wsq_ref[:] += fold(wf * wf)
            w = wf.astype(BF16)
            wbf[:] = w
            if first:
                a_copy(0).wait()
            m0 = rowsum(dot(abf[:IMG, :CIN], w)) * (1.0 / IMG)
            stat[:2 * SUB] = jnp.zeros((2 * SUB, CB), F32)
        if do_post:
            mean = stat[2 * SUB:2 * SUB + 1]
            inv = stat[3 * SUB:3 * SUB + 1]
            sc = g_ref[:] * inv
            sh = b_ref[:] - mean * sc
            pool[:] = jnp.zeros_like(pool)
            pc = cols(j - 1)
            cnt[:, pc] = jnp.zeros((IMG, CB), F32)
            sx[:, pc] = jnp.zeros((IMG, CB), F32)

        def chunk(i, carry):
            base = pl.multiple_of(i * crow, crow)
            if do_post:
                pl.when(i == 4)(stages)
            if do_mm:
                if first:
                    pl.when(i > 0)(lambda: a_copy(i).wait())
                r = pl.ds(base, crow)
                zc = dot(abf[r, :CIN], wbf[:])
                zbuf[slot, r, :] = zc
                d = zc - m0
                stat[:SUB] += fold(d)
                stat[SUB:2 * SUB] += fold(d * d)
                at_ref[:, r] = abf[r, pl.ds(pl.multiple_of(j * IMG, IMG), IMG)].astype(F32).T.astype(BF16)
            if do_post:
                for n in range(0, IMG, NT):
                    nr = slice(n, n + NT)
                    pa, ca, xa = pool[nr], cnt[nr, pc], sx[nr, pc]
                    for p in range(CH):
                        r = pl.ds(base + p * IMG + n, NT)
                        zz = zbuf[prev, r, :]
                        u = zz * sc + sh + s_ref[r, :].astype(F32)
                        mk = u > 0
                        pa = pa + jnp.maximum(u, 0.0)
                        ca = ca + jnp.where(mk, 1.0, 0.0)
                        xa = xa + jnp.where(mk, zz, 0.0)
                    pool[nr], cnt[nr, pc], sx[nr, pc] = pa, ca, xa
            return carry

        lax.fori_loop(0, NCH, chunk, 0)
        if do_post:
            pfull[core, y, x, :, pc] = pool[:] * (1.0 / POS)
            sx[:, pc] = (sx[:, pc] - mean * cnt[:, pc]) * inv
            sv[:1, pc] = mean
            sv[SUB:SUB + 1, pc] = inv
            sc_ref[:, pc] = sc
            sh_ref[:, pc] = sh
            each(start, gather_own(pfull, gs, gr, j - 1))
        if do_mm:
            dm = rowsum(stat[:SUB]) * (1.0 / ROWS)
            q = rowsum(stat[SUB:2 * SUB]) * (1.0 / ROWS)
            stat[2 * SUB:2 * SUB + 1] = m0 + dm
            stat[3 * SUB:3 * SUB + 1] = lax.rsqrt(jnp.maximum(q - dm * dm, 0.0) + BN_EPS)
            z_copy(j).start()

    @pl.when(j == 0)
    def _():
        step(True, True, False)

    @pl.when(jnp.logical_and(j > 0, j < NB))
    def _():
        step(False, True, True)

    @pl.when(j == NB)
    def _():
        for b in range(6):
            wt_copy(b).start()
        step(False, False, True)

    @pl.when(j == NB + 1)
    def _():
        for b in range(6, NB):
            wt_copy(b).start()
        stages()
        wtb[CLASSES:] = jnp.zeros((KP - CLASSES, COUT), BF16)
        for b in range(NB):
            wt_copy(b).wait()
            view = wt_view(b)

            def cast(i, acc):
                w = view[span(i, 40), :]
                wtb[span(i, 40), b * CB:(b + 1) * CB] = w.astype(BF16)
                return acc + fold(w * w)
            fsq_ref[:, b * CB:(b + 1) * CB] = lax.fori_loop(0, CLASSES // 40, cast, jnp.zeros((SUB, CB), F32))
        wtb_copy().start()

    @pl.when(j == NB + 2)
    def _():
        stages()
        own = pfull[core, y, x].astype(BF16)
        lg = dot_t(own, wtb[:])
        _, dl = softmax_terms(lg, bpad[:], label_rows(lab_ref[:]))
        dlb = dl.astype(BF16)

        def col(b, carry):
            c = cols(b)
            dp = dot(dlb, wtb[:, c]) * (1.0 / POS)
            dbeta = rowsum(dp * cnt[:, c])
            dgamma = rowsum(dp * sx[:, c])
            sc = sc_ref[:, c]
            cc = -(sc * sv[SUB:SUB + 1, c]) * (dgamma * (1.0 / ROWS))
            cc_ref[:, c] = cc
            bb_ref[:, c] = -sc * (dbeta * (1.0 / ROWS)) - sv[:1, c] * cc
            da_ref[:, c] = dp * sc
            db_ref[:1, c] = dgamma
            db_ref[1:, c] = dbeta
            return carry
        lax.fori_loop(0, NB, col, 0)

    @pl.when(j == NB + TAIL)
    def _():
        stages()
        each(wait, labels)
        lall_ref[:] = lfull[:]
        wtb_copy().wait()

        def drain(b, carry):
            each(wait_send, gather_all(pfull, gs, gr, b))
            return carry
        lax.fori_loop(0, NB, drain, 0)


def whole(*shape):
    return pl.BlockSpec(shape, lambda j: (0,) * len(shape))


def struct(shape, dtype=F32):
    return jax.ShapeDtypeStruct(shape, dtype)


def fvmem(*shape):
    return pltpu.VMEM(shape, F32)


def bvmem(*shape):
    return pltpu.VMEM(shape, BF16)


def dma(*shape):
    return pltpu.SemaphoreType.DMA(shape)


HBM = pl.BlockSpec(memory_space=pl.ANY)
QUAD = (2, 2, 2)


def forward(a, w, s, gamma, beta, labels, bias, wt):
    prev = lambda j: (0, jnp.clip(j - 1, 0, NB - 1))
    cur = lambda j: (0, jnp.minimum(j, NB - 1))
    late = lambda j: (0, jnp.clip(j - 4, 0, NB - 1))
    vec, lab = (1, COUT), QUAD + (1, IMG)
    return pl.pallas_call(
        fwd_kernel,
        grid=(NB + 1 + TAIL,),
        in_specs=[HBM, pl.BlockSpec((CIN, CB), cur), pl.BlockSpec((ROWS, CB), prev), pl.BlockSpec((1, CB), prev), pl.BlockSpec((1, CB), prev),
                  whole(1, IMG), whole(1, CLASSES), HBM],
        out_specs=[HBM, pl.BlockSpec((IMG, ROWS), lambda j: (jnp.minimum(j, NB - 1), 0)), pl.BlockSpec((TOTAL, CB), late), whole(*lab),
                   whole(SUB, CB), whole(SUB, COUT), HBM, whole(IMG, COUT)] + [whole(*vec)] * 4 + [whole(2, COUT)],
        out_shape=[struct((NB, ROWS, CB)), struct((CIN, ROWS), BF16), struct((TOTAL, COUT), BF16), struct(lab, jnp.int32),
                   struct((SUB, CB)), struct((SUB, COUT)), struct((KP, COUT), BF16), struct((IMG, COUT))] + [struct(vec)] * 4 + [struct((2, COUT))],
        scratch_shapes=[bvmem(ROWS, APAD), fvmem(2, ROWS, CB), bvmem(CIN, CB), fvmem(4 * SUB, CB), fvmem(*QUAD, IMG, COUT), pltpu.VMEM(lab, jnp.int32),
                        fvmem(IMG, CB), fvmem(IMG, COUT), fvmem(IMG, COUT), fvmem(2 * SUB, COUT), bvmem(KP, COUT), fvmem(1, KP),
                        dma(NCH), dma(2), dma(NB), pltpu.SemaphoreType.DMA, dma(5, NB), dma(5, NB), dma(DEVS), dma(DEVS)],
        compiler_params=pltpu.CompilerParams(vmem_limit_bytes=63 * MIB, collective_id=0, has_side_effects=True),
        cost_estimate=pl.CostEstimate(flops=2 * ROWS * CIN * COUT, bytes_accessed=2 * ROWS * COUT * 4, transcendentals=0),
        name="fwd_conv",
    )(a, w, s, gamma, beta, labels, bias, wt)


def bwd_kernel(at_hbm, z_ref, s_ref, sc_ref, sh_ref, bb_ref, cc_ref, da_ref, db_ref, pall_hbm, wtb_hbm, lab_ref, bias_ref,
               g_hbm, dbo_ref, gsq_ref, gfc_hbm, fsq_ref, gb_ref, loss_ref,
               atv, dz, dw, rd, ha, hb, ra, rb, ka, kb, r2a, r2b, gfull, dball, bpad, ss, rs, gs, gr, bs, br, osem, isem, fsem):
    j = pl.program_id(0)
    slot = lax.rem(j, 2)
    prev = 1 - slot
    me, core, x, y = position()
    plan = pl.ds(0, COUT)
    pall = atv.at[:, plan]
    wtb = atv.at[:, pl.ds(COUT, COUT)]
    dlt = atv.at[:, pl.ds(2 * COUT, TOTAL)]

    at_copy = pltpu.make_async_copy(at_hbm, atv, isem.at[0])
    pall_copy = pltpu.make_async_copy(pall_hbm, pall, isem.at[1])
    wtb_copy = pltpu.make_async_copy(wtb_hbm, wtb, isem.at[2])
    db_copies = [rcopy(db_ref, dball.at[me], bs.at[k], br.at[k], lax.rem(me + k, DEVS)) for k in range(1, DEVS)]

    @pl.when(j == 0)
    def _():
        at_copy.start()
        enter_all()
        each(start, db_copies)
        dball[me] = db_ref[:]
        for r in (gsq_ref, fsq_ref, gb_ref, loss_ref):
            r[:] = jnp.zeros_like(r)
        set_bias(bpad, bias_ref)

    @pl.when(j == 1)
    def _():
        at_copy.wait()

    def out_copy(b):
        c = cols(b)
        return pltpu.make_async_copy(gfull.at[:, :, :, :, c], g_hbm.at[:, :, :, :, c], osem.at[b])

    def core_copy(b, k=0):
        return rcopy(dw.at[lax.rem(b, 2), span(1 - core, HALF), :], rd.at[b], ss.at[k, b], rs.at[k, b], neighbour(PN))

    def first_copies(b, k=1, m=2):
        sl = lax.rem(b, 2)
        return (rcopy(ha.at[sl, 1 - x], ra.at[b], ss.at[k, b], rs.at[k, b], neighbour(XN)),
                rcopy(hb.at[sl, 1 - y], rb.at[b], ss.at[m, b], rs.at[m, b], neighbour(YN)))

    def second_copies(b, k=3, m=4):
        sl = lax.rem(b, 2)
        return (rcopy(ka.at[sl, 1 - y], r2a.at[b], ss.at[k, b], rs.at[k, b], neighbour(YN)),
                rcopy(kb.at[sl, 1 - x], r2b.at[b], ss.at[m, b], rs.at[m, b], neighbour(XN)))

    def stage1(b):
        core_copy(b).wait()
        sl = lax.rem(b, 2)
        for q, (py, px) in enumerate((py, px) for py in range(2) for px in range(2)):
            own = pl.ds(pl.multiple_of(core * HALF + q * QR, QR), QR)
            got = slice(q * QR, (q + 1) * QR)
            ha[sl, px, py] = dw[sl, own, :HC] + rd[b, got, :HC]
            hb[sl, py, px] = dw[sl, own, HC:] + rd[b, got, HC:]
        each(start, first_copies(b))

    def stage2(b):
        sl = lax.rem(b, 2)
        each(wait, first_copies(b))
        for k in range(2):
            ka[sl, k] = ha[sl, x, k] + ra[b, k]
            kb[sl, k] = hb[sl, y, k] + rb[b, k]
        each(start, second_copies(b))

    def stage3(b):
        sl = lax.rem(b, 2)
        each(wait, second_copies(b))
        gfull[core, y, x, :, cols(b, HC)] = ka[sl, y] + r2a[b]
        gfull[core, y, x, :, cols(b, HC, HC)] = kb[sl, x] + r2b[b]
        each(start, gather_own(gfull, gs, gr, b))

    def stage4(b):
        each(wait_recv, gather_own(gfull, gs, gr, b))
        each(start, gather_on(gfull, gs, gr, b))

    def stage5(b):
        each(wait_recv, gather_on(gfull, gs, gr, b))
        each(start, gather_core(gfull, gs, gr, b))

    def stage6(b):
        each(wait_recv, gather_core(gfull, gs, gr, b))
        out_copy(b).start()
        acc = gsq_ref[:]
        for q in pieces():
            gv = gfull[q + (slice(None), cols(b))]
            acc = acc + fold(gv * gv)
        gsq_ref[:] = acc

    def stages():
        stage_list(j, (stage1, stage2, stage3, stage4, stage5, stage6))

    def step(do_pre, do_mm):
        if do_pre:
            sc, sh, bb, cc = sc_ref[:], sh_ref[:], bb_ref[:], cc_ref[:]

        def pre(base, slabs):
            for n in range(0, IMG, NT):
                da = da_ref[n:n + NT, :]
                for p in range(slabs):
                    r = pl.ds(base + p * IMG + n, NT)
                    zz = z_ref[r, :]
                    u = zz * sc + sh + s_ref[r, :].astype(F32)
                    dz[slot, r, :] = (jnp.where(u > 0, da, 0.0) + (zz * cc + bb)).astype(BF16)

        def mm(base, size):
            return dot(atv[:, pl.ds(base, size)], dz[prev, pl.ds(base, size), :])

        rest = NBIG * BIG
        if do_mm:
            dw[prev] = mm(rest, ROWS - rest)
        if do_pre:
            pre(rest, POS - NBIG * BTILE)

        def chunk(i, carry):
            base = pl.multiple_of(i * BIG, BIG)
            if do_mm:
                pl.when(i == 1)(stages)
                dw[prev] += mm(base, BIG)
            if do_pre:
                pre(base, BTILE)
            return carry
        lax.fori_loop(0, NBIG, chunk, 0)
        if do_mm:
            core_copy(j - 1).start()

    @pl.when(j == 0)
    def _():
        step(True, False)

    @pl.when(jnp.logical_and(j > 0, j < NB))
    def _():
        step(True, True)

    def logits_unit(i):
        rows = span(i, LB)
        lg = dot_t(pall[rows, :], wtb[:])
        lab = jnp.concatenate([label_rows(lab_ref[i // 2, lax.rem(i, 2), k]) for k in range(2)])
        lterm, dl = softmax_terms(lg, bpad[:], lab)
        loss_ref[:] += fold(lterm)
        gb_ref[:] += fold(dl)
        dlt[:, pl.ds(pl.multiple_of(i * LB, LB), LB)] = dl.T.astype(BF16)

    def fc_copies(c):
        sl = lax.rem(c, 4)
        return [pltpu.make_async_copy(rd.at[sl * 2 + h], gfc_hbm.at[pl.ds(h * HALF, HALF), cols(c)], fsem.at[h, c]) for h in range(2)]

    def dfc_unit(c):
        pl.when(c >= 4)(lambda: each(wait, fc_copies(c - 4)))
        acc = jnp.zeros((SUB, CB), F32)
        for h in range(2):
            g = dot(dlt[pl.ds(h * HALF, HALF), :], pall[:, cols(c)])
            rd[lax.rem(c, 4) * 2 + h] = g
            acc = acc + fold(g * g)
        fsq_ref[:, cols(c)] = acc
        each(start, fc_copies(c))

    def loop(lo, hi, fn):
        def body(i, carry):
            fn(i)
            return carry
        lax.fori_loop(lo, hi, body, 0)

    @pl.when(j == NB)
    def _():
        step(False, True)
        pall_copy.start()
        wtb_copy.start()

    @pl.when(j > NB)
    def _():
        stages()
        k = j - NB - 1

        @pl.when(k == 0)
        def _():
            pall_copy.wait()
            wtb_copy.wait()

        loop(jnp.minimum(k * 3, 4), jnp.minimum(k * 3 + 3, 4), logits_unit)
        loop(jnp.clip(k * 3 - 3, 0, NB), jnp.clip(k * 3, 0, NB), dfc_unit)

    @pl.when(j == NB + BTAIL - 1)
    def _():
        each(wait, db_copies)
        acc = dball[0]
        for k in range(1, DEVS):
            acc = acc + dball[k]
        dbo_ref[:] = acc
        for c in range(4, NB):
            each(wait, fc_copies(c))

        def drain(b):
            each(wait_send, gather_all(gfull, gs, gr, b))
            out_copy(b).wait()
        loop(0, NB, drain)


def backward(at, z, s, sc, sh, bb, cc, da, dgb, pall, wtb, lab, bias):
    cur = lambda j: (0, jnp.minimum(j, NB - 1))
    row = pl.BlockSpec((1, CB), cur)
    pair, quad, side = (2, QR, HC), (2, 2, 2, QR, HC), (NB, QR, HC)
    return pl.pallas_call(
        bwd_kernel,
        grid=(NB + BTAIL,),
        in_specs=[HBM, pl.BlockSpec((None, ROWS, CB), lambda j: (jnp.minimum(j, NB - 1), 0, 0)), pl.BlockSpec((ROWS, CB), cur), row, row, row, row,
                  pl.BlockSpec((IMG, CB), cur), whole(2, COUT), HBM, HBM, whole(2, 2, 2, 1, IMG), whole(1, CLASSES)],
        out_specs=[HBM, whole(2, COUT), whole(SUB, CB), HBM, whole(SUB, COUT), whole(SUB, KP), whole(SUB, KP)],
        out_shape=[struct(QUAD + (QR, COUT)), struct((2, COUT)), struct((SUB, CB)), struct((KP, COUT)), struct((SUB, COUT)), struct((SUB, KP)), struct((SUB, KP))],
        scratch_shapes=[bvmem(CIN, ROWS), bvmem(2, ROWS, CB), fvmem(2, CIN, CB), fvmem(NB, HALF, CB), fvmem(*quad), fvmem(*quad),
                        fvmem(NB, *pair), fvmem(NB, *pair), fvmem(2, *pair), fvmem(2, *pair), fvmem(*side), fvmem(*side),
                        fvmem(*QUAD, QR, COUT), fvmem(DEVS, 2, COUT), fvmem(1, KP),
                        dma(5, NB), dma(5, NB), dma(5, NB), dma(5, NB), dma(DEVS), dma(DEVS), dma(NB), dma(3), dma(2, NB)],
        compiler_params=pltpu.CompilerParams(vmem_limit_bytes=63 * MIB, collective_id=1, has_side_effects=True),
        cost_estimate=pl.CostEstimate(flops=2 * ROWS * CIN * COUT, bytes_accessed=2 * ROWS * COUT * 4, transcendentals=0),
        name="bwd_conv",
    )(at, z, s, sc, sh, bb, cc, da, dgb, pall, wtb, lab, bias)


def trust_of(wsq, gsq):
    wn = jnp.sqrt(lanesum(rowsum(wsq)))
    gn = jnp.sqrt(lanesum(rowsum(gsq)))
    return TRUST_COEF * wn / (gn + WEIGHT_DECAY * wn)


def update_kernel(lr_ref, w_ref, v_ref, g_ref, wsq_ref, gsq_ref, wt_ref, vt_ref, gt_ref, tsq_ref, fsq_ref, bias_ref, vbias_ref, gb_ref, ls_ref,
                  gam_ref, bet_ref, vgam_ref, vbet_ref, dgb_ref,
                  wo_ref, vo_ref, wto_ref, vto_ref, bo_ref, vbo_ref, go_ref, vgo_ref, beo_ref, vbeo_ref, loss_ref):
    j = pl.program_id(0)
    lr = lr_ref[0]

    def plain(p, v, g, po, vo):
        nv = MOMENTUM * v[:] + lr * g
        vo[:] = nv
        po[:] = p[:] - nv

    @pl.when(j == 0)
    def _():
        plain(gam_ref, vgam_ref, dgb_ref[:1], go_ref, vgo_ref)
        plain(bet_ref, vbet_ref, dgb_ref[1:], beo_ref, vbeo_ref)
        plain(bias_ref, vbias_ref, rowsum(gb_ref[:])[:, :CLASSES], bo_ref, vbo_ref)
        loss_ref[:] = lanesum(rowsum(ls_ref[:])) * (-1.0 / TOTAL)

    def lars(w_ref, v_ref, g_ref, wsq, gsq, wo, vo, rows):
        rate = jnp.broadcast_to(lr * trust_of(wsq[:], gsq[:]), (SUB, CB))

        def row(i, carry):
            for q in range(2):
                r = pl.ds(pl.multiple_of(i * 2 * SUB + q * SUB, SUB), SUB)
                for c in range(0, COUT, CB):
                    cc = slice(c, c + CB)
                    w = w_ref[r, cc]
                    nv = MOMENTUM * v_ref[r, cc] + rate * (g_ref[r, cc] + WEIGHT_DECAY * w)
                    vo[r, cc] = nv
                    wo[r, cc] = w - nv
            return carry
        lax.fori_loop(0, rows // (2 * SUB), row, 0)

    @pl.when(j < NU)
    def _():
        lars(w_ref, v_ref, g_ref, wsq_ref, gsq_ref, wo_ref, vo_ref, UB)

    @pl.when(j >= NU)
    def _():
        lars(wt_ref, vt_ref, gt_ref, tsq_ref, fsq_ref, wto_ref, vto_ref, FB)


def update_all(*args):
    conv = pl.BlockSpec((UB, COUT), lambda j: (jnp.minimum(j, NU - 1), 0))
    fc = pl.BlockSpec((FB, COUT), lambda j: (jnp.clip(j - NU, 0, NF - 1), 0))
    vec, bvec, one = (1, COUT), (1, CLASSES), (1, 1)
    vs, bs = whole(*vec), whole(*bvec)
    big, fcs = struct((CIN, COUT)), struct((CLASSES, COUT))
    return pl.pallas_call(
        update_kernel,
        grid=(NU + NF,),
        in_specs=[pl.BlockSpec(memory_space=pltpu.SMEM), conv, conv, conv, whole(SUB, CB), whole(SUB, CB), fc, fc, fc, whole(SUB, COUT), whole(SUB, COUT),
                  bs, bs, whole(SUB, KP), whole(SUB, KP), vs, vs, vs, vs, whole(2, COUT)],
        out_specs=[conv, conv, fc, fc, bs, bs, vs, vs, vs, vs, whole(*one)],
        out_shape=[big, big, fcs, fcs] + [struct(bvec)] * 2 + [struct(vec)] * 4 + [struct(one)],
        compiler_params=pltpu.CompilerParams(vmem_limit_bytes=63 * MIB),
        cost_estimate=pl.CostEstimate(flops=CIN * COUT * 16, bytes_accessed=10 * CIN * COUT * 4, transcendentals=0),
        name="update",
    )(*args)


def solution(mesh):
    def local_step(act_in, shortcut, labels, w_conv, gamma, beta, w_fc, fc_bias, vel_conv, vel_gamma, vel_beta, vel_fc, vel_bias, lr):
        a = act_in.transpose(1, 2, 0, 3).reshape(ROWS, CIN)
        s = shortcut.transpose(1, 2, 0, 3).reshape(ROWS, COUT)
        wt = w_fc.T
        bias = fc_bias[None]
        z, at, pall, lab, wsq, tsq, wtb, da, sc, sh, bb, cc, dgb = forward(a, w_conv, s, gamma[None], beta[None], labels[None], bias, wt)
        g8, dgb, gsq, gfc, fsq, gb, ls = backward(at, z, s, sc, sh, bb, cc, da, dgb, pall, wtb, lab, bias)
        wo, vo, wto, vto, bo, vbo, go, vgo, beo, vbeo, loss = update_all(
            lr.reshape(1), w_conv, vel_conv, g8.reshape(CIN, COUT), wsq, gsq, wt, vel_fc.T, gfc, tsq, fsq, bias, vel_bias[None], gb, ls,
            gamma[None], beta[None], vel_gamma[None], vel_beta[None], dgb)
        return (wo, go[0], beo[0], wto.T, bo[0], vo, vgo[0], vbeo[0], vto.T, vbo[0], loss[0, 0])

    return jax.shard_map(local_step, mesh=mesh, in_specs=(P('dp'),) * 3 + (P(),) * 11, out_specs=(P(),) * 11, check_vma=False)
```

time: 465 us -> 212 us (0.46)
  Pallas kernels: 0 us -> 211 us
  waiting for transfers between devices: 172 us -> 0 us
  other arithmetic: 126 us -> 0 us
  matrix products: 85.8 us -> 0 us
  local copies, waits for them, and re-layouts: 36.8 us -> 0 us
  blocking collectives: 23.8 us -> 0 us
  between operations: 18.3 us -> 1.46 us
    pallas_call x0 -> x3, Pallas kernels: none -> 211 us  [the longest x1 98.8 us: backward(): pl.pallas_call(bwd_kernel, grid=(NB + BTAIL,), in_specs=[HBM, pl.BlockSpe...]
    psum x1 -> x0, waiting for transfers between devices: 172 us -> none  [local_step(): lax.psum(local_terms, 'dp')]
    reduce_sum x9 -> x0, other arithmetic: 95.9 us -> none  [the longest x1 29.9 us: forward_backward(): d_beta = jnp.sum(d_pre, axis=(0, 1))]
    dot_general x5 -> x0, matrix products: 85.8 us -> none  [the longest x1 39.1 us: forward_backward(): jnp.einsum('bpc,bpd->cd', act_grid, d_conv_out.astype(jnp.bfloat16), pref...]
    unnamed x22 -> x0, local copies, waits for them, and re-layouts: 36.8 us -> none
    sub x5 -> x0, other arithmetic: 29.9 us -> none  [the longest x2 28.1 us: lars_update(): return (weight - new_vel, new_vel)]
    psum x1 -> x0, blocking collectives: 23.8 us -> none  [local_step(): lax.psum(local_terms, 'dp')]
  transfers between devices with their start and end apart: 1 -> 0, of which waited for: 1 -> 0; matrix products, arithmetic and copies ran while one was open for 7% -> 0% of each run, Pallas kernels for 0% -> 0%
where the time goes in v4:
time: 212 us
  Pallas kernels  211 us (100%)
    pallas_call x1, Pallas kernels, backward(): pl.pallas_call(bwd_kernel, grid=(NB + BTAIL,), in_specs=[HBM, pl.BlockSpe...  98.8 us
    pallas_call x1, Pallas kernels, forward(): pl.pallas_call(fwd_kernel, grid=(NB + 1 + TAIL,), in_specs=[HBM, pl.Block...  81.6 us
    pallas_call x1, Pallas kernels, update_all(): pl.pallas_call(update_kernel, grid=(NU + NF,), in_specs=[pl.BlockSpec(mem...  30.5 us

profile of v4, /device:TPU:1, one launch (start us, length us, event | category | flops | bytes accessed | tf_op | source)
XLA Modules:
  0.0 212.3 jit_solution(16469851793972710150)
XLA Ops:
  0.6 81.6 %fwd_conv.1 = (f32[8,6272,256]{2,1,0:T(8,128)}, bf16[1024,6272]{1,0:T(8,128)(2,1)}, bf16[1024,2048]{1,0:T(8,128)(2,1)}, s32[2,2,2,1,128]{4,3,2,1,0:T(1,128)}, f3...) custom-call(bf16[6272,1024]{1,0:T(8,128)(2,1)} %bitcast.43, ...), custom_call_target="tpu_custom_call" | custom-call | flops 26306674688 | bytes 102760448 | tf_op jit(solution)/shard_map/fwd_conv/pallas_call | solution.py:409
  82.2 98.8 %bwd_conv.1 = (f32[2,2,2,128,2048]{4,3,2,1,0:T(8,128)}, f32[2,2048]{1,0:T(2,128)}, f32[8,256]{1,0:T(8,128)}, f32[1024,2048]{1,0:T(8,128)}, f32[8,2048]{1,0:T(8,1...) custom-call(bf16[1024,6272]{1,0:T(8,128)(2,1)} %get-tuple-element.42.at_hbm, f32[8,6272,256]{2,1,0:T(8,128)} %get-tuple-element.43.z_ref, ...), custom_call_target="tpu_custom_call" | custom-call | flops 26306674688 | bytes 102760448 | tf_op jit(solution)/shard_map/bwd_conv/pallas_call | solution.py:630
  181.6 30.5 %update.1 = (f32[1024,2048]{1,0:T(8,128)}, f32[1024,2048]{1,0:T(8,128)}, f32[1000,2048]{1,0:T(8,128)}, f32[1000,2048]{1,0:T(8,128)}, f32[1,1000]{1,0:T(1,128)}, ...) custom-call(f32[1]{0:T(128)} %bitcast.26.lr_ref, ...), custom_call_target="tpu_custom_call" | custom-call | flops 33554432 | bytes 83886080 | tf_op jit(solution)/shard_map/update/pallas_call | solution.py:701

commit v5 on v4

--- a/solution.py
+++ b/solution.py
@@ -29,6 +29,8 @@
 CH = 7
 NCH = POS // CH
 NT = 16
+PIECES = 8
+BPIECES = 4
 APAD = CIN + LANES
 TAIL = 3
 BTAIL = 7
@@ -186,10 +188,9 @@
 
 def fwd_kernel(a_hbm, w_ref, s_ref, g_ref, b_ref, lab_ref, bias_ref, wt_hbm,
                z_hbm, at_ref, pall_ref, lall_ref, wsq_ref, fsq_ref, wtb_hbm, da_ref, sc_ref, sh_ref, bb_ref, cc_ref, db_ref,
-               abf, zbuf, wbf, stat, pfull, lfull, pool, cnt, sx, sv, wtb, bpad, asem, zsem, wsem, osem, gs, gr, ls, lr):
+               abf, z0, z1, wbf, stat, pfull, lfull, pool, cnt, sx, sv, wtb, bpad, asem, zsem, wsem, osem, gs, gr, ls, lr):
     j = pl.program_id(0)
-    slot = lax.rem(j, 2)
-    prev = 1 - slot
+    zs = (z0, z1)
     me, core, x, y = position()
     crow = CH * IMG
 
@@ -197,12 +198,11 @@
         r = span(i, crow)
         return pltpu.make_async_copy(a_hbm.at[r, :], abf.at[r, :CIN], asem.at[i])
 
-    def z_copy(jj):
-        sl = lax.rem(jj, 2)
-        return pltpu.make_async_copy(zbuf.at[sl], z_hbm.at[jj], zsem.at[sl])
+    def z_copy(jj, par):
+        return pltpu.make_async_copy(zs[par], z_hbm.at[jj], zsem.at[par])
 
     def wt_view(b):
-        return zbuf.at[b // 6, pl.ds((b % 6) * CLASSES, CLASSES), :]
+        return zs[b // 6].at[pl.ds((b % 6) * CLASSES, CLASSES), :]
 
     def wt_copy(b):
         return pltpu.make_async_copy(wt_hbm.at[:, pl.ds(b * CB, CB)], wt_view(b), wsem.at[b])
@@ -241,11 +241,11 @@
     def stages():
         stage_list(j, (second, third, last))
 
-    @pl.when(jnp.logical_and(j >= 2, j < NB + 2))
-    def _():
-        z_copy(j - 2).wait()
-
-    def step(first, do_mm, do_post):
+    def step(par, do_mm, do_post):
+        first = not do_post
+        slot, prev = zs[par], zs[1 - par]
+        if do_post:
+            pl.when(j >= 2)(lambda: z_copy(j - 2, par).wait())
         if do_mm:
             wf = w_ref[:]
             wsq_ref[:] += fold(wf * wf)
@@ -255,6 +255,9 @@
                 a_copy(0).wait()
             m0 = rowsum(dot(abf[:IMG, :CIN], w)) * (1.0 / IMG)
             stat[:2 * SUB] = jnp.zeros((2 * SUB, CB), F32)
+        if do_post and not do_mm:
+            for b in range(6):
+                wt_copy(b).start()
         if do_post:
             mean = stat[2 * SUB:2 * SUB + 1]
             inv = stat[3 * SUB:3 * SUB + 1]
@@ -265,36 +268,57 @@
             cnt[:, pc] = jnp.zeros((IMG, CB), F32)
             sx[:, pc] = jnp.zeros((IMG, CB), F32)
 
+        def post(base, n, slabs):
+            nr = slice(n, n + NT)
+            pa, ca, xa = pool[nr], cnt[nr, pc], sx[nr, pc]
+            for p in range(slabs):
+                r = pl.ds(base + p * IMG + n, NT)
+                zz = prev[r, :]
+                u = zz * sc + sh + s_ref[r, :].astype(F32)
+                mk = u > 0
+                pa = pa + jnp.maximum(u, 0.0)
+                ca = ca + jnp.where(mk, 1.0, 0.0)
+                xa = xa + jnp.where(mk, zz, 0.0)
+            pool[nr], cnt[nr, pc], sx[nr, pc] = pa, ca, xa
+
+        def flip(base, rows):
+            r = pl.ds(base, rows)
+            at_ref[:, r] = abf[r, pl.ds(pl.multiple_of(j * IMG, IMG), IMG)].astype(F32).T.astype(BF16)
+
+        def region(base, slabs, parts):
+            size = slabs * IMG // parts
+            for k in range(parts):
+                if do_mm:
+                    r = pl.ds(base + k * size, size)
+                    zc = dot(abf[r, :CIN], wbf[:])
+                if do_post:
+                    for n in range(k * IMG // parts, (k + 1) * IMG // parts, NT):
+                        post(base, n, slabs)
+                if do_mm:
+                    slot[r, :] = zc
+                    d = zc - m0
+                    stat[:SUB] += fold(d)
+                    stat[SUB:2 * SUB] += fold(d * d)
+
+            if do_mm:
+                flip(base, slabs * IMG)
+
         def chunk(i, carry):
-            base = pl.multiple_of(i * crow, crow)
-            if do_post:
-                pl.when(i == 4)(stages)
-            if do_mm:
-                if first:
-                    pl.when(i > 0)(lambda: a_copy(i).wait())
-                r = pl.ds(base, crow)
-                zc = dot(abf[r, :CIN], wbf[:])
-                zbuf[slot, r, :] = zc
-                d = zc - m0
-                stat[:SUB] += fold(d)
-                stat[SUB:2 * SUB] += fold(d * d)
-                at_ref[:, r] = abf[r, pl.ds(pl.multiple_of(j * IMG, IMG), IMG)].astype(F32).T.astype(BF16)
-            if do_post:
-                for n in range(0, IMG, NT):
-                    nr = slice(n, n + NT)
-                    pa, ca, xa = pool[nr], cnt[nr, pc], sx[nr, pc]
-                    for p in range(CH):
-                        r = pl.ds(base + p * IMG + n, NT)
-                        zz = zbuf[prev, r, :]
-                        u = zz * sc + sh + s_ref[r, :].astype(F32)
-                        mk = u > 0
-                        pa = pa + jnp.maximum(u, 0.0)
-                        ca = ca + jnp.where(mk, 1.0, 0.0)
-                        xa = xa + jnp.where(mk, zz, 0.0)
-                    pool[nr], cnt[nr, pc], sx[nr, pc] = pa, ca, xa
+            if first:
+                pl.when(i > 0)(lambda: a_copy(i).wait())
+            region(pl.multiple_of(i * crow, crow), CH, 4)
             return carry
 
-        lax.fori_loop(0, NCH, chunk, 0)
+        def chunk2(i, carry):
+            pl.when(i == 2)(stages)
+            region(pl.multiple_of(i * 2 * crow, 2 * crow), 2 * CH, PIECES)
+            return carry
+
+        if first:
+            lax.fori_loop(0, NCH, chunk, 0)
+        else:
+            lax.fori_loop(0, NCH // 2, chunk2, 0)
+            region(pl.multiple_of((jnp.minimum(me, 0) + NCH - 1) * crow, crow), CH, 4)
         if do_post:
             pfull[core, y, x, :, pc] = pool[:] * (1.0 / POS)
             sx[:, pc] = (sx[:, pc] - mean * cnt[:, pc]) * inv
@@ -308,24 +332,24 @@
             q = rowsum(stat[SUB:2 * SUB]) * (1.0 / ROWS)
             stat[2 * SUB:2 * SUB + 1] = m0 + dm
             stat[3 * SUB:3 * SUB + 1] = lax.rsqrt(jnp.maximum(q - dm * dm, 0.0) + BN_EPS)
-            z_copy(j).start()
+            z_copy(j, par).start()
 
     @pl.when(j == 0)
     def _():
-        step(True, True, False)
-
-    @pl.when(jnp.logical_and(j > 0, j < NB))
-    def _():
-        step(False, True, True)
+        step(0, True, False)
+
+    for par in range(2):
+        @pl.when(jnp.logical_and(jnp.logical_and(j > 0, j < NB), lax.rem(j, 2) == par))
+        def _():
+            step(par, True, True)
 
     @pl.when(j == NB)
     def _():
-        for b in range(6):
-            wt_copy(b).start()
-        step(False, False, True)
+        step(0, False, True)
 
     @pl.when(j == NB + 1)
     def _():
+        z_copy(NB - 1, 1).wait()
         for b in range(6, NB):
             wt_copy(b).start()
         stages()
@@ -415,7 +439,7 @@
                    whole(SUB, CB), whole(SUB, COUT), HBM, whole(IMG, COUT)] + [whole(*vec)] * 4 + [whole(2, COUT)],
         out_shape=[struct((NB, ROWS, CB)), struct((CIN, ROWS), BF16), struct((TOTAL, COUT), BF16), struct(lab, jnp.int32),
                    struct((SUB, CB)), struct((SUB, COUT)), struct((KP, COUT), BF16), struct((IMG, COUT))] + [struct(vec)] * 4 + [struct((2, COUT))],
-        scratch_shapes=[bvmem(ROWS, APAD), fvmem(2, ROWS, CB), bvmem(CIN, CB), fvmem(4 * SUB, CB), fvmem(*QUAD, IMG, COUT), pltpu.VMEM(lab, jnp.int32),
+        scratch_shapes=[bvmem(ROWS, APAD), fvmem(ROWS, CB), fvmem(ROWS, CB), bvmem(CIN, CB), fvmem(4 * SUB, CB), fvmem(*QUAD, IMG, COUT), pltpu.VMEM(lab, jnp.int32),
                         fvmem(IMG, CB), fvmem(IMG, COUT), fvmem(IMG, COUT), fvmem(2 * SUB, COUT), bvmem(KP, COUT), fvmem(1, KP),
                         dma(NCH), dma(2), dma(NB), pltpu.SemaphoreType.DMA, dma(5, NB), dma(5, NB), dma(DEVS), dma(DEVS)],
         compiler_params=pltpu.CompilerParams(vmem_limit_bytes=63 * MIB, collective_id=0, has_side_effects=True),
@@ -426,10 +450,9 @@
 
 def bwd_kernel(at_hbm, z_ref, s_ref, sc_ref, sh_ref, bb_ref, cc_ref, da_ref, db_ref, pall_hbm, wtb_hbm, lab_ref, bias_ref,
                g_hbm, dbo_ref, gsq_ref, gfc_hbm, fsq_ref, gb_ref, loss_ref,
-               atv, dz, dw, rd, ha, hb, ra, rb, ka, kb, r2a, r2b, gfull, dball, bpad, ss, rs, gs, gr, bs, br, osem, isem, fsem):
+               atv, dz0, dz1, dw, rd, ha, hb, ra, rb, ka, kb, r2a, r2b, gfull, dball, bpad, ss, rs, gs, gr, bs, br, osem, isem, fsem):
     j = pl.program_id(0)
-    slot = lax.rem(j, 2)
-    prev = 1 - slot
+    dzs = (dz0, dz1)
     me, core, x, y = position()
     plan = pl.ds(0, COUT)
     pall = atv.at[:, plan]
@@ -517,35 +540,42 @@
     def stages():
         stage_list(j, (stage1, stage2, stage3, stage4, stage5, stage6))
 
-    def step(do_pre, do_mm):
+    def step(par, do_pre, do_mm):
+        slot, prev = dzs[par], dzs[1 - par]
+        out = dw.at[1 - par]
         if do_pre:
             sc, sh, bb, cc = sc_ref[:], sh_ref[:], bb_ref[:], cc_ref[:]
 
-        def pre(base, slabs):
-            for n in range(0, IMG, NT):
-                da = da_ref[n:n + NT, :]
-                for p in range(slabs):
-                    r = pl.ds(base + p * IMG + n, NT)
-                    zz = z_ref[r, :]
-                    u = zz * sc + sh + s_ref[r, :].astype(F32)
-                    dz[slot, r, :] = (jnp.where(u > 0, da, 0.0) + (zz * cc + bb)).astype(BF16)
-
-        def mm(base, size):
-            return dot(atv[:, pl.ds(base, size)], dz[prev, pl.ds(base, size), :])
+        def pre(base, n):
+            da = da_ref[n:n + NT, :]
+            for p in range(CH):
+                r = pl.ds(base + p * IMG + n, NT)
+                zz = z_ref[r, :]
+                u = zz * sc + sh + s_ref[r, :].astype(F32)
+                slot[r, :] = (jnp.where(u > 0, da, 0.0) + (zz * cc + bb)).astype(BF16)
+
+        def body(base, slabs, add):
+            work = [functools.partial(pre, base + p * IMG, n) for p in range(0, slabs, CH) for n in range(0, IMG, NT)]
+            size = slabs * IMG
+            for k in range(BPIECES):
+                m = slice(k * CIN // BPIECES, (k + 1) * CIN // BPIECES)
+                if do_mm:
+                    g = dot(atv[m, pl.ds(base, size)], prev[pl.ds(base, size), :])
+                if do_pre:
+                    n = len(work)
+                    for f in work[k * n // BPIECES:(k + 1) * n // BPIECES]:
+                        f()
+                if do_mm:
+                    out[m] = out[m] + g if add else g
 
         rest = NBIG * BIG
-        if do_mm:
-            dw[prev] = mm(rest, ROWS - rest)
-        if do_pre:
-            pre(rest, POS - NBIG * BTILE)
+        body(rest, POS - NBIG * BTILE, False)
 
         def chunk(i, carry):
             base = pl.multiple_of(i * BIG, BIG)
             if do_mm:
                 pl.when(i == 1)(stages)
-                dw[prev] += mm(base, BIG)
-            if do_pre:
-                pre(base, BTILE)
+            body(base, BTILE, True)
             return carry
         lax.fori_loop(0, NBIG, chunk, 0)
         if do_mm:
@@ -553,11 +583,12 @@
 
     @pl.when(j == 0)
     def _():
-        step(True, False)
-
-    @pl.when(jnp.logical_and(j > 0, j < NB))
-    def _():
-        step(True, True)
+        step(0, True, False)
+
+    for par in range(2):
+        @pl.when(jnp.logical_and(jnp.logical_and(j > 0, j < NB), lax.rem(j, 2) == par))
+        def _():
+            step(par, True, True)
 
     def logits_unit(i):
         rows = span(i, LB)
@@ -590,7 +621,7 @@
 
     @pl.when(j == NB)
     def _():
-        step(False, True)
+        step(0, False, True)
         pall_copy.start()
         wtb_copy.start()
 
@@ -634,7 +665,7 @@
                   pl.BlockSpec((IMG, CB), cur), whole(2, COUT), HBM, HBM, whole(2, 2, 2, 1, IMG), whole(1, CLASSES)],
         out_specs=[HBM, whole(2, COUT), whole(SUB, CB), HBM, whole(SUB, COUT), whole(SUB, KP), whole(SUB, KP)],
         out_shape=[struct(QUAD + (QR, COUT)), struct((2, COUT)), struct((SUB, CB)), struct((KP, COUT)), struct((SUB, COUT)), struct((SUB, KP)), struct((SUB, KP))],
-        scratch_shapes=[bvmem(CIN, ROWS), bvmem(2, ROWS, CB), fvmem(2, CIN, CB), fvmem(NB, HALF, CB), fvmem(*quad), fvmem(*quad),
+        scratch_shapes=[bvmem(CIN, ROWS), bvmem(ROWS, CB), bvmem(ROWS, CB), fvmem(2, CIN, CB), fvmem(NB, HALF, CB), fvmem(*quad), fvmem(*quad),
                         fvmem(NB, *pair), fvmem(NB, *pair), fvmem(2, *pair), fvmem(2, *pair), fvmem(*side), fvmem(*side),
                         fvmem(*QUAD, QR, COUT), fvmem(DEVS, 2, COUT), fvmem(1, KP),
                         dma(5, NB), dma(5, NB), dma(5, NB), dma(5, NB), dma(DEVS), dma(DEVS), dma(NB), dma(3), dma(2, NB)],

time: 212 us -> 199 us (0.939)
  Pallas kernels: 211 us -> 197 us
    pallas_call x1, Pallas kernels: 81.6 us -> 69.8 us  [forward(): pl.pallas_call(fwd_kernel, grid=(NB + 1 + TAIL,), in_specs=[HBM, pl.Block...]
where the time goes in v5:
time: 199 us
  Pallas kernels  197 us (99%)
    pallas_call x1, Pallas kernels, backward(): pl.pallas_call(bwd_kernel, grid=(NB + BTAIL,), in_specs=[HBM, pl.BlockSpe...  96.9 us
    pallas_call x1, Pallas kernels, forward(): pl.pallas_call(fwd_kernel, grid=(NB + 1 + TAIL,), in_specs=[HBM, pl.Block...  69.8 us
    pallas_call x1, Pallas kernels, update_all(): pl.pallas_call(update_kernel, grid=(NU + NF,), in_specs=[pl.BlockSpec(mem...  30.5 us

profile of v5, /device:TPU:1, one launch (start us, length us, event | category | flops | bytes accessed | tf_op | source)
XLA Modules:
  0.0 198.7 jit_solution(7258053521215570309)
XLA Ops:
  0.6 69.8 %fwd_conv.1 = (f32[8,6272,256]{2,1,0:T(8,128)}, bf16[1024,6272]{1,0:T(8,128)(2,1)}, bf16[1024,2048]{1,0:T(8,128)(2,1)}, s32[2,2,2,1,128]{4,3,2,1,0:T(1,128)}, f3...) custom-call(bf16[6272,1024]{1,0:T(8,128)(2,1)} %bitcast.43, ...), custom_call_target="tpu_custom_call" | custom-call | flops 26306674688 | bytes 102760448 | tf_op jit(solution)/shard_map/fwd_conv/pallas_call | solution.py:433
  70.5 96.9 %bwd_conv.1 = (f32[2,2,2,128,2048]{4,3,2,1,0:T(8,128)}, f32[2,2048]{1,0:T(2,128)}, f32[8,256]{1,0:T(8,128)}, f32[1024,2048]{1,0:T(8,128)}, f32[8,2048]{1,0:T(8,1...) custom-call(bf16[1024,6272]{1,0:T(8,128)(2,1)} %get-tuple-element.42.at_hbm, f32[8,6272,256]{2,1,0:T(8,128)} %get-tuple-element.43.z_ref, ...), custom_call_target="tpu_custom_call" | custom-call | flops 26306674688 | bytes 102760448 | tf_op jit(solution)/shard_map/bwd_conv/pallas_call | solution.py:661
  168.1 30.5 %update.1 = (f32[1024,2048]{1,0:T(8,128)}, f32[1024,2048]{1,0:T(8,128)}, f32[1000,2048]{1,0:T(8,128)}, f32[1000,2048]{1,0:T(8,128)}, f32[1,1000]{1,0:T(1,128)}, ...) custom-call(f32[1]{0:T(128)} %bitcast.26.lr_ref, ...), custom_call_target="tpu_custom_call" | custom-call | flops 33554432 | bytes 83886080 | tf_op jit(solution)/shard_map/update/pallas_call | solution.py:732

commit v6 on v5

--- a/solution.py
+++ b/solution.py
@@ -32,7 +32,10 @@
 PIECES = 8
 BPIECES = 4
 APAD = CIN + LANES
-TAIL = 3
+TAIL = 1
+NG = 6
+NP = NB - NG
+PG, PT = NG * CB, NP * CB
 BTAIL = 7
 QR = CIN // DEVS
 HALF = CIN // 2
@@ -149,15 +152,17 @@
     return gather_own(*a) + gather_on(*a) + gather_core(*a)
 
 
-def when_block(b, fn):
-    @pl.when(jnp.logical_and(b >= 0, b < NB))
-    def _():
-        fn(b)
-
-
-def stage_list(j, fns, lag=2):
+def stage_list(j, blocks, fns, lag=2):
     for k, fn in enumerate(fns):
-        when_block(j - lag - k, fn)
+        b = j - lag - k
+        pl.when(jnp.logical_and(b >= 0, b < blocks))(functools.partial(fn, b))
+
+
+def loop(lo, hi, fn):
+    def body(i, carry):
+        fn(i)
+        return carry
+    lax.fori_loop(lo, hi, body, 0)
 
 
 def pieces():
@@ -186,9 +191,9 @@
     bpad[:, :CLASSES] = bias_ref[:]
 
 
-def fwd_kernel(a_hbm, w_ref, s_ref, g_ref, b_ref, lab_ref, bias_ref, wt_hbm,
-               z_hbm, at_ref, pall_ref, lall_ref, wsq_ref, fsq_ref, wtb_hbm, da_ref, sc_ref, sh_ref, bb_ref, cc_ref, db_ref,
-               abf, z0, z1, wbf, stat, pfull, lfull, pool, cnt, sx, sv, wtb, bpad, asem, zsem, wsem, osem, gs, gr, ls, lr):
+def fwd_kernel(a_hbm, w_ref, s_ref, g_ref, b_ref, lab_ref, bias_ref, wt_ref,
+               z_hbm, at_ref, pall_ref, ptail_ref, lall_ref, wsq_ref, fsq_ref, wtb_hbm, da_ref, sc_ref, sh_ref, bb_ref, cc_ref, db_ref,
+               abf, z0, z1, wbf, stat, pfull, lfull, pool, cnt, sx, sv, wtb, bpad, asem, zsem, osem, gs, gr, ls, lr):
     j = pl.program_id(0)
     zs = (z0, z1)
     me, core, x, y = position()
@@ -200,12 +205,6 @@
 
     def z_copy(jj, par):
         return pltpu.make_async_copy(zs[par], z_hbm.at[jj], zsem.at[par])
-
-    def wt_view(b):
-        return zs[b // 6].at[pl.ds((b % 6) * CLASSES, CLASSES), :]
-
-    def wt_copy(b):
-        return pltpu.make_async_copy(wt_hbm.at[:, pl.ds(b * CB, CB)], wt_view(b), wsem.at[b])
 
     def wtb_copy():
         return pltpu.make_async_copy(wtb, wtb_hbm, osem)
@@ -223,6 +222,7 @@
         each(start, labels)
         lfull[core, y, x] = lab_ref[:]
         wsq_ref[:] = jnp.zeros_like(wsq_ref)
+        wtb[CLASSES:] = jnp.zeros((KP - CLASSES, COUT), BF16)
         set_bias(bpad, bias_ref)
 
     def second(b):
@@ -239,7 +239,7 @@
             pall_ref[span(q, IMG), :] = pfull[c, py, px, :, cols(b)].astype(BF16)
 
     def stages():
-        stage_list(j, (second, third, last))
+        stage_list(j, NG, (second, third, last))
 
     def step(par, do_mm, do_post):
         first = not do_post
@@ -249,6 +249,9 @@
         if do_mm:
             wf = w_ref[:]
             wsq_ref[:] += fold(wf * wf)
+            wtf = wt_ref[:]
+            fsq_ref[:, cols(j)] = fold(wtf * wtf)
+            wtb[:CLASSES, cols(j)] = wtf.astype(BF16)
             w = wf.astype(BF16)
             wbf[:] = w
             if first:
@@ -256,8 +259,7 @@
             m0 = rowsum(dot(abf[:IMG, :CIN], w)) * (1.0 / IMG)
             stat[:2 * SUB] = jnp.zeros((2 * SUB, CB), F32)
         if do_post and not do_mm:
-            for b in range(6):
-                wt_copy(b).start()
+            wtb_copy().start()
         if do_post:
             mean = stat[2 * SUB:2 * SUB + 1]
             inv = stat[3 * SUB:3 * SUB + 1]
@@ -326,7 +328,7 @@
             sv[SUB:SUB + 1, pc] = inv
             sc_ref[:, pc] = sc
             sh_ref[:, pc] = sh
-            each(start, gather_own(pfull, gs, gr, j - 1))
+            pl.when(j - 1 < NG)(lambda: each(start, gather_own(pfull, gs, gr, j - 1)))
         if do_mm:
             dm = rowsum(stat[:SUB]) * (1.0 / ROWS)
             q = rowsum(stat[SUB:2 * SUB]) * (1.0 / ROWS)
@@ -349,27 +351,9 @@
 
     @pl.when(j == NB + 1)
     def _():
-        z_copy(NB - 1, 1).wait()
-        for b in range(6, NB):
-            wt_copy(b).start()
         stages()
-        wtb[CLASSES:] = jnp.zeros((KP - CLASSES, COUT), BF16)
-        for b in range(NB):
-            wt_copy(b).wait()
-            view = wt_view(b)
-
-            def cast(i, acc):
-                w = view[span(i, 40), :]
-                wtb[span(i, 40), b * CB:(b + 1) * CB] = w.astype(BF16)
-                return acc + fold(w * w)
-            fsq_ref[:, b * CB:(b + 1) * CB] = lax.fori_loop(0, CLASSES // 40, cast, jnp.zeros((SUB, CB), F32))
-        wtb_copy().start()
-
-    @pl.when(j == NB + 2)
-    def _():
-        stages()
-        own = pfull[core, y, x].astype(BF16)
-        lg = dot_t(own, wtb[:])
+        ptail_ref[:] = pfull[core, y, x, :, PG:]
+        lg = dot_t(pfull[core, y, x].astype(BF16), wtb[:])
         _, dl = softmax_terms(lg, bpad[:], label_rows(lab_ref[:]))
         dlb = dl.astype(BF16)
 
@@ -388,17 +372,11 @@
             return carry
         lax.fori_loop(0, NB, col, 0)
 
-    @pl.when(j == NB + TAIL)
-    def _():
-        stages()
         each(wait, labels)
         lall_ref[:] = lfull[:]
         wtb_copy().wait()
-
-        def drain(b, carry):
-            each(wait_send, gather_all(pfull, gs, gr, b))
-            return carry
-        lax.fori_loop(0, NB, drain, 0)
+        z_copy(NB - 1, 1).wait()
+        loop(0, NG, lambda b: each(wait_send, gather_all(pfull, gs, gr, b)))
 
 
 def whole(*shape):
@@ -428,29 +406,29 @@
 def forward(a, w, s, gamma, beta, labels, bias, wt):
     prev = lambda j: (0, jnp.clip(j - 1, 0, NB - 1))
     cur = lambda j: (0, jnp.minimum(j, NB - 1))
-    late = lambda j: (0, jnp.clip(j - 4, 0, NB - 1))
+    late = lambda j: (0, jnp.clip(j - 4, 0, NG - 1))
     vec, lab = (1, COUT), QUAD + (1, IMG)
     return pl.pallas_call(
         fwd_kernel,
         grid=(NB + 1 + TAIL,),
         in_specs=[HBM, pl.BlockSpec((CIN, CB), cur), pl.BlockSpec((ROWS, CB), prev), pl.BlockSpec((1, CB), prev), pl.BlockSpec((1, CB), prev),
-                  whole(1, IMG), whole(1, CLASSES), HBM],
-        out_specs=[HBM, pl.BlockSpec((IMG, ROWS), lambda j: (jnp.minimum(j, NB - 1), 0)), pl.BlockSpec((TOTAL, CB), late), whole(*lab),
+                  whole(1, IMG), whole(1, CLASSES), pl.BlockSpec((CLASSES, CB), cur)],
+        out_specs=[HBM, pl.BlockSpec((IMG, ROWS), lambda j: (jnp.minimum(j, NB - 1), 0)), pl.BlockSpec((TOTAL, CB), late), whole(IMG, PT), whole(*lab),
                    whole(SUB, CB), whole(SUB, COUT), HBM, whole(IMG, COUT)] + [whole(*vec)] * 4 + [whole(2, COUT)],
-        out_shape=[struct((NB, ROWS, CB)), struct((CIN, ROWS), BF16), struct((TOTAL, COUT), BF16), struct(lab, jnp.int32),
+        out_shape=[struct((NB, ROWS, CB)), struct((CIN, ROWS), BF16), struct((TOTAL, PG), BF16), struct((IMG, PT)), struct(lab, jnp.int32),
                    struct((SUB, CB)), struct((SUB, COUT)), struct((KP, COUT), BF16), struct((IMG, COUT))] + [struct(vec)] * 4 + [struct((2, COUT))],
         scratch_shapes=[bvmem(ROWS, APAD), fvmem(ROWS, CB), fvmem(ROWS, CB), bvmem(CIN, CB), fvmem(4 * SUB, CB), fvmem(*QUAD, IMG, COUT), pltpu.VMEM(lab, jnp.int32),
                         fvmem(IMG, CB), fvmem(IMG, COUT), fvmem(IMG, COUT), fvmem(2 * SUB, COUT), bvmem(KP, COUT), fvmem(1, KP),
-                        dma(NCH), dma(2), dma(NB), pltpu.SemaphoreType.DMA, dma(5, NB), dma(5, NB), dma(DEVS), dma(DEVS)],
+                        dma(NCH), dma(2), pltpu.SemaphoreType.DMA, dma(5, NG), dma(5, NG), dma(DEVS), dma(DEVS)],
         compiler_params=pltpu.CompilerParams(vmem_limit_bytes=63 * MIB, collective_id=0, has_side_effects=True),
         cost_estimate=pl.CostEstimate(flops=2 * ROWS * CIN * COUT, bytes_accessed=2 * ROWS * COUT * 4, transcendentals=0),
         name="fwd_conv",
     )(a, w, s, gamma, beta, labels, bias, wt)
 
 
-def bwd_kernel(at_hbm, z_ref, s_ref, sc_ref, sh_ref, bb_ref, cc_ref, da_ref, db_ref, pall_hbm, wtb_hbm, lab_ref, bias_ref,
+def bwd_kernel(at_hbm, z_ref, s_ref, sc_ref, sh_ref, bb_ref, cc_ref, da_ref, db_ref, pall_hbm, ptail_hbm, wtb_hbm, lab_ref, bias_ref,
                g_hbm, dbo_ref, gsq_ref, gfc_hbm, fsq_ref, gb_ref, loss_ref,
-               atv, dz0, dz1, dw, rd, ha, hb, ra, rb, ka, kb, r2a, r2b, gfull, dball, bpad, ss, rs, gs, gr, bs, br, osem, isem, fsem):
+               atv, dz0, dz1, dw, rd, ha, hb, ra, rb, ka, kb, r2a, r2b, gfull, dball, ptail, bpad, ps, pr, ss, rs, gs, gr, bs, br, osem, isem, fsem):
     j = pl.program_id(0)
     dzs = (dz0, dz1)
     me, core, x, y = position()
@@ -460,14 +438,19 @@
     dlt = atv.at[:, pl.ds(2 * COUT, TOTAL)]
 
     at_copy = pltpu.make_async_copy(at_hbm, atv, isem.at[0])
-    pall_copy = pltpu.make_async_copy(pall_hbm, pall, isem.at[1])
+    pall_copy = pltpu.make_async_copy(pall_hbm, atv.at[:, pl.ds(0, PG)], isem.at[1])
     wtb_copy = pltpu.make_async_copy(wtb_hbm, wtb, isem.at[2])
+    ptail_copy = pltpu.make_async_copy(ptail_hbm, ptail.at[core, y, x], isem.at[3])
     db_copies = [rcopy(db_ref, dball.at[me], bs.at[k], br.at[k], lax.rem(me + k, DEVS)) for k in range(1, DEVS)]
 
     @pl.when(j == 0)
     def _():
+        ptail_copy.start()
         at_copy.start()
         enter_all()
+        ptail_copy.wait()
+        for b in range(NP):
+            each(start, gather_own(ptail, ps, pr, b))
         each(start, db_copies)
         dball[me] = db_ref[:]
         for r in (gsq_ref, fsq_ref, gb_ref, loss_ref):
@@ -518,7 +501,6 @@
         each(wait, second_copies(b))
         gfull[core, y, x, :, cols(b, HC)] = ka[sl, y] + r2a[b]
         gfull[core, y, x, :, cols(b, HC, HC)] = kb[sl, x] + r2b[b]
-        each(start, gather_own(gfull, gs, gr, b))
 
     def stage4(b):
         each(wait_recv, gather_own(gfull, gs, gr, b))
@@ -537,8 +519,20 @@
             acc = acc + fold(gv * gv)
         gsq_ref[:] = acc
 
+    def pooled_on():
+        for b in range(NP):
+            each(wait_recv, gather_own(ptail, ps, pr, b))
+            each(start, gather_on(ptail, ps, pr, b))
+
+    def pooled_core():
+        for b in range(NP):
+            each(wait_recv, gather_on(ptail, ps, pr, b))
+            each(start, gather_core(ptail, ps, pr, b))
+
     def stages():
-        stage_list(j, (stage1, stage2, stage3, stage4, stage5, stage6))
+        stage_list(j, NB, (stage1, stage2, stage3))
+        pl.when(j == 1)(pooled_on)
+        pl.when(j == 2)(pooled_core)
 
     def step(par, do_pre, do_mm):
         slot, prev = dzs[par], dzs[1 - par]
@@ -613,12 +607,6 @@
         fsq_ref[:, cols(c)] = acc
         each(start, fc_copies(c))
 
-    def loop(lo, hi, fn):
-        def body(i, carry):
-            fn(i)
-            return carry
-        lax.fori_loop(lo, hi, body, 0)
-
     @pl.when(j == NB)
     def _():
         step(0, False, True)
@@ -629,9 +617,18 @@
     def _():
         stages()
         k = j - NB - 1
+        third = lambda n: jnp.clip(3 * n, 0, NB)
+        loop(jnp.where(k == 0, 0, jnp.minimum(k + NB - 3, NB)), jnp.minimum(k + NB - 2, NB), lambda b: each(start, gather_own(gfull, gs, gr, b)))
+        loop(third(k - 1), third(k), stage4)
+        loop(third(k - 2), third(k - 1), stage5)
+        loop(third(k - 3), third(k - 2), stage6)
 
         @pl.when(k == 0)
         def _():
+            for b in range(NP):
+                each(wait_recv, gather_core(ptail, ps, pr, b))
+            for q, (c, py, px) in enumerate(pieces()):
+                atv[span(q, IMG), PG:COUT] = ptail[c, py, px].astype(BF16)
             pall_copy.wait()
             wtb_copy.wait()
 
@@ -652,9 +649,10 @@
             each(wait_send, gather_all(gfull, gs, gr, b))
             out_copy(b).wait()
         loop(0, NB, drain)
-
-
-def backward(at, z, s, sc, sh, bb, cc, da, dgb, pall, wtb, lab, bias):
+        loop(0, NP, lambda b: each(wait_send, gather_all(ptail, ps, pr, b)))
+
+
+def backward(*args):
     cur = lambda j: (0, jnp.minimum(j, NB - 1))
     row = pl.BlockSpec((1, CB), cur)
     pair, quad, side = (2, QR, HC), (2, 2, 2, QR, HC), (NB, QR, HC)
@@ -662,17 +660,17 @@
         bwd_kernel,
         grid=(NB + BTAIL,),
         in_specs=[HBM, pl.BlockSpec((None, ROWS, CB), lambda j: (jnp.minimum(j, NB - 1), 0, 0)), pl.BlockSpec((ROWS, CB), cur), row, row, row, row,
-                  pl.BlockSpec((IMG, CB), cur), whole(2, COUT), HBM, HBM, whole(2, 2, 2, 1, IMG), whole(1, CLASSES)],
+                  pl.BlockSpec((IMG, CB), cur), whole(2, COUT), HBM, HBM, HBM, whole(2, 2, 2, 1, IMG), whole(1, CLASSES)],
         out_specs=[HBM, whole(2, COUT), whole(SUB, CB), HBM, whole(SUB, COUT), whole(SUB, KP), whole(SUB, KP)],
         out_shape=[struct(QUAD + (QR, COUT)), struct((2, COUT)), struct((SUB, CB)), struct((KP, COUT)), struct((SUB, COUT)), struct((SUB, KP)), struct((SUB, KP))],
         scratch_shapes=[bvmem(CIN, ROWS), bvmem(ROWS, CB), bvmem(ROWS, CB), fvmem(2, CIN, CB), fvmem(NB, HALF, CB), fvmem(*quad), fvmem(*quad),
                         fvmem(NB, *pair), fvmem(NB, *pair), fvmem(2, *pair), fvmem(2, *pair), fvmem(*side), fvmem(*side),
-                        fvmem(*QUAD, QR, COUT), fvmem(DEVS, 2, COUT), fvmem(1, KP),
-                        dma(5, NB), dma(5, NB), dma(5, NB), dma(5, NB), dma(DEVS), dma(DEVS), dma(NB), dma(3), dma(2, NB)],
+                        fvmem(*QUAD, QR, COUT), fvmem(DEVS, 2, COUT), fvmem(*QUAD, IMG, PT), fvmem(1, KP),
+                        dma(5, NP), dma(5, NP), dma(5, NB), dma(5, NB), dma(5, NB), dma(5, NB), dma(DEVS), dma(DEVS), dma(NB), dma(4), dma(2, NB)],
         compiler_params=pltpu.CompilerParams(vmem_limit_bytes=63 * MIB, collective_id=1, has_side_effects=True),
         cost_estimate=pl.CostEstimate(flops=2 * ROWS * CIN * COUT, bytes_accessed=2 * ROWS * COUT * 4, transcendentals=0),
         name="bwd_conv",
-    )(at, z, s, sc, sh, bb, cc, da, dgb, pall, wtb, lab, bias)
+    )(*args)
 
 
 def trust_of(wsq, gsq):
@@ -748,8 +746,8 @@
         s = shortcut.transpose(1, 2, 0, 3).reshape(ROWS, COUT)
         wt = w_fc.T
         bias = fc_bias[None]
-        z, at, pall, lab, wsq, tsq, wtb, da, sc, sh, bb, cc, dgb = forward(a, w_conv, s, gamma[None], beta[None], labels[None], bias, wt)
-        g8, dgb, gsq, gfc, fsq, gb, ls = backward(at, z, s, sc, sh, bb, cc, da, dgb, pall, wtb, lab, bias)
+        z, at, pall, ptail, lab, wsq, tsq, wtb, da, sc, sh, bb, cc, dgb = forward(a, w_conv, s, gamma[None], beta[None], labels[None], bias, wt)
+        g8, dgb, gsq, gfc, fsq, gb, ls = backward(at, z, s, sc, sh, bb, cc, da, dgb, pall, ptail, wtb, lab, bias)
         wo, vo, wto, vto, bo, vbo, go, vgo, beo, vbeo, loss = update_all(
             lr.reshape(1), w_conv, vel_conv, g8.reshape(CIN, COUT), wsq, gsq, wt, vel_fc.T, gfc, tsq, fsq, bias, vel_bias[None], gb, ls,
             gamma[None], beta[None], vel_gamma[None], vel_beta[None], dgb)

time: 199 us -> 200 us (level)
    pallas_call x1, Pallas kernels: 96.9 us -> 104 us  [backward(): pl.pallas_call(bwd_kernel, grid=(NB + BTAIL,), in_specs=[HBM, pl.BlockSpe...]
    pallas_call x1, Pallas kernels: 69.8 us -> 64.1 us  [forward(): pl.pallas_call(fwd_kernel, grid=(NB + 1 + TAIL,), in_specs=[HBM, pl.Block...]
where the time goes in v6:
time: 200 us
  Pallas kernels  198 us (99%)
    pallas_call x1, Pallas kernels, backward(): pl.pallas_call(bwd_kernel, grid=(NB + BTAIL,), in_specs=[HBM, pl.BlockSpe...  104 us
    pallas_call x1, Pallas kernels, forward(): pl.pallas_call(fwd_kernel, grid=(NB + 1 + TAIL,), in_specs=[HBM, pl.Block...  64.1 us
    pallas_call x1, Pallas kernels, update_all(): pl.pallas_call(update_kernel, grid=(NU + NF,), in_specs=[pl.BlockSpec(mem...  30.5 us

profile of v6, /device:TPU:1, one launch (start us, length us, event | category | flops | bytes accessed | tf_op | source)
XLA Modules:
  0.0 199.7 jit_solution(13719355102302375221)
XLA Ops:
  0.6 64.1 %fwd_conv.1 = (f32[8,6272,256]{2,1,0:T(8,128)}, bf16[1024,6272]{1,0:T(8,128)(2,1)}, bf16[1024,1536]{1,0:T(8,128)(2,1)}, f32[128,512]{1,0:T(8,128)}, s32[2,2,2,1,...) custom-call(bf16[6272,1024]{1,0:T(8,128)(2,1)} %bitcast.43, ...), custom_call_target="tpu_custom_call" | custom-call | flops 26306674688 | bytes 102760448 | tf_op jit(solution)/shard_map/fwd_conv/pallas_call | solution.py:411
  64.8 103.6 %bwd_conv.1 = (f32[2,2,2,128,2048]{4,3,2,1,0:T(8,128)}, f32[2,2048]{1,0:T(2,128)}, f32[8,256]{1,0:T(8,128)}, f32[1024,2048]{1,0:T(8,128)}, f32[8,2048]{1,0:T(8,1...) custom-call(bf16[1024,6272]{1,0:T(8,128)(2,1)} %get-tuple-element.43.at_hbm, f32[8,6272,256]{2,1,0:T(8,128)} %get-tuple-element.44.z_ref, ...), custom_call_target="tpu_custom_call" | custom-call | flops 26306674688 | bytes 102760448 | tf_op jit(solution)/shard_map/bwd_conv/pallas_call | solution.py:659
  169.1 30.5 %update.1 = (f32[1024,2048]{1,0:T(8,128)}, f32[1024,2048]{1,0:T(8,128)}, f32[1000,2048]{1,0:T(8,128)}, f32[1000,2048]{1,0:T(8,128)}, f32[1,1000]{1,0:T(1,128)}, ...) custom-call(f32[1]{0:T(128)} %bitcast.26.lr_ref, ...), custom_call_target="tpu_custom_call" | custom-call | flops 33554432 | bytes 83886080 | tf_op jit(solution)/shard_map/update/pallas_call | solution.py:730

commit v7 on v6

--- a/solution.py
+++ b/solution.py
@@ -501,6 +501,7 @@
         each(wait, second_copies(b))
         gfull[core, y, x, :, cols(b, HC)] = ka[sl, y] + r2a[b]
         gfull[core, y, x, :, cols(b, HC, HC)] = kb[sl, x] + r2b[b]
+        each(start, gather_own(gfull, gs, gr, b))
 
     def stage4(b):
         each(wait_recv, gather_own(gfull, gs, gr, b))
@@ -530,7 +531,7 @@
             each(start, gather_core(ptail, ps, pr, b))
 
     def stages():
-        stage_list(j, NB, (stage1, stage2, stage3))
+        stage_list(j, NB, (stage1, stage2, stage3, stage4, stage5, stage6))
         pl.when(j == 1)(pooled_on)
         pl.when(j == 2)(pooled_core)
 
@@ -617,11 +618,6 @@
     def _():
         stages()
         k = j - NB - 1
-        third = lambda n: jnp.clip(3 * n, 0, NB)
-        loop(jnp.where(k == 0, 0, jnp.minimum(k + NB - 3, NB)), jnp.minimum(k + NB - 2, NB), lambda b: each(start, gather_own(gfull, gs, gr, b)))
-        loop(third(k - 1), third(k), stage4)
-        loop(third(k - 2), third(k - 1), stage5)
-        loop(third(k - 3), third(k - 2), stage6)
 
         @pl.when(k == 0)
         def _():

time: 200 us -> 195 us (0.975)
  Pallas kernels: 198 us -> 193 us
    pallas_call x1, Pallas kernels: 104 us -> 98.7 us  [backward(): pl.pallas_call(bwd_kernel, grid=(NB + BTAIL,), in_specs=[HBM, pl.BlockSpe...]
where the time goes in v7:
time: 195 us
  Pallas kernels  193 us (99%)
    pallas_call x1, Pallas kernels, backward(): pl.pallas_call(bwd_kernel, grid=(NB + BTAIL,), in_specs=[HBM, pl.BlockSpe...  98.7 us
    pallas_call x1, Pallas kernels, forward(): pl.pallas_call(fwd_kernel, grid=(NB + 1 + TAIL,), in_specs=[HBM, pl.Block...  64.1 us
    pallas_call x1, Pallas kernels, update_all(): pl.pallas_call(update_kernel, grid=(NU + NF,), in_specs=[pl.BlockSpec(mem...  30.5 us

profile of v7, /device:TPU:1, one launch (start us, length us, event | category | flops | bytes accessed | tf_op | source)
XLA Modules:
  0.0 194.7 jit_solution(14412171716772406084)
XLA Ops:
  0.6 64.1 %fwd_conv.1 = (f32[8,6272,256]{2,1,0:T(8,128)}, bf16[1024,6272]{1,0:T(8,128)(2,1)}, bf16[1024,1536]{1,0:T(8,128)(2,1)}, f32[128,512]{1,0:T(8,128)}, s32[2,2,2,1,...) custom-call(bf16[6272,1024]{1,0:T(8,128)(2,1)} %bitcast.43, ...), custom_call_target="tpu_custom_call" | custom-call | flops 26306674688 | bytes 102760448 | tf_op jit(solution)/shard_map/fwd_conv/pallas_call | solution.py:411
  64.8 98.7 %bwd_conv.1 = (f32[2,2,2,128,2048]{4,3,2,1,0:T(8,128)}, f32[2,2048]{1,0:T(2,128)}, f32[8,256]{1,0:T(8,128)}, f32[1024,2048]{1,0:T(8,128)}, f32[8,2048]{1,0:T(8,1...) custom-call(bf16[1024,6272]{1,0:T(8,128)(2,1)} %get-tuple-element.43.at_hbm, f32[8,6272,256]{2,1,0:T(8,128)} %get-tuple-element.44.z_ref, ...), custom_call_target="tpu_custom_call" | custom-call | flops 26306674688 | bytes 102760448 | tf_op jit(solution)/shard_map/bwd_conv/pallas_call | solution.py:655
  164.1 30.5 %update.1 = (f32[1024,2048]{1,0:T(8,128)}, f32[1024,2048]{1,0:T(8,128)}, f32[1000,2048]{1,0:T(8,128)}, f32[1000,2048]{1,0:T(8,128)}, f32[1,1000]{1,0:T(1,128)}, ...) custom-call(f32[1]{0:T(128)} %bitcast.26.lr_ref, ...), custom_call_target="tpu_custom_call" | custom-call | flops 33554432 | bytes 83886080 | tf_op jit(solution)/shard_map/update/pallas_call | solution.py:726

commit v8 on v7

--- a/solution.py
+++ b/solution.py
@@ -36,7 +36,8 @@
 NG = 6
 NP = NB - NG
 PG, PT = NG * CB, NP * CB
-BTAIL = 7
+LAGS = (2, 3, 4, 6, 8, 9)
+BTAIL = LAGS[-1]
 QR = CIN // DEVS
 HALF = CIN // 2
 BIG = 1792
@@ -152,9 +153,9 @@
     return gather_own(*a) + gather_on(*a) + gather_core(*a)
 
 
-def stage_list(j, blocks, fns, lag=2):
-    for k, fn in enumerate(fns):
-        b = j - lag - k
+def stage_list(j, blocks, fns, lags):
+    for fn, lag in zip(fns, lags):
+        b = j - lag
         pl.when(jnp.logical_and(b >= 0, b < blocks))(functools.partial(fn, b))
 
 
@@ -239,7 +240,7 @@
             pall_ref[span(q, IMG), :] = pfull[c, py, px, :, cols(b)].astype(BF16)
 
     def stages():
-        stage_list(j, NG, (second, third, last))
+        stage_list(j, NG, (second, third, last), (2, 3, 4))
 
     def step(par, do_mm, do_post):
         first = not do_post
@@ -531,7 +532,7 @@
             each(start, gather_core(ptail, ps, pr, b))
 
     def stages():
-        stage_list(j, NB, (stage1, stage2, stage3, stage4, stage5, stage6))
+        stage_list(j, NB, (stage1, stage2, stage3, stage4, stage5, stage6), LAGS)
         pl.when(j == 1)(pooled_on)
         pl.when(j == 2)(pooled_core)
 

time: 195 us -> 194 us (level)
  no operation moved by 1% of the time
where the time goes in v8:
time: 194 us
  Pallas kernels  193 us (99%)
    pallas_call x1, Pallas kernels, backward(): pl.pallas_call(bwd_kernel, grid=(NB + BTAIL,), in_specs=[HBM, pl.BlockSpe...  98.2 us
    pallas_call x1, Pallas kernels, forward(): pl.pallas_call(fwd_kernel, grid=(NB + 1 + TAIL,), in_specs=[HBM, pl.Block...  64.1 us
    pallas_call x1, Pallas kernels, update_all(): pl.pallas_call(update_kernel, grid=(NU + NF,), in_specs=[pl.BlockSpec(mem...  30.5 us

profile of v8, /device:TPU:1, one launch (start us, length us, event | category | flops | bytes accessed | tf_op | source)
XLA Modules:
  0.0 194.3 jit_solution(12898202308056519541)
XLA Ops:
  0.6 64.1 %fwd_conv.1 = (f32[8,6272,256]{2,1,0:T(8,128)}, bf16[1024,6272]{1,0:T(8,128)(2,1)}, bf16[1024,1536]{1,0:T(8,128)(2,1)}, f32[128,512]{1,0:T(8,128)}, s32[2,2,2,1,...) custom-call(bf16[6272,1024]{1,0:T(8,128)(2,1)} %bitcast.43, ...), custom_call_target="tpu_custom_call" | custom-call | flops 26306674688 | bytes 102760448 | tf_op jit(solution)/shard_map/fwd_conv/pallas_call | solution.py:412
  64.8 98.2 %bwd_conv.1 = (f32[2,2,2,128,2048]{4,3,2,1,0:T(8,128)}, f32[2,2048]{1,0:T(2,128)}, f32[8,256]{1,0:T(8,128)}, f32[1024,2048]{1,0:T(8,128)}, f32[8,2048]{1,0:T(8,1...) custom-call(bf16[1024,6272]{1,0:T(8,128)(2,1)} %get-tuple-element.43.at_hbm, f32[8,6272,256]{2,1,0:T(8,128)} %get-tuple-element.44.z_ref, ...), custom_call_target="tpu_custom_call" | custom-call | flops 26306674688 | bytes 102760448 | tf_op jit(solution)/shard_map/bwd_conv/pallas_call | solution.py:656
  163.7 30.5 %update.1 = (f32[1024,2048]{1,0:T(8,128)}, f32[1024,2048]{1,0:T(8,128)}, f32[1000,2048]{1,0:T(8,128)}, f32[1000,2048]{1,0:T(8,128)}, f32[1,1000]{1,0:T(1,128)}, ...) custom-call(f32[1]{0:T(128)} %bitcast.26.lr_ref, ...), custom_call_target="tpu_custom_call" | custom-call | flops 33554432 | bytes 83886080 | tf_op jit(solution)/shard_map/update/pallas_call | solution.py:727

commit v9 on v8

--- a/solution.py
+++ b/solution.py
@@ -43,8 +43,8 @@
 BIG = 1792
 BTILE = BIG // IMG
 NBIG = ROWS // BIG
-UB = 128
-FB = 208
+UB = 64
+FB = 112
 NU = CIN // UB
 NF = pl.cdiv(CLASSES, FB)
 LB = 256
@@ -313,7 +313,6 @@
             return carry
 
         def chunk2(i, carry):
-            pl.when(i == 2)(stages)
             region(pl.multiple_of(i * 2 * crow, 2 * crow), 2 * CH, PIECES)
             return carry
 
@@ -321,6 +320,7 @@
             lax.fori_loop(0, NCH, chunk, 0)
         else:
             lax.fori_loop(0, NCH // 2, chunk2, 0)
+            stages()
             region(pl.multiple_of((jnp.minimum(me, 0) + NCH - 1) * crow, crow), CH, 4)
         if do_post:
             pfull[core, y, x, :, pc] = pool[:] * (1.0 / POS)
@@ -534,7 +534,7 @@
     def stages():
         stage_list(j, NB, (stage1, stage2, stage3, stage4, stage5, stage6), LAGS)
         pl.when(j == 1)(pooled_on)
-        pl.when(j == 2)(pooled_core)
+        pl.when(j == 3)(pooled_core)
 
     def step(par, do_pre, do_mm):
         slot, prev = dzs[par], dzs[1 - par]

time: 194 us -> 200 us (1.031)
  Pallas kernels: 193 us -> 198 us
    pallas_call x1, Pallas kernels: 30.5 us -> 36.4 us  [update_all(): pl.pallas_call(update_kernel, grid=(NU + NF,), in_specs=[pl.BlockSpec(mem...]
    pallas_call x1, Pallas kernels: 98.2 us -> 95.6 us  [backward(): pl.pallas_call(bwd_kernel, grid=(NB + BTAIL,), in_specs=[HBM, pl.BlockSpe...]
where the time goes in v9:
time: 200 us; the launch traced here: 199 us
  Pallas kernels  198 us (99%)
    pallas_call x1, Pallas kernels, backward(): pl.pallas_call(bwd_kernel, grid=(NB + BTAIL,), in_specs=[HBM, pl.BlockSpe...  95.6 us
    pallas_call x1, Pallas kernels, forward(): pl.pallas_call(fwd_kernel, grid=(NB + 1 + TAIL,), in_specs=[HBM, pl.Block...  65.6 us
    pallas_call x1, Pallas kernels, update_all(): pl.pallas_call(update_kernel, grid=(NU + NF,), in_specs=[pl.BlockSpec(mem...  36.4 us

profile of v9, /device:TPU:1, one launch (start us, length us, event | category | flops | bytes accessed | tf_op | source)
XLA Modules:
  0.0 199.0 jit_solution(11138277439081713562)
XLA Ops:
  0.6 65.6 %fwd_conv.1 = (f32[8,6272,256]{2,1,0:T(8,128)}, bf16[1024,6272]{1,0:T(8,128)(2,1)}, bf16[1024,1536]{1,0:T(8,128)(2,1)}, f32[128,512]{1,0:T(8,128)}, s32[2,2,2,1,...) custom-call(bf16[6272,1024]{1,0:T(8,128)(2,1)} %bitcast.43, ...), custom_call_target="tpu_custom_call" | custom-call | flops 26306674688 | bytes 102760448 | tf_op jit(solution)/shard_map/fwd_conv/pallas_call | solution.py:412
  66.2 95.6 %bwd_conv.1 = (f32[2,2,2,128,2048]{4,3,2,1,0:T(8,128)}, f32[2,2048]{1,0:T(2,128)}, f32[8,256]{1,0:T(8,128)}, f32[1024,2048]{1,0:T(8,128)}, f32[8,2048]{1,0:T(8,1...) custom-call(bf16[1024,6272]{1,0:T(8,128)(2,1)} %get-tuple-element.43.at_hbm, f32[8,6272,256]{2,1,0:T(8,128)} %get-tuple-element.44.z_ref, ...), custom_call_target="tpu_custom_call" | custom-call | flops 26306674688 | bytes 102760448 | tf_op jit(solution)/shard_map/bwd_conv/pallas_call | solution.py:656
  162.4 36.4 %update.1 = (f32[1024,2048]{1,0:T(8,128)}, f32[1024,2048]{1,0:T(8,128)}, f32[1000,2048]{1,0:T(8,128)}, f32[1000,2048]{1,0:T(8,128)}, f32[1,1000]{1,0:T(1,128)}, ...) custom-call(f32[1]{0:T(128)} %bitcast.26.lr_ref, ...), custom_call_target="tpu_custom_call" | custom-call | flops 33554432 | bytes 83886080 | tf_op jit(solution)/shard_map/update/pallas_call | solution.py:727

commit v10 on v9

--- a/solution.py
+++ b/solution.py
@@ -43,10 +43,8 @@
 BIG = 1792
 BTILE = BIG // IMG
 NBIG = ROWS // BIG
-UB = 64
-FB = 112
+UB = 256
 NU = CIN // UB
-NF = pl.cdiv(CLASSES, FB)
 LB = 256
 MIB = 1024 * 1024
 F32 = jnp.float32
@@ -313,6 +311,7 @@
             return carry
 
         def chunk2(i, carry):
+            pl.when(i == 2)(stages)
             region(pl.multiple_of(i * 2 * crow, 2 * crow), 2 * CH, PIECES)
             return carry
 
@@ -320,7 +319,6 @@
             lax.fori_loop(0, NCH, chunk, 0)
         else:
             lax.fori_loop(0, NCH // 2, chunk2, 0)
-            stages()
             region(pl.multiple_of((jnp.minimum(me, 0) + NCH - 1) * crow, crow), CH, 4)
         if do_post:
             pfull[core, y, x, :, pc] = pool[:] * (1.0 / POS)
@@ -709,24 +707,18 @@
             return carry
         lax.fori_loop(0, rows // (2 * SUB), row, 0)
 
-    @pl.when(j < NU)
-    def _():
-        lars(w_ref, v_ref, g_ref, wsq_ref, gsq_ref, wo_ref, vo_ref, UB)
-
-    @pl.when(j >= NU)
-    def _():
-        lars(wt_ref, vt_ref, gt_ref, tsq_ref, fsq_ref, wto_ref, vto_ref, FB)
+    lars(w_ref, v_ref, g_ref, wsq_ref, gsq_ref, wo_ref, vo_ref, UB)
+    lars(wt_ref, vt_ref, gt_ref, tsq_ref, fsq_ref, wto_ref, vto_ref, UB)
 
 
 def update_all(*args):
-    conv = pl.BlockSpec((UB, COUT), lambda j: (jnp.minimum(j, NU - 1), 0))
-    fc = pl.BlockSpec((FB, COUT), lambda j: (jnp.clip(j - NU, 0, NF - 1), 0))
+    conv = fc = pl.BlockSpec((UB, COUT), lambda j: (j, 0))
     vec, bvec, one = (1, COUT), (1, CLASSES), (1, 1)
     vs, bs = whole(*vec), whole(*bvec)
     big, fcs = struct((CIN, COUT)), struct((CLASSES, COUT))
     return pl.pallas_call(
         update_kernel,
-        grid=(NU + NF,),
+        grid=(NU,),
         in_specs=[pl.BlockSpec(memory_space=pltpu.SMEM), conv, conv, conv, whole(SUB, CB), whole(SUB, CB), fc, fc, fc, whole(SUB, COUT), whole(SUB, COUT),
                   bs, bs, whole(SUB, KP), whole(SUB, KP), vs, vs, vs, vs, whole(2, COUT)],
         out_specs=[conv, conv, fc, fc, bs, bs, vs, vs, vs, vs, whole(*one)],

time: 200 us -> 190 us (0.950)
  Pallas kernels: 198 us -> 188 us
    pallas_call x1, Pallas kernels: 36.4 us -> 28.1 us  [update_all(): pl.pallas_call(update_kernel, grid=(NU,), in_specs=[pl.BlockSpec(memory_s...]
where the time goes in v10:
time: 190 us
  Pallas kernels  188 us (99%)
    pallas_call x1, Pallas kernels, backward(): pl.pallas_call(bwd_kernel, grid=(NB + BTAIL,), in_specs=[HBM, pl.BlockSpe...  96 us
    pallas_call x1, Pallas kernels, forward(): pl.pallas_call(fwd_kernel, grid=(NB + 1 + TAIL,), in_specs=[HBM, pl.Block...  64.1 us
    pallas_call x1, Pallas kernels, update_all(): pl.pallas_call(update_kernel, grid=(NU,), in_specs=[pl.BlockSpec(memory_s...  28.1 us

profile of v10, /device:TPU:1, one launch (start us, length us, event | category | flops | bytes accessed | tf_op | source)
XLA Modules:
  0.0 189.7 jit_solution(15904488631701998899)
XLA Ops:
  0.6 64.1 %fwd_conv.1 = (f32[8,6272,256]{2,1,0:T(8,128)}, bf16[1024,6272]{1,0:T(8,128)(2,1)}, bf16[1024,1536]{1,0:T(8,128)(2,1)}, f32[128,512]{1,0:T(8,128)}, s32[2,2,2,1,...) custom-call(bf16[6272,1024]{1,0:T(8,128)(2,1)} %bitcast.43, ...), custom_call_target="tpu_custom_call" | custom-call | flops 26306674688 | bytes 102760448 | tf_op jit(solution)/shard_map/fwd_conv/pallas_call | solution.py:410
  64.8 96.0 %bwd_conv.1 = (f32[2,2,2,128,2048]{4,3,2,1,0:T(8,128)}, f32[2,2048]{1,0:T(2,128)}, f32[8,256]{1,0:T(8,128)}, f32[1024,2048]{1,0:T(8,128)}, f32[8,2048]{1,0:T(8,1...) custom-call(bf16[1024,6272]{1,0:T(8,128)(2,1)} %get-tuple-element.43.at_hbm, f32[8,6272,256]{2,1,0:T(8,128)} %get-tuple-element.44.z_ref, ...), custom_call_target="tpu_custom_call" | custom-call | flops 26306674688 | bytes 102760448 | tf_op jit(solution)/shard_map/bwd_conv/pallas_call | solution.py:654
  161.5 28.1 %update.1 = (f32[1024,2048]{1,0:T(8,128)}, f32[1024,2048]{1,0:T(8,128)}, f32[1000,2048]{1,0:T(8,128)}, f32[1000,2048]{1,0:T(8,128)}, f32[1,1000]{1,0:T(1,128)}, ...) custom-call(f32[1]{0:T(128)} %bitcast.26.lr_ref, ...), custom_call_target="tpu_custom_call" | custom-call | flops 33554432 | bytes 83886080 | tf_op jit(solution)/shard_map/update/pallas_call | solution.py:719

commit v11 on v10

--- a/solution.py
+++ b/solution.py
@@ -427,7 +427,7 @@
 
 def bwd_kernel(at_hbm, z_ref, s_ref, sc_ref, sh_ref, bb_ref, cc_ref, da_ref, db_ref, pall_hbm, ptail_hbm, wtb_hbm, lab_ref, bias_ref,
                g_hbm, dbo_ref, gsq_ref, gfc_hbm, fsq_ref, gb_ref, loss_ref,
-               atv, dz0, dz1, dw, rd, ha, hb, ra, rb, ka, kb, r2a, r2b, gfull, dball, ptail, bpad, ps, pr, ss, rs, gs, gr, bs, br, osem, isem, fsem):
+               atv, dz0, dz1, dw, rd, ha, hb, ra, rb, ka, kb, r2a, r2b, gfull, dball, ptail, bpad, asem, ps, pr, ss, rs, gs, gr, bs, br, osem, isem, fsem):
     j = pl.program_id(0)
     dzs = (dz0, dz1)
     me, core, x, y = position()
@@ -436,7 +436,12 @@
     wtb = atv.at[:, pl.ds(COUT, COUT)]
     dlt = atv.at[:, pl.ds(2 * COUT, TOTAL)]
 
-    at_copy = pltpu.make_async_copy(at_hbm, atv, isem.at[0])
+
+    def at_copy(i, size=BIG):
+        c = pl.ds(pl.multiple_of(i * BIG, BIG), size)
+        return pltpu.make_async_copy(at_hbm.at[:, c], atv.at[:, c], asem.at[i])
+
+    at_rest = at_copy(NBIG, ROWS - NBIG * BIG)
     pall_copy = pltpu.make_async_copy(pall_hbm, atv.at[:, pl.ds(0, PG)], isem.at[1])
     wtb_copy = pltpu.make_async_copy(wtb_hbm, wtb, isem.at[2])
     ptail_copy = pltpu.make_async_copy(ptail_hbm, ptail.at[core, y, x], isem.at[3])
@@ -445,7 +450,9 @@
     @pl.when(j == 0)
     def _():
         ptail_copy.start()
-        at_copy.start()
+        at_rest.start()
+        for i in range(NBIG):
+            at_copy(i).start()
         enter_all()
         ptail_copy.wait()
         for b in range(NP):
@@ -455,10 +462,6 @@
         for r in (gsq_ref, fsq_ref, gb_ref, loss_ref):
             r[:] = jnp.zeros_like(r)
         set_bias(bpad, bias_ref)
-
-    @pl.when(j == 1)
-    def _():
-        at_copy.wait()
 
     def out_copy(b):
         c = cols(b)
@@ -563,12 +566,17 @@
                     out[m] = out[m] + g if add else g
 
         rest = NBIG * BIG
+        new = do_mm and do_pre and par == 1
+        if new:
+            pl.when(j == 1)(at_rest.wait)
         body(rest, POS - NBIG * BTILE, False)
 
         def chunk(i, carry):
             base = pl.multiple_of(i * BIG, BIG)
             if do_mm:
                 pl.when(i == 1)(stages)
+            if new:
+                pl.when(j == 1)(lambda: at_copy(i).wait())
             body(base, BTILE, True)
             return carry
         lax.fori_loop(0, NBIG, chunk, 0)
@@ -661,7 +669,7 @@
         scratch_shapes=[bvmem(CIN, ROWS), bvmem(ROWS, CB), bvmem(ROWS, CB), fvmem(2, CIN, CB), fvmem(NB, HALF, CB), fvmem(*quad), fvmem(*quad),
                         fvmem(NB, *pair), fvmem(NB, *pair), fvmem(2, *pair), fvmem(2, *pair), fvmem(*side), fvmem(*side),
                         fvmem(*QUAD, QR, COUT), fvmem(DEVS, 2, COUT), fvmem(*QUAD, IMG, PT), fvmem(1, KP),
-                        dma(5, NP), dma(5, NP), dma(5, NB), dma(5, NB), dma(5, NB), dma(5, NB), dma(DEVS), dma(DEVS), dma(NB), dma(4), dma(2, NB)],
+                        dma(NBIG + 1), dma(5, NP), dma(5, NP), dma(5, NB), dma(5, NB), dma(5, NB), dma(5, NB), dma(DEVS), dma(DEVS), dma(NB), dma(4), dma(2, NB)],
         compiler_params=pltpu.CompilerParams(vmem_limit_bytes=63 * MIB, collective_id=1, has_side_effects=True),
         cost_estimate=pl.CostEstimate(flops=2 * ROWS * CIN * COUT, bytes_accessed=2 * ROWS * COUT * 4, transcendentals=0),
         name="bwd_conv",

time: 190 us -> 193 us (1.016)
  Pallas kernels: 188 us -> 191 us
    pallas_call x1, Pallas kernels: 96 us -> 99.1 us  [backward(): pl.pallas_call(bwd_kernel, grid=(NB + BTAIL,), in_specs=[HBM, pl.BlockSpe...]
where the time goes in v11:
time: 193 us
  Pallas kernels  191 us (99%)
    pallas_call x1, Pallas kernels, backward(): pl.pallas_call(bwd_kernel, grid=(NB + BTAIL,), in_specs=[HBM, pl.BlockSpe...  99.1 us
    pallas_call x1, Pallas kernels, forward(): pl.pallas_call(fwd_kernel, grid=(NB + 1 + TAIL,), in_specs=[HBM, pl.Block...  64.1 us
    pallas_call x1, Pallas kernels, update_all(): pl.pallas_call(update_kernel, grid=(NU,), in_specs=[pl.BlockSpec(memory_s...  28.1 us

profile of v11, /device:TPU:1, one launch (start us, length us, event | category | flops | bytes accessed | tf_op | source)
XLA Modules:
  0.0 192.8 jit_solution(1277727024679745447)
XLA Ops:
  0.6 64.1 %fwd_conv.1 = (f32[8,6272,256]{2,1,0:T(8,128)}, bf16[1024,6272]{1,0:T(8,128)(2,1)}, bf16[1024,1536]{1,0:T(8,128)(2,1)}, f32[128,512]{1,0:T(8,128)}, s32[2,2,2,1,...) custom-call(bf16[6272,1024]{1,0:T(8,128)(2,1)} %bitcast.43, ...), custom_call_target="tpu_custom_call" | custom-call | flops 26306674688 | bytes 102760448 | tf_op jit(solution)/shard_map/fwd_conv/pallas_call | solution.py:410
  64.8 99.1 %bwd_conv.1 = (f32[2,2,2,128,2048]{4,3,2,1,0:T(8,128)}, f32[2,2048]{1,0:T(2,128)}, f32[8,256]{1,0:T(8,128)}, f32[1024,2048]{1,0:T(8,128)}, f32[8,2048]{1,0:T(8,1...) custom-call(bf16[1024,6272]{1,0:T(8,128)(2,1)} %get-tuple-element.43.at_hbm, f32[8,6272,256]{2,1,0:T(8,128)} %get-tuple-element.44.z_ref, ...), custom_call_target="tpu_custom_call" | custom-call | flops 26306674688 | bytes 102760448 | tf_op jit(solution)/shard_map/bwd_conv/pallas_call | solution.py:662
  164.5 28.1 %update.1 = (f32[1024,2048]{1,0:T(8,128)}, f32[1024,2048]{1,0:T(8,128)}, f32[1000,2048]{1,0:T(8,128)}, f32[1000,2048]{1,0:T(8,128)}, f32[1,1000]{1,0:T(1,128)}, ...) custom-call(f32[1]{0:T(128)} %bitcast.26.lr_ref, ...), custom_call_target="tpu_custom_call" | custom-call | flops 33554432 | bytes 83886080 | tf_op jit(solution)/shard_map/update/pallas_call | solution.py:727

commit v12 on v10

--- a/solution.py
+++ b/solution.py
@@ -36,7 +36,7 @@
 NG = 6
 NP = NB - NG
 PG, PT = NG * CB, NP * CB
-LAGS = (2, 3, 4, 6, 8, 9)
+LAGS = (2, 3, 4, 5, 7, 8)
 BTAIL = LAGS[-1]
 QR = CIN // DEVS
 HALF = CIN // 2

time: 190 us -> 190 us (level)
  no operation moved by 1% of the time
where the time goes in v12:
time: 190 us; the launch traced here: 189 us
  Pallas kernels  188 us (99%)
    pallas_call x1, Pallas kernels, backward(): pl.pallas_call(bwd_kernel, grid=(NB + BTAIL,), in_specs=[HBM, pl.BlockSpe...  95.7 us
    pallas_call x1, Pallas kernels, forward(): pl.pallas_call(fwd_kernel, grid=(NB + 1 + TAIL,), in_specs=[HBM, pl.Block...  64.1 us
    pallas_call x1, Pallas kernels, update_all(): pl.pallas_call(update_kernel, grid=(NU,), in_specs=[pl.BlockSpec(memory_s...  28.1 us

profile of v12, /device:TPU:1, one launch (start us, length us, event | category | flops | bytes accessed | tf_op | source)
XLA Modules:
  0.0 189.4 jit_solution(12567255249767595283)
XLA Ops:
  0.6 64.1 %fwd_conv.1 = (f32[8,6272,256]{2,1,0:T(8,128)}, bf16[1024,6272]{1,0:T(8,128)(2,1)}, bf16[1024,1536]{1,0:T(8,128)(2,1)}, f32[128,512]{1,0:T(8,128)}, s32[2,2,2,1,...) custom-call(bf16[6272,1024]{1,0:T(8,128)(2,1)} %bitcast.43, ...), custom_call_target="tpu_custom_call" | custom-call | flops 26306674688 | bytes 102760448 | tf_op jit(solution)/shard_map/fwd_conv/pallas_call | solution.py:410
  64.8 95.7 %bwd_conv.1 = (f32[2,2,2,128,2048]{4,3,2,1,0:T(8,128)}, f32[2,2048]{1,0:T(2,128)}, f32[8,256]{1,0:T(8,128)}, f32[1024,2048]{1,0:T(8,128)}, f32[8,2048]{1,0:T(8,1...) custom-call(bf16[1024,6272]{1,0:T(8,128)(2,1)} %get-tuple-element.43.at_hbm, f32[8,6272,256]{2,1,0:T(8,128)} %get-tuple-element.44.z_ref, ...), custom_call_target="tpu_custom_call" | custom-call | flops 26306674688 | bytes 102760448 | tf_op jit(solution)/shard_map/bwd_conv/pallas_call | solution.py:654
  161.1 28.1 %update.1 = (f32[1024,2048]{1,0:T(8,128)}, f32[1024,2048]{1,0:T(8,128)}, f32[1000,2048]{1,0:T(8,128)}, f32[1000,2048]{1,0:T(8,128)}, f32[1,1000]{1,0:T(1,128)}, ...) custom-call(f32[1]{0:T(128)} %bitcast.26.lr_ref, ...), custom_call_target="tpu_custom_call" | custom-call | flops 33554432 | bytes 83886080 | tf_op jit(solution)/shard_map/update/pallas_call | solution.py:719
